TPU v7x, 32 devices: a whole 2x2x4 slice. The times are simulated.
32 devices in a mesh: curve: 32 (over z, y, x, core).
Axes of the slice: x: 2, y: 2, z: 4, core: 2. Of those that a mesh axis runs over, the one named last changes fastest.
Arguments:
- nodal_state: float32 [5, 64, 16384], P(None, None, 'curve'), may hold values from -9 to 9, as said below
- inverse_jacobian: float32 [16384], P('curve'), may hold values from 1 to 4
- speeds: float32 [3, 5], replicated, may hold values from -1.5 to 1.5
- refine_flags: int32 [16384], P('curve'), may hold values from 0 to 1, as said below
- send_index: int32 [12288], P('curve'), may hold values from 0 to 3071, as said below
- face_source: int32 [6, 16384], P(None, 'curve'), may hold values from 0 to 3455, as said below
Outputs:
- refined_state: float32 [5, 64, 30720], P(None, None, 'curve')
- refined_jacobian: float32 [30720], P('curve')
Inputs may be any that keep to these rules, and one draw needn't show every extreme that they name: `nodal_state`: each element's 64 node values are a level plus a linear part plus noise of an amplitude that varies from element to element. `refine_flags`: exactly 64 flags per device on average over all devices, at most 128 on one device, a number that is reached; the refined elements of a device go only to itself and its two curve neighbours, at most 224 to each neighbour, a number that is reached. `send_index`: per device, four blocks of 96 entries for destination offsets -2, -1, 1, 2 along the curve (cyclically): entries f * 512 + n of the traces that device reads, in increasing order, then zeros in unused slots; the blocks for offsets -1 and 1 are always full. `face_source`: face pairing is symmetric: across face 2 d of an element lies face 2 d + 1 of its neighbour; neighbours are on the same device or on one within two curve offsets.
All inputs are finite; a program needn't handle non-finite values.
Results may differ from a plain program's by a relative error of at most 0.0003.
Values sent between devices are 32-bit elements; how exact they have to be, the bound alone decides.
No kernel may reach another device: no remote copies, remote signals or barrier semaphores. Data moves between devices by JAX's collectives and lax.ppermute only.
A program may use at most 64 MiB of HBM per device.

v0:
```python
import math

import jax
import jax.numpy as jnp
import numpy as np
from jax import lax
from jax.experimental import pallas as pl
from jax.experimental.pallas import tpu as pltpu
from jax.sharding import PartitionSpec as P

E_NEW = 960
TIME_STEP = 0.02
OFFSETS = (-2, -1, 1, 2)
LANES = 128
BF = jnp.bfloat16
F32 = jnp.float32


def lagrange_at(points, targets):
    values_at = np.ones((len(targets), 4))
    for basis_id in range(4):
        for partner in range(4):
            if partner != basis_id:
                values_at[:, basis_id] *= (targets - points[partner]) / (
                    points[basis_id] - points[partner]
                )
    return values_at


def modes_table(points):
    return np.linalg.inv(np.polynomial.legendre.legvander(points, 3))


def node_constants():
    root = 1.0 / math.sqrt(5.0)
    points = np.array([-1.0, -root, root, 1.0])
    deriv = np.zeros((4, 4))
    bary = np.array([1.0 / np.prod([points[r] - points[c] for c in range(4) if c != r]) for r in range(4)])
    for r in range(4):
        for c in range(4):
            if r != c:
                deriv[r, c] = bary[c] / bary[r] / (points[r] - points[c])
        deriv[r, r] = -np.sum(deriv[r])
    sides = (lagrange_at(points, (points - 1.0) / 2.0), lagrange_at(points, (points + 1.0) / 2.0))
    return deriv, modes_table(points), sides


DERIV, MODES, SIDES = node_constants()
INV_W = (6.0, 1.2, 1.2, 6.0)
SELF_SURFACE = (-3.0, 0.0, 0.0, 3.0)


def low_half(shape=(8, LANES)):
    return lax.broadcasted_iota(jnp.int32, shape, 0) < 4


def swap_halves(x):
    return pltpu.roll(x, 4, axis=0)


def trace_of(ref, t, face):
    dim, side = face // 2, face % 2
    if dim == 0:
        return ref[t, pl.ds(3 * side, 16, stride=4), :]
    if dim == 2:
        return ref[t, 48 * side : 48 * side + 16, :]
    low = low_half()
    tiles = [ref[t, 16 * k + 8 * side : 16 * k + 8 * side + 8, :] for k in range(4)]
    halves = []
    for k in (0, 2):
        if side == 0:
            halves.append(jnp.where(low, tiles[k], swap_halves(tiles[k + 1])))
        else:
            halves.append(jnp.where(low, swap_halves(tiles[k]), tiles[k + 1]))
    return jnp.concatenate(halves, axis=0)


def add_to_face(ref, t, face, value):
    dim, side = face // 2, face % 2
    if dim == 0:
        where_at = (t, pl.ds(3 * side, 16, stride=4), slice(None))
        ref[where_at] = ref[where_at] + value
    elif dim == 2:
        where_at = (t, slice(48 * side, 48 * side + 16), slice(None))
        ref[where_at] = ref[where_at] + value
    else:
        low = low_half()
        keep = low if side == 0 else jnp.logical_not(low)
        for k in range(4):
            half = value[8 * (k // 2) : 8 * (k // 2) + 8, :]
            if (k % 2) != side:
                half = swap_halves(half)
            where_at = (t, slice(16 * k + 8 * side, 16 * k + 8 * side + 8), slice(None))
            ref[where_at] = ref[where_at] + jnp.where(keep, half, 0.0)


def split_two(x):
    high = x.astype(BF)
    return high, (x - high.astype(F32)).astype(BF)


def one_hot(row, count):
    ids = lax.broadcasted_iota(jnp.int32, (count, row.shape[1]), 0)
    return jnp.where(ids == row, 1.0, 0.0).astype(BF)


def dot32(a, b):
    return jnp.dot(a, b, preferred_element_type=F32)


def send_kernel(u_ref, idx_ref, jac_ref, flag_ref, *rest):
    outs, lhs, gathered = rest[:4], rest[4], rest[5]
    elements = u_ref.shape[2]
    slots = idx_ref.shape[1] // 4
    for v in range(5):
        high, low = split_two(u_ref[v])
        lhs[v * 64 : (v + 1) * 64, :] = high
        lhs[320 + v * 64 : 320 + (v + 1) * 64, :] = low
    row = jnp.broadcast_to(idx_ref[...], (8, 4 * slots))
    row = jnp.concatenate([row, jnp.zeros((8, 512 - 4 * slots), jnp.int32)], axis=1)
    blocks = [row[:, :LANES]]
    for b in range(1, 4):
        blocks.append(pltpu.roll(row, 512 - slots * b, axis=1)[:, :LANES])
    idx = jnp.concatenate(blocks, axis=1)
    face = jnp.zeros_like(idx)
    for f in range(1, 6):
        face = face + (idx >= f * elements).astype(jnp.int32)
    elem = idx - face * elements
    picked = dot32(lhs[...], one_hot(elem[0:1], elements))
    for b in range(4):
        part = picked[:320, b * LANES : (b + 1) * LANES] + picked[320:, b * LANES : (b + 1) * LANES]
        gathered[b * 5 : (b + 1) * 5] = part.reshape(5, 64, LANES)
    flags = flag_ref[...].astype(F32)
    count = elements + 7.0 * jnp.sum(flags)
    rows = lax.broadcasted_iota(jnp.int32, (8, LANES), 0)
    groups = elements // LANES
    for b in range(4):
        fb = jnp.broadcast_to(face[0:1, b * LANES : (b + 1) * LANES], (16, LANES))
        for v in range(5):
            value = trace_of(gathered, b * 5 + v, 0)
            for f in range(1, 6):
                value = jnp.where(fb == f, trace_of(gathered, b * 5 + v, f), value)
            outs[b][v * 16 : (v + 1) * 16, :] = value
        near = 0 if OFFSETS[b] < 0 else groups - 2
        meta = jnp.full((8, LANES), count, F32)
        for r in range(2):
            meta = jnp.where(rows == r, jac_ref[near + r : near + r + 1, :], meta)
            meta = jnp.where(rows == 2 + r, flags[near + r : near + r + 1, :], meta)
        outs[b][80:88, :] = meta


def line_rates(x, speed, blend):
    square = [x[m] * x[m] for m in range(4)]
    prod = {}
    for m in range(4):
        for n in range(m + 1, 4):
            prod[m, n] = x[m] * x[n]
    half_speed = 0.5 * jnp.abs(speed)
    flux = []
    for m in range(3):
        central = square[m] + prod[m, m + 1] + square[m + 1]
        reach = jnp.maximum(jnp.abs(x[m]), jnp.abs(x[m + 1]))
        flux.append((speed / 6.0) * central - half_speed * reach * (x[m + 1] - x[m]))
    out = []
    for n in range(4):
        high = None
        diag = -2.0 * DERIV[n, n] / 3.0 + SELF_SURFACE[n]
        for m in range(4):
            if m != n:
                pair = prod[min(m, n), max(m, n)] + square[m]
                term = float(-DERIV[n, m] / 3.0) * pair
                high = term if high is None else high + term
        if n in (0, 3):
            high = high + float(diag) * square[n]
        high = speed * high
        if n == 0:
            low = -INV_W[0] * flux[0]
        elif n == 3:
            low = INV_W[3] * flux[2]
        else:
            low = INV_W[n] * (flux[n - 1] - flux[n])
        out.append(high + blend * (low - high))
    return out


def local_kernel(u_ref, jac_ref, fs_ref, sp_ref, modes_ref, base_ref, slab_ref, out_ref, lhs, rows_s):
    elements = u_ref.shape[2]
    groups = elements // LANES
    for v in range(5):
        for g in range(groups):
            slab_ref[g * 5 + v] = u_ref[v, :, g * LANES : (g + 1) * LANES]
    modal = jnp.dot(
        modes_ref[:, :64], u_ref[0], precision=lax.Precision.HIGHEST, preferred_element_type=F32
    )
    energy = modal * modal
    top = jnp.sum(energy * modes_ref[:, 64:65], axis=0, keepdims=True)
    whole = jnp.sum(energy, axis=0, keepdims=True)
    ratio = top / (whole + 1e-06)
    blend_all = 0.5 * ratio / (ratio + 0.1)
    for g in range(groups):
        rows_s[g] = jnp.broadcast_to(blend_all[:, g * LANES : (g + 1) * LANES], (8, LANES))
        rows_s[groups + g] = jnp.broadcast_to(jac_ref[g : g + 1, :] * TIME_STEP, (8, LANES))

    def one(t, carry):
        g = t // 5
        v = t - 5 * g
        blend = rows_s[g]
        scale = rows_s[groups + g]
        low = low_half()
        for kh in range(2):
            at = [(t, pl.ds(32 * kh + i, 8, stride=4), slice(None)) for i in range(4)]
            rate = line_rates([slab_ref[a] for a in at], sp_ref[0, v], blend)
            for i in range(4):
                base_ref[at[i]] = rate[i]
        tile = [[slab_ref[t, 16 * k + 8 * h : 16 * k + 8 * h + 8, :] for h in range(2)] for k in range(4)]
        rates = [[None, None] for _ in range(4)]
        for h in range(2):
            r = line_rates([tile[k][h] for k in range(4)], sp_ref[2, v], blend)
            for k in range(4):
                rates[k][h] = r[k]
        for k in (0, 2):
            x = []
            for h in range(2):
                x.append(jnp.where(low, tile[k][h], swap_halves(tile[k + 1][h])))
                x.append(jnp.where(low, swap_halves(tile[k][h]), tile[k + 1][h]))
            r = line_rates(x, sp_ref[1, v], blend)
            for h in range(2):
                first, second = r[2 * h], r[2 * h + 1]
                rates[k][h] = rates[k][h] + jnp.where(low, first, swap_halves(second))
                rates[k + 1][h] = rates[k + 1][h] + jnp.where(low, swap_halves(first), second)
        for k in range(4):
            for h in range(2):
                at = (t, slice(16 * k + 8 * h, 16 * k + 8 * h + 8), slice(None))
                base_ref[at] = tile[k][h] + scale * (rates[k][h] + base_ref[at])
        return carry

    lax.fori_loop(0, 5 * groups, one, 0)

    for f in range(6):
        partner = f + 1 - 2 * (f % 2)
        for g in range(groups):
            for v in range(5):
                high, low = split_two(trace_of(slab_ref, g * 5 + v, partner))
                lhs[v * 16 : (v + 1) * 16, g * LANES : (g + 1) * LANES] = high
                lhs[80 + v * 16 : 80 + (v + 1) * 16, g * LANES : (g + 1) * LANES] = low
        picked = dot32(lhs[...], one_hot(fs_ref[f : f + 1, :] - partner * elements, elements))
        near = fs_ref[f : f + 1, :] < 6 * elements
        out_ref[f] = jnp.where(near, picked[:80] + picked[80:], 0.0)


def face_kernel(base_ref, slab_ref, out_ref, fs_ref, jac_ref, sp_ref, flag_ref, r0, r1, r2, r3, *rest):
    head_ref, tail_ref, width_ref, lhs, outside = rest
    elements = fs_ref.shape[1]
    groups = elements // LANES
    slots = 96
    for b, ref in enumerate((r0, r1, r2, r3)):
        high, low = split_two(ref[0:80, :])
        lhs[0:80, b * LANES : (b + 1) * LANES] = high
        lhs[80:160, b * LANES : (b + 1) * LANES] = low
    half = 5 * (groups // 2)
    head_ref[...] = base_ref[0:half]
    tail_ref[...] = base_ref[half : 2 * half]
    for f in range(6):
        ghost = fs_ref[f : f + 1, :] - 6 * elements
        place = jnp.zeros_like(ghost)
        for b in range(1, 4):
            place = place + (ghost >= b * slots).astype(jnp.int32)
        column = ghost + place * (LANES - slots)
        picked = dot32(lhs[...], one_hot(column, 4 * LANES))
        outside[f] = out_ref[f] + (picked[:80] + picked[80:])
    for g in range(groups):
        ref, first = (head_ref, 0) if g < groups // 2 else (tail_ref, groups // 2)
        scale = jnp.broadcast_to(jac_ref[g : g + 1, :] * TIME_STEP, (16, LANES))
        for v in range(5):
            t = g * 5 + v
            for f in range(6):
                speed = sp_ref[f // 2, v]
                inner = trace_of(slab_ref, t, f)
                outer = outside[f, v * 16 : (v + 1) * 16, g * LANES : (g + 1) * LANES]
                central = inner * inner + inner * outer + outer * outer
                reach = (3.0 * jnp.abs(speed)) * jnp.maximum(jnp.abs(inner), jnp.abs(outer))
                sign = 1.0 if f % 2 == 0 else -1.0
                value = (sign * speed) * central - reach * (inner - outer)
                add_to_face(ref, (g - first) * 5 + v, f, scale * value)
    me = lax.axis_index("curve")
    total = lax.axis_size("curve")
    lower = me < total // 2
    count = jnp.full((8, LANES), elements + 7.0 * jnp.sum(flag_ref[...].astype(F32)), F32)
    own = count
    for o, ref in zip(OFFSETS, (r0, r1, r2, r3)):
        there = me + o
        wanted = jnp.logical_and(lower if o < 0 else jnp.logical_not(lower), jnp.logical_and(there >= 0, there < total))
        value = jnp.broadcast_to(ref[87:88, :], (8, LANES))
        count = count + value * jnp.where(wanted, 1.0, 0.0)
    width_ref[0:8] = count
    width_ref[8:16] = own


def refine_kernel(low_ref, head_ref, tail_ref, up_ref, w_ref, own_ref, r1, r2, jac_ref, flag_ref, *rest):
    out_ref, jout_ref, lhs, res, coef, cols = rest
    halves = (low_ref, head_ref, tail_ref, up_ref)
    total = lax.axis_size("curve")
    me = lax.axis_index("curve")
    for b, ref in enumerate(halves):
        for g in range(2):
            high, low = split_two(ref[5 * g : 5 * g + 5].reshape(320, LANES))
            at = slice((2 * b + g) * LANES, (2 * b + g + 1) * LANES)
            lhs[0:320, at] = high
            lhs[320:640, at] = low
    jac = jnp.concatenate([r1[80:82, :], jac_ref[...], r2[80:82, :]], axis=0)
    flag = jnp.concatenate([r1[82:84, :], flag_ref[...].astype(F32), r2[82:84, :]], axis=0)
    sizes = 1.0 + 7.0 * flag
    lane0 = lax.broadcasted_iota(jnp.int32, (LANES, LANES), 0)
    lane1 = lax.broadcasted_iota(jnp.int32, (LANES, LANES), 1)
    upper = jnp.where(lane0 < lane1, 1.0, 0.0).astype(BF)
    sizes_b = sizes.astype(BF)
    within = dot32(sizes_b, upper)
    row_total = jnp.sum(sizes, axis=1, keepdims=True)
    running = jnp.zeros((1, 1), F32)
    starts = []
    for r in range(8):
        starts.append(running)
        running = running + row_total[r : r + 1]
    row0 = lax.broadcasted_iota(jnp.int32, (8, LANES), 0)
    before = within
    for r in range(8):
        before = before + jnp.where(row0 == r, starts[r], 0.0)
    width = w_ref[0:8]
    if own_ref is not None:
        width = width
    mine = own_ref[8:16]
    lower = jnp.where(me < total // 2, 1.0, 0.0)
    begin = lower * (width - mine) + (1.0 - lower) * (float(total * E_NEW) - width)
    begin = begin - (me * E_NEW).astype(F32)
    place = before + (begin - starts[2])
    ends = place + sizes
    place_hi = jnp.floor(place * (1.0 / 256.0))
    place_lo = place - 256.0 * place_hi
    jac_a = jac.astype(BF)
    jac_b = (jac - jac_a.astype(F32)).astype(BF)
    jac_c = (jac - jac_a.astype(F32) - jac_b.astype(F32)).astype(BF)
    rows16 = lax.broadcasted_iota(jnp.int32, (16, LANES), 0)
    extras = [jac_a.astype(F32), jac_b.astype(F32), jac_c.astype(F32), flag, place_hi, place_lo]
    for r in range(8):
        block = jnp.zeros((16, LANES), F32)
        for q, item in enumerate(extras):
            block = jnp.where(rows16 == q, jnp.broadcast_to(item[r : r + 1, :], (16, LANES)), block)
        lhs[640:656, r * LANES : (r + 1) * LANES] = block.astype(BF)
        cols[0, r * LANES : (r + 1) * LANES, :] = jnp.transpose(jnp.broadcast_to(place[r : r + 1, :], (LANES, LANES)))
        cols[1, r * LANES : (r + 1) * LANES, :] = jnp.transpose(jnp.broadcast_to(ends[r : r + 1, :], (LANES, LANES)))

    spans = ((0, 768), (256, 768), (256, 1024), (256, 1024))
    for pair, (k0, k1) in enumerate(spans):
        pieces = []
        for h in range(2):
            slot = (lax.broadcasted_iota(jnp.int32, (8, LANES), 1) + (2 * pair + h) * LANES).astype(F32)
            slot_b = jnp.broadcast_to(slot[0:1], (k1 - k0, LANES))
            hit = jnp.logical_and(slot_b >= cols[0, k0:k1, :], slot_b < cols[1, k0:k1, :])
            pieces.append(jnp.where(hit, 1.0, 0.0).astype(BF))
        picked = dot32(lhs[:, k0:k1], jnp.concatenate(pieces, axis=1))
        for h in range(2):
            g = 2 * pair + h
            lanes = slice(h * LANES, (h + 1) * LANES)
            width_at = min(LANES, E_NEW - g * LANES)
            res[...] = (picked[0:320, lanes] + picked[320:640, lanes]).reshape(5, 64, LANES)
            extra = picked[640:656, lanes]
            jac_new = (extra[0:1] + extra[1:2] + extra[2:3]) * (1.0 + extra[3:4])
            jout_ref[0:1, g * LANES : g * LANES + width_at] = jac_new[:, :width_at]
            fl = jnp.broadcast_to(extra[3:4], (8, LANES))
            slot = (lax.broadcasted_iota(jnp.int32, (8, LANES), 1) + g * LANES).astype(F32)
            child = slot - (256.0 * extra[4:5] + extra[5:6])
            bit2 = jnp.where(child >= 4.0, 1.0, 0.0)
            child = child - 4.0 * bit2
            bit1 = jnp.where(child >= 2.0, 1.0, 0.0)
            bit0 = child - 2.0 * bit1
            for d, bit in enumerate((bit0, bit1, bit2)):
                both = fl * bit
                for i in range(4):
                    for m in range(4):
                        eye = 1.0 if i == m else 0.0
                        c = fl * float(SIDES[0][i, m] - eye) + both * float(SIDES[1][i, m] - SIDES[0][i, m]) + eye
                        coef[16 * d + 4 * i + m] = c

            def apply(d, x):
                out = []
                for i in range(4):
                    acc = coef[16 * d + 4 * i] * x[0]
                    for m in range(1, 4):
                        acc = acc + coef[16 * d + 4 * i + m] * x[m]
                    out.append(acc)
                return out

            def one(v, carry):
                low = low_half()
                for kh in range(2):
                    at = [(v, pl.ds(32 * kh + i, 8, stride=4), slice(None)) for i in range(4)]
                    y = apply(0, [res[a] for a in at])
                    for i in range(4):
                        res[at[i]] = y[i]
                tile = [[res[v, 16 * k + 8 * q : 16 * k + 8 * q + 8, :] for q in range(2)] for k in range(4)]
                for q in range(2):
                    y = apply(2, [tile[k][q] for k in range(4)])
                    for k in range(4):
                        tile[k][q] = y[k]
                for k in (0, 2):
                    x = []
                    for q in range(2):
                        x.append(jnp.where(low, tile[k][q], swap_halves(tile[k + 1][q])))
                        x.append(jnp.where(low, swap_halves(tile[k][q]), tile[k + 1][q]))
                    y = apply(1, x)
                    for q in range(2):
                        first, second = y[2 * q], y[2 * q + 1]
                        a = jnp.where(low, first, swap_halves(second))
                        b = jnp.where(low, swap_halves(first), second)
                        lanes_out = slice(g * LANES, g * LANES + width_at)
                        out_ref[v, 16 * k + 8 * q : 16 * k + 8 * q + 8, lanes_out] = a[:, :width_at]
                        out_ref[v, 16 * (k + 1) + 8 * q : 16 * (k + 1) + 8 * q + 8, lanes_out] = b[:, :width_at]
                return carry

            lax.fori_loop(0, 5, one, 0)


def add_kernel(*refs):
    total = refs[0][...]
    for ref in refs[1:-1]:
        total = total + ref[...]
    refs[-1][...] = total


VMEM = pl.BlockSpec(memory_space=pltpu.MemorySpace.VMEM)
SMEM = pl.BlockSpec(memory_space=pltpu.MemorySpace.SMEM)


def call(body, outs, specs, scratch, name):
    return pl.pallas_call(
        body,
        out_shape=tuple(jax.ShapeDtypeStruct(s, F32) for s in outs),
        in_specs=specs,
        out_specs=tuple(VMEM for _ in outs),
        scratch_shapes=scratch,
        name=name,
    )


def shards(nodal_state, inverse_jacobian, speeds, refine_flags, send_index, face_source):
    elements = nodal_state.shape[2]
    groups = elements // LANES
    total = lax.axis_size("curve")
    half = total // 2
    idx = send_index.reshape(1, -1)
    jac = inverse_jacobian.reshape(groups, LANES)
    flags = refine_flags.reshape(groups, LANES)
    degrees = np.arange(4)
    top = (np.maximum(np.maximum(degrees[:, None, None], degrees[None, :, None]), degrees) == 3).reshape(64, 1)
    kron = np.kron(MODES, np.kron(MODES, MODES))
    modes = jnp.asarray(np.concatenate([kron, np.repeat(top, 64, axis=1)], axis=1), F32)

    sends = call(
        send_kernel,
        [(88, LANES)] * 4,
        [VMEM] * 4,
        [pltpu.VMEM((640, elements), BF), pltpu.VMEM((20, 64, LANES), F32)],
        "send",
    )(nodal_state, idx, jac, flags)
    received = [None] * 4
    for b, o in enumerate(OFFSETS):
        pairs = [(i, (i + o) % total) for i in range(total)]
        received[3 - b] = lax.ppermute(sends[b], "curve", pairs)

    base, slab, outside = call(
        local_kernel,
        [(5 * groups, 64, LANES), (5 * groups, 64, LANES), (6, 80, elements)],
        [VMEM, VMEM, VMEM, SMEM, VMEM],
        [pltpu.VMEM((160, elements), BF), pltpu.VMEM((2 * groups, 8, LANES), F32)],
        "local",
    )(nodal_state, jac, face_source, speeds, modes)

    head, tail, width = call(
        face_kernel,
        [(5 * groups // 2, 64, LANES), (5 * groups // 2, 64, LANES), (16, LANES)],
        [VMEM] * 5 + [SMEM] + [VMEM] * 5,
        [pltpu.VMEM((160, 4 * LANES), BF), pltpu.VMEM((6, 80, elements), F32)],
        "faces",
    )(base, slab, outside, face_source, jac, speeds, flags, *received)

    from_lower = lax.ppermute(tail, "curve", [(i, i + 1) for i in range(total - 1)])
    from_upper = lax.ppermute(head, "curve", [(i + 1, i) for i in range(total - 1)])

    own = width
    reach = 3
    while reach < half:
        shifts = (reach,) if 2 * reach >= half else (reach, 2 * reach)
        parts = [width]
        for s in shifts:
            pairs = [(i, i + s) for i in range(half - s)]
            pairs += [(i, i - s) for i in range(half + s, total)]
            parts.append(lax.ppermute(width, "curve", pairs))
        width = call(add_kernel, [(16, LANES)], [VMEM] * len(parts), [], "add")(*parts)[0]
        reach *= len(shifts) + 1

    state, new_jac = call(
        refine_kernel,
        [(5, 64, E_NEW), (1, E_NEW)],
        [VMEM] * 10,
        [
            pltpu.VMEM((656, 8 * LANES), BF),
            pltpu.VMEM((5, 64, LANES), F32),
            pltpu.VMEM((48, 8, LANES), F32),
            pltpu.VMEM((2, 8 * LANES, LANES), F32),
        ],
        "refine",
    )(from_lower, head, tail, from_upper, width, own, received[1], received[2], jac, flags)
    return state, new_jac.reshape(E_NEW)


def solution(mesh):
    return jax.shard_map(
        shards,
        mesh=mesh,
        in_specs=(
            P(None, None, "curve"),
            P("curve"),
            P(),
            P("curve"),
            P("curve"),
            P(None, "curve"),
        ),
        out_specs=(P(None, None, "curve"), P("curve")),
        check_vma=False,
    )
```

profile of v0, /device:TPU:0, one launch (start us, length us, event | category | flops | bytes accessed | tf_op | source)
XLA Modules:
  0.0 54.5 jit_solution(6935900852025394234)
XLA Ops:
  0.6 1.2 %reshape.18.idx_ref = s32[1,384]{1,0:T(1,128)} reshape(s32[384]{0:T(512)} %param.11) | data formatting | bytes 3072 | tf_op jit(solution)/shard_map/reshape | solution.py:450
  1.9 2.4 %send.1 = (f32[88,128]{1,0:T(8,128)}, f32[88,128]{1,0:T(8,128)}, f32[88,128]{1,0:T(8,128)}, f32[88,128]{1,0:T(8,128)}) custom-call(f32[5,64,512]{2,1,0:T(8,128)} %u_ref.3, s32[1,384]{1,0:T(1,128)} %reshape.18.idx_ref, f32[4,128]{1,0:T(4,128)} %bitcast.3, s32[4,128]{1,0:T(4,128)} %bitcast.7), custom_call_target="tpu_custom_call" | custom-call | tf_op jit(solution)/shard_map/send/pallas_call | solution.py:458
  4.3 3.0 %collective-permute-start = (f32[88,128]{1,0:T(8,128)}, f32[88,128]{1,0:T(8,128)S(1)}, u32[]{:S(2)}, u32[]{:S(2)}) collective-permute-start(f32[88,128]{1,0:T(8,128)} %get-tuple-element.17), channel_id=1, source_target_pairs={{0,2},{1,3},{2,4},{3,5},{4,6},{5,7},{6,8},{7,9},{8,10},{9,11},{10,... | collective-permute-start | bytes 135176 | tf_op jit(solution)/shard_map/ppermute | solution.py:468
  7.2 5.3 %collective-permute-start.2 = (f32[88,128]{1,0:T(8,128)}, f32[88,128]{1,0:T(8,128)S(1)}, u32[]{:S(2)}, u32[]{:S(2)}) collective-permute-start(f32[88,128]{1,0:T(8,128)} %get-tuple-element.19), channel_id=1, source_target_pairs={{0,31},{1,0},{2,1},{3,2},{4,3},{5,4},{6,5},{7,6},{8,7},{9,8},{10,9... | collective-permute-start | bytes 135176 | tf_op jit(solution)/shard_map/ppermute | solution.py:468
  12.6 0.4 collective-permute-start.3
  13.0 5.4 %local.1 = (f32[20,64,128]{2,1,0:T(8,128)}, f32[20,64,128]{2,1,0:T(8,128)}, f32[6,80,512]{2,1,0:T(8,128)}) custom-call(f32[5,64,512]{2,1,0:T(8,128)} %u_ref.3, f32[4,128]{1,0:T(4,128)} %bitcast.4, s32[6,512]{1,0:T(8,128)} %fs_ref.3, f32[3,5]{1,0:T(4,128)} %sp_ref.3, f32[64,128]{1,0:T(8,128)} %constant.2.clone.modes_ref), custom_call_target="tpu_custom_call" | custom-call | tf_op jit(solution)/shard_map/local/pallas_call | solution.py:470
  18.5 0.6 %copy-done.4 = f32[88,128]{1,0:T(8,128)} copy-done((f32[88,128]{1,0:T(8,128)}, f32[88,128]{1,0:T(8,128)S(1)}, u32[]{:S(2)}) %copy-start.4) | copy-done | bytes 45080
  19.0 0.0 copy-done.2
  19.1 0.0 copy-done.5
  19.1 3.6 %faces.1 = (f32[10,64,128]{2,1,0:T(8,128)}, f32[10,64,128]{2,1,0:T(8,128)}, f32[16,128]{1,0:T(8,128)}) custom-call(f32[20,64,128]{2,1,0:T(8,128)} %get-tuple-element.14.base_ref, f32[20,64,128]{2,1,0:T(8,128)} %get-tuple-element.15.slab_ref, f32[6,80,512]{2,1,0:T(8,128)} %get-tuple-element.16.out_ref, s32[6,512]{1,0:T(8,128)} %fs_ref.3, f32[4,128]{1,0:T(4,128)} %bitcast.5, ...), custom_call_target="tpu_custom_call" | custom-call | tf_op jit(solution)/shard_map/faces/pallas_call | solution.py:478
  22.7 1.6 %collective-permute-start.4 = (f32[10,64,128]{2,1,0:T(8,128)}, f32[10,64,128]{2,1,0:T(8,128)S(1)}, u32[]{:S(2)}, u32[]{:S(2)}) collective-permute-start(f32[10,64,128]{2,1,0:T(8,128)} %get-tuple-element.21.tail_ref), channel_id=1, source_target_pairs={{0,1},{1,2},{2,3},{3,4},{4,5},{5,6},{6,7},{7,8},{8,9},{9,10},{10,1... | collective-permute-start | bytes 983048 | tf_op jit(solution)/shard_map/ppermute | solution.py:486
  24.3 1.3 %collective-permute-start.5 = (f32[10,64,128]{2,1,0:T(8,128)}, f32[10,64,128]{2,1,0:T(8,128)S(1)}, u32[]{:S(2)}, u32[]{:S(2)}) collective-permute-start(f32[10,64,128]{2,1,0:T(8,128)} %get-tuple-element.22.head_ref), channel_id=1, source_target_pairs={{1,0},{2,1},{3,2},{4,3},{5,4},{6,5},{7,6},{8,7},{9,8},{10,9},{11,1... | collective-permute-start | bytes 983048 | tf_op jit(solution)/shard_map/ppermute | solution.py:487
  25.6 4.4 %collective-permute-start.7 = (f32[16,128]{1,0:T(8,128)}, f32[16,128]{1,0:T(8,128)S(1)}, u32[]{:S(2)}, u32[]{:S(2)}) collective-permute-start(f32[16,128]{1,0:T(8,128)} %get-tuple-element.23.refs_0_.own_ref), channel_id=1, source_target_pairs={{0,6},{1,7},{2,8},{3,9},{4,10},{5,11},{6,12},{7,13},{8,14},{9,15},... | collective-permute-start | bytes 24584 | tf_op jit(solution)/shard_map/ppermute | solution.py:497
  30.1 2.6 %collective-permute-start.6 = (f32[16,128]{1,0:T(8,128)}, f32[16,128]{1,0:T(8,128)S(1)}, u32[]{:S(2)}, u32[]{:S(2)}) collective-permute-start(f32[16,128]{1,0:T(8,128)} %get-tuple-element.23.refs_0_.own_ref), channel_id=1, source_target_pairs={{0,3},{1,4},{2,5},{3,6},{4,7},{5,8},{6,9},{7,10},{8,11},{9,12},{10... | collective-permute-start | bytes 24584 | tf_op jit(solution)/shard_map/ppermute | solution.py:497
  32.7 1.5 %collective-permute-done.6.refs_1_ = f32[16,128]{1,0:T(8,128)S(1)} collective-permute-done((f32[16,128]{1,0:T(8,128)}, f32[16,128]{1,0:T(8,128)S(1)}, u32[]{:S(2)}, u32[]{:S(2)}) %collective-permute-start.6) | collective-permute-done | bytes 8224 | tf_op jit(solution)/shard_map/ppermute | solution.py:497
  34.2 0.6 %copy-done.8 = f32[16,128]{1,0:T(8,128)} copy-done((f32[16,128]{1,0:T(8,128)}, f32[16,128]{1,0:T(8,128)S(1)}, u32[]{:S(2)}) %copy-start.8) | copy-done | bytes 8216
  34.8 1.3 %add.2.refs_0_ = f32[16,128]{1,0:T(8,128)} custom-call(f32[16,128]{1,0:T(8,128)} %get-tuple-element.23.refs_0_.own_ref, f32[16,128]{1,0:T(8,128)} %copy-done.8, f32[16,128]{1,0:T(8,128)} %copy-done.7), custom_call_target="tpu_custom_call" | custom-call | tf_op jit(solution)/shard_map/add/pallas_call | solution.py:498
  36.2 6.4 %collective-permute-start.8 = (f32[16,128]{1,0:T(8,128)}, f32[16,128]{1,0:T(8,128)S(1)}, u32[]{:S(2)}, u32[]{:S(2)}) collective-permute-start(f32[16,128]{1,0:T(8,128)} %add.2.refs_0_), channel_id=1, source_target_pairs={{0,9},{1,10},{2,11},{3,12},{4,13},{5,14},{6,15},{25,16},{26,17},{2... | collective-permute-start | bytes 24584 | tf_op jit(solution)/shard_map/ppermute | solution.py:497
  42.6 1.6 %collective-permute-done.8.refs_1_ = f32[16,128]{1,0:T(8,128)S(1)} collective-permute-done((f32[16,128]{1,0:T(8,128)}, f32[16,128]{1,0:T(8,128)S(1)}, u32[]{:S(2)}, u32[]{:S(2)}) %collective-permute-start.8) | collective-permute-done | bytes 8224 | tf_op jit(solution)/shard_map/ppermute | solution.py:497
  44.1 0.6 %copy-done.6 = f32[16,128]{1,0:T(8,128)} copy-done((f32[16,128]{1,0:T(8,128)}, f32[16,128]{1,0:T(8,128)S(1)}, u32[]{:S(2)}) %copy-start.6) | copy-done | bytes 8216
  44.7 1.3 %add.3.w_ref = f32[16,128]{1,0:T(8,128)} custom-call(f32[16,128]{1,0:T(8,128)} %add.2.refs_0_, f32[16,128]{1,0:T(8,128)} %copy-done.6), custom_call_target="tpu_custom_call" | custom-call | tf_op jit(solution)/shard_map/add/pallas_call | solution.py:498
  46.0 0.7 %copy-done = f32[10,64,128]{2,1,0:T(8,128)} copy-done((f32[10,64,128]{2,1,0:T(8,128)}, f32[10,64,128]{2,1,0:T(8,128)S(1)}, u32[]{:S(2)}) %copy-start) | copy-done | bytes 327704
  46.8 0.7 %copy-done.1 = f32[10,64,128]{2,1,0:T(8,128)} copy-done((f32[10,64,128]{2,1,0:T(8,128)}, f32[10,64,128]{2,1,0:T(8,128)S(1)}, u32[]{:S(2)}) %copy-start.1) | copy-done | bytes 327704
  47.5 7.0 %refine.1 = (f32[5,64,960]{2,1,0:T(8,128)}, f32[1,960]{1,0:T(1,128)}) custom-call(f32[10,64,128]{2,1,0:T(8,128)} %copy-done, f32[10,64,128]{2,1,0:T(8,128)} %get-tuple-element.22.head_ref, f32[10,64,128]{2,1,0:T(8,128)} %get-tuple-element.21.tail_ref, f32[10,64,128]{2,1,0:T(8,128)} %copy-done.1, f32[16,128]{1,0:T(8,128)} %add.3.w_ref, ...), custom_call_target="tpu_custom_call" | custom-call | tf_op jit(solution)/shard_map/refine/pallas_call | solution.py:501
  (19 shorter events, 0.1 us)
Async XLA Ops:
  4.3 14.1 %collective-permute-start = (f32[88,128]{1,0:T(8,128)}, f32[88,128]{1,0:T(8,128)S(1)}, u32[]{:S(2)}, u32[]{:S(2)}) collective-permute-start(f32[88,128]{1,0:T(8,128)} %get-tuple-element.17), channel_id=1, source_target_pairs={{0,2},{1,3},{2,4},{3,5},{4,6},{5,7},{6,8},{7,9},{8,10},{9,11},{10,... | collective-permute-start | bytes 135176 | tf_op jit(solution)/shard_map/ppermute | solution.py:468
  7.2 11.2 %collective-permute-start.1 = (f32[88,128]{1,0:T(8,128)}, f32[88,128]{1,0:T(8,128)S(1)}, u32[]{:S(2)}, u32[]{:S(2)}) collective-permute-start(f32[88,128]{1,0:T(8,128)} %get-tuple-element.18), channel_id=1, source_target_pairs={{0,1},{1,2},{2,3},{3,4},{4,5},{5,6},{6,7},{7,8},{8,9},{9,10},{10,1... | collective-permute-start | bytes 135176 | tf_op jit(solution)/shard_map/ppermute | solution.py:468
  7.2 11.2 %collective-permute-start.2 = (f32[88,128]{1,0:T(8,128)}, f32[88,128]{1,0:T(8,128)S(1)}, u32[]{:S(2)}, u32[]{:S(2)}) collective-permute-start(f32[88,128]{1,0:T(8,128)} %get-tuple-element.19), channel_id=1, source_target_pairs={{0,31},{1,0},{2,1},{3,2},{4,3},{5,4},{6,5},{7,6},{8,7},{9,8},{10,9... | collective-permute-start | bytes 135176 | tf_op jit(solution)/shard_map/ppermute | solution.py:468
  12.6 5.9 %collective-permute-start.3 = (f32[88,128]{1,0:T(8,128)}, f32[88,128]{1,0:T(8,128)S(1)}, u32[]{:S(2)}, u32[]{:S(2)}) collective-permute-start(f32[88,128]{1,0:T(8,128)} %get-tuple-element.20), channel_id=1, source_target_pairs={{0,30},{1,31},{2,0},{3,1},{4,2},{5,3},{6,4},{7,5},{8,6},{9,7},{10,... | collective-permute-start | bytes 135176 | tf_op jit(solution)/shard_map/ppermute | solution.py:468
  18.4 0.6 %copy-start.4 = (f32[88,128]{1,0:T(8,128)}, f32[88,128]{1,0:T(8,128)S(1)}, u32[]{:S(2)}) copy-start(f32[88,128]{1,0:T(8,128)S(1)} %collective-permute-done.r0) | copy-start | bytes 135172
  18.4 0.6 %copy-start.2 = (f32[88,128]{1,0:T(8,128)}, f32[88,128]{1,0:T(8,128)S(1)}, u32[]{:S(2)}) copy-start(f32[88,128]{1,0:T(8,128)S(1)} %collective-permute-done.1.r1) | copy-start | bytes 135172
  18.4 0.6 %copy-start.3 = (f32[88,128]{1,0:T(8,128)}, f32[88,128]{1,0:T(8,128)S(1)}, u32[]{:S(2)}) copy-start(f32[88,128]{1,0:T(8,128)S(1)} %collective-permute-done.2.r2) | copy-start | bytes 135172
  18.5 0.6 %copy-start.5 = (f32[88,128]{1,0:T(8,128)}, f32[88,128]{1,0:T(8,128)S(1)}, u32[]{:S(2)}) copy-start(f32[88,128]{1,0:T(8,128)S(1)} %collective-permute-done.3.r3) | copy-start | bytes 135172
  22.7 23.3 %collective-permute-start.4 = (f32[10,64,128]{2,1,0:T(8,128)}, f32[10,64,128]{2,1,0:T(8,128)S(1)}, u32[]{:S(2)}, u32[]{:S(2)}) collective-permute-start(f32[10,64,128]{2,1,0:T(8,128)} %get-tuple-element.21.tail_ref), channel_id=1, source_target_pairs={{0,1},{1,2},{2,3},{3,4},{4,5},{5,6},{6,7},{7,8},{8,9},{9,10},{10,1... | collective-permute-start | bytes 983048 | tf_op jit(solution)/shard_map/ppermute | solution.py:486
  24.3 21.7 %collective-permute-start.5 = (f32[10,64,128]{2,1,0:T(8,128)}, f32[10,64,128]{2,1,0:T(8,128)S(1)}, u32[]{:S(2)}, u32[]{:S(2)}) collective-permute-start(f32[10,64,128]{2,1,0:T(8,128)} %get-tuple-element.22.head_ref), channel_id=1, source_target_pairs={{1,0},{2,1},{3,2},{4,3},{5,4},{6,5},{7,6},{8,7},{9,8},{10,9},{11,1... | collective-permute-start | bytes 983048 | tf_op jit(solution)/shard_map/ppermute | solution.py:487
  25.6 7.0 %collective-permute-start.7 = (f32[16,128]{1,0:T(8,128)}, f32[16,128]{1,0:T(8,128)S(1)}, u32[]{:S(2)}, u32[]{:S(2)}) collective-permute-start(f32[16,128]{1,0:T(8,128)} %get-tuple-element.23.refs_0_.own_ref), channel_id=1, source_target_pairs={{0,6},{1,7},{2,8},{3,9},{4,10},{5,11},{6,12},{7,13},{8,14},{9,15},... | collective-permute-start | bytes 24584 | tf_op jit(solution)/shard_map/ppermute | solution.py:497
  30.1 4.2 %collective-permute-start.6 = (f32[16,128]{1,0:T(8,128)}, f32[16,128]{1,0:T(8,128)S(1)}, u32[]{:S(2)}, u32[]{:S(2)}) collective-permute-start(f32[16,128]{1,0:T(8,128)} %get-tuple-element.23.refs_0_.own_ref), channel_id=1, source_target_pairs={{0,3},{1,4},{2,5},{3,6},{4,7},{5,8},{6,9},{7,10},{8,11},{9,12},{10... | collective-permute-start | bytes 24584 | tf_op jit(solution)/shard_map/ppermute | solution.py:497
  32.7 1.6 %copy-start.7 = (f32[16,128]{1,0:T(8,128)}, f32[16,128]{1,0:T(8,128)S(1)}, u32[]{:S(2)}) copy-start(f32[16,128]{1,0:T(8,128)S(1)} %collective-permute-done.7.refs_2_) | copy-start | bytes 24580
  34.2 0.6 %copy-start.8 = (f32[16,128]{1,0:T(8,128)}, f32[16,128]{1,0:T(8,128)S(1)}, u32[]{:S(2)}) copy-start(f32[16,128]{1,0:T(8,128)S(1)} %collective-permute-done.6.refs_1_) | copy-start | bytes 24580
  36.2 8.0 %collective-permute-start.8 = (f32[16,128]{1,0:T(8,128)}, f32[16,128]{1,0:T(8,128)S(1)}, u32[]{:S(2)}, u32[]{:S(2)}) collective-permute-start(f32[16,128]{1,0:T(8,128)} %add.2.refs_0_), channel_id=1, source_target_pairs={{0,9},{1,10},{2,11},{3,12},{4,13},{5,14},{6,15},{25,16},{26,17},{2... | collective-permute-start | bytes 24584 | tf_op jit(solution)/shard_map/ppermute | solution.py:497
  44.1 0.6 %copy-start.6 = (f32[16,128]{1,0:T(8,128)}, f32[16,128]{1,0:T(8,128)S(1)}, u32[]{:S(2)}) copy-start(f32[16,128]{1,0:T(8,128)S(1)} %collective-permute-done.8.refs_1_) | copy-start | bytes 24580
  46.0 0.7 %copy-start = (f32[10,64,128]{2,1,0:T(8,128)}, f32[10,64,128]{2,1,0:T(8,128)S(1)}, u32[]{:S(2)}) copy-start(f32[10,64,128]{2,1,0:T(8,128)S(1)} %collective-permute-done.4.low_ref) | copy-start | bytes 983044
  46.8 0.7 %copy-start.1 = (f32[10,64,128]{2,1,0:T(8,128)}, f32[10,64,128]{2,1,0:T(8,128)S(1)}, u32[]{:S(2)}) copy-start(f32[10,64,128]{2,1,0:T(8,128)S(1)} %collective-permute-done.5.up_ref) | copy-start | bytes 983044
where the time goes:
time: 54.9 us; the launch traced here: 54.5 us
  starting transfers between devices  25 us (46%)
  Pallas kernels  21 us (38%)
  local copies, waits for them, and re-layouts  4.52 us (8%)
  waiting for transfers between devices  3.12 us (6%)
  between operations  0.75 us (1%)
    ppermute x3, starting transfers between devices, shards(): parts.append(lax.ppermute(width, 'curve', pairs))  13.4 us
    ppermute x4, starting transfers between devices, shards(): received[3 - b] = lax.ppermute(sends[b], 'curve', pairs)  8.71 us
    pallas_call x1, Pallas kernels, shards(): call(refine_kernel, [(5, 64, E_NEW), (1, E_NEW)], [VMEM] * 10, [pltpu.VME...  6.96 us
    pallas_call x1, Pallas kernels, shards(): call(local_kernel, [(5 * groups, 64, LANES), (5 * groups, 64, LANES), (6,...  5.41 us
    pallas_call x1, Pallas kernels, shards(): call(face_kernel, [(5 * groups // 2, 64, LANES), (5 * groups // 2, 64, LA...  3.63 us
    unnamed x18, local copies, waits for them, and re-layouts  3.27 us
    ppermute x3, waiting for transfers between devices, shards(): parts.append(lax.ppermute(width, 'curve', pairs))  3.1 us
    pallas_call x2, Pallas kernels, shards(): call(add_kernel, [(16, LANES)], [VMEM] * len(parts), [], 'add')(*parts)[0]  2.63 us
  transfers between devices with their start and end apart: 9, of which 2 were waited for; matrix products, arithmetic and copies ran while one was open for 0% of the time, Pallas kernels for 15%

commit v1 on v0

--- a/solution.py
+++ b/solution.py
@@ -111,12 +111,13 @@
 def send_kernel(u_ref, idx_ref, jac_ref, flag_ref, *rest):
     outs, lhs, gathered = rest[:4], rest[4], rest[5]
     elements = u_ref.shape[2]
-    slots = idx_ref.shape[1] // 4
+    slots = idx_ref.shape[0] * LANES // 4
     for v in range(5):
         high, low = split_two(u_ref[v])
         lhs[v * 64 : (v + 1) * 64, :] = high
         lhs[320 + v * 64 : 320 + (v + 1) * 64, :] = low
-    row = jnp.broadcast_to(idx_ref[...], (8, 4 * slots))
+    row = jnp.concatenate([idx_ref[r : r + 1, :] for r in range(idx_ref.shape[0])], axis=1)
+    row = jnp.broadcast_to(row, (8, 4 * slots))
     row = jnp.concatenate([row, jnp.zeros((8, 512 - 4 * slots), jnp.int32)], axis=1)
     blocks = [row[:, :LANES]]
     for b in range(1, 4):
@@ -439,6 +440,7 @@
         out_specs=tuple(VMEM for _ in outs),
         scratch_shapes=scratch,
         name=name,
+        compiler_params=pltpu.CompilerParams(vmem_limit_bytes=16 << 20),
     )
 
 
@@ -447,7 +449,7 @@
     groups = elements // LANES
     total = lax.axis_size("curve")
     half = total // 2
-    idx = send_index.reshape(1, -1)
+    idx = send_index.reshape(-1, LANES)
     jac = inverse_jacobian.reshape(groups, LANES)
     flags = refine_flags.reshape(groups, LANES)
     degrees = np.arange(4)

time: 54.9 us -> 46.4 us (0.85)
  Pallas kernels: 21 us -> 12.1 us
  local copies, waits for them, and re-layouts: 4.52 us -> 5.3 us
    pallas_call x2, Pallas kernels: 2.63 us -> 0.01 us  [shards(): call(add_kernel, [(16, LANES)], [VMEM] * len(parts), [], 'add')(*parts)[0]]
    unnamed x18, local copies, waits for them, and re-layouts: 3.27 us -> 5.3 us
    pallas_call x1, Pallas kernels: 2.41 us -> 0.61 us  [shards(): call(send_kernel, [(88, LANES)] * 4, [VMEM] * 4, [pltpu.VMEM((640, elemen...]
    pallas_call x1, Pallas kernels: 3.63 us -> 1.89 us  [shards(): call(face_kernel, [(5 * groups // 2, 64, LANES), (5 * groups // 2, 64, LA...]
    pallas_call x1, Pallas kernels: 5.41 us -> 3.91 us  [shards(): call(local_kernel, [(5 * groups, 64, LANES), (5 * groups, 64, LANES), (6,...]
    pallas_call x1, Pallas kernels: 6.96 us -> 5.64 us  [shards(): call(refine_kernel, [(5, 64, E_NEW), (1, E_NEW)], [VMEM] * 10, [pltpu.VME...]
    reshape x1 -> x0, local copies, waits for them, and re-layouts: 1.25 us -> none  [shards(): idx = send_index.reshape(1, -1)]
  transfers between devices with their start and end apart: 9 -> 9, of which waited for: 2 -> 2; matrix products, arithmetic and copies ran while one was open for 0% -> 0% of each run, Pallas kernels for 15% -> 9%
where the time goes in v1:
time: 46.4 us; the launch traced here: 45.9 us
  starting transfers between devices  25.1 us (54%)
  Pallas kernels  12.1 us (26%)
  local copies, waits for them, and re-layouts  5.3 us (11%)
  waiting for transfers between devices  2.71 us (6%)
  between operations  0.78 us (2%)
    ppermute x3, starting transfers between devices, shards(): parts.append(lax.ppermute(width, 'curve', pairs))  13.4 us
    ppermute x4, starting transfers between devices, shards(): received[3 - b] = lax.ppermute(sends[b], 'curve', pairs)  8.82 us
    pallas_call x1, Pallas kernels, shards(): call(refine_kernel, [(5, 64, E_NEW), (1, E_NEW)], [VMEM] * 10, [pltpu.VME...  5.64 us
    unnamed x18, local copies, waits for them, and re-layouts  5.3 us
    pallas_call x1, Pallas kernels, shards(): call(local_kernel, [(5 * groups, 64, LANES), (5 * groups, 64, LANES), (6,...  3.91 us
    ppermute x3, waiting for transfers between devices, shards(): parts.append(lax.ppermute(width, 'curve', pairs))  2.69 us
    pallas_call x1, Pallas kernels, shards(): call(face_kernel, [(5 * groups // 2, 64, LANES), (5 * groups // 2, 64, LA...  1.89 us
    ppermute x1, starting transfers between devices, shards(): lax.ppermute(tail, 'curve', [(i, i + 1) for i in range(total - 1)])  1.59 us
  transfers between devices with their start and end apart: 9, of which 2 were waited for; matrix products, arithmetic and copies ran while one was open for 0% of the time, Pallas kernels for 9%

profile of v1, /device:TPU:0, one launch (start us, length us, event | category | flops | bytes accessed | tf_op | source)
XLA Modules:
  0.0 45.9 jit_solution(16524931447017553298)
XLA Ops:
  0.6 1.1 %copy-done = f32[5,64,512]{2,1,0:T(8,128)S(1)} copy-done((f32[5,64,512]{2,1,0:T(8,128)S(1)}, f32[5,64,512]{2,1,0:T(8,128)}, u32[]{:S(2)}) %copy-start) | copy-done | bytes 655384
  1.7 0.7 %copy-done.3 = f32[512]{0:T(512)S(1)} copy-done((f32[512]{0:T(512)S(1)}, f32[512]{0:T(512)}, u32[]{:S(2)}) %copy-start.3) | copy-done | bytes 2072
  2.4 0.7 %copy-done.5 = s32[512]{0:T(512)S(1)} copy-done((s32[512]{0:T(512)S(1)}, s32[512]{0:T(512)}, u32[]{:S(2)}) %copy-start.5) | copy-done | bytes 2072
  3.1 0.7 %copy-done.8 = s32[384]{0:T(512)S(1)} copy-done((s32[384]{0:T(512)S(1)}, s32[384]{0:T(512)}, u32[]{:S(2)}) %copy-start.8) | copy-done | bytes 1560
  3.8 0.6 %send.1 = (f32[88,128]{1,0:T(8,128)S(1)}, f32[88,128]{1,0:T(8,128)S(1)}, f32[88,128]{1,0:T(8,128)S(1)}, f32[88,128]{1,0:T(8,128)S(1)}) custom-call(f32[5,64,512]{2,1,0:T(8,128)S(1)} %copy-done, s32[3,128]{1,0:T(4,128)S(1)} %bitcast.11, f32[4,128]{1,0:T(4,128)S(1)} %bitcast.4, s32[4,128]{1,0:T(4,128)S(1)} %bitcast.8), custom_call_target="tpu_custom_call" | custom-call | tf_op jit(solution)/shard_map/send/pallas_call | solution.py:460
  4.4 3.0 %collective-permute-start = (f32[88,128]{1,0:T(8,128)S(1)}, f32[88,128]{1,0:T(8,128)S(1)}, u32[]{:S(2)}, u32[]{:S(2)}) collective-permute-start(f32[88,128]{1,0:T(8,128)S(1)} %get-tuple-element.17), channel_id=1, source_target_pairs={{0,2},{1,3},{2,4},{3,5},{4,6},{5,7},{6,8},{7,9},{8,10},{9,11},{10,... | collective-permute-start | bytes 135176 | tf_op jit(solution)/shard_map/ppermute | solution.py:470
  7.4 0.0 collective-permute-start.1
  7.4 5.3 %collective-permute-start.2 = (f32[88,128]{1,0:T(8,128)S(1)}, f32[88,128]{1,0:T(8,128)S(1)}, u32[]{:S(2)}, u32[]{:S(2)}) collective-permute-start(f32[88,128]{1,0:T(8,128)S(1)} %get-tuple-element.19), channel_id=1, source_target_pairs={{0,31},{1,0},{2,1},{3,2},{4,3},{5,4},{6,5},{7,6},{8,7},{9,8},{10,9... | collective-permute-start | bytes 135176 | tf_op jit(solution)/shard_map/ppermute | solution.py:470
  12.8 0.5 %collective-permute-start.3 = (f32[88,128]{1,0:T(8,128)S(1)}, f32[88,128]{1,0:T(8,128)S(1)}, u32[]{:S(2)}, u32[]{:S(2)}) collective-permute-start(f32[88,128]{1,0:T(8,128)S(1)} %get-tuple-element.20), channel_id=1, source_target_pairs={{0,30},{1,31},{2,0},{3,1},{4,2},{5,3},{6,4},{7,5},{8,6},{9,7},{10,... | collective-permute-start | bytes 135176 | tf_op jit(solution)/shard_map/ppermute | solution.py:470
  13.2 0.7 %copy-done.1 = s32[6,512]{1,0:T(8,128)S(1)} copy-done((s32[6,512]{1,0:T(8,128)S(1)}, s32[6,512]{1,0:T(8,128)}, u32[]{:S(2)}) %copy-start.1) | copy-done | bytes 12312
  13.9 0.8 %copy-done.2 = f32[64,128]{1,0:T(8,128)S(1)} copy-done((f32[64,128]{1,0:T(8,128)S(1)}, f32[64,128]{1,0:T(8,128)}, u32[]{:S(2)}) %copy-start.2) | copy-done | bytes 32792
  14.7 0.7 %copy-done.7 = f32[3,5]{1,0:T(4,128)S(1)} copy-done((f32[3,5]{1,0:T(4,128)S(1)}, f32[3,5]{1,0:T(4,128)}, u32[]{:S(2)}) %copy-start.7) | copy-done | bytes 84
  15.4 3.9 %local.1 = (f32[20,64,128]{2,1,0:T(8,128)S(1)}, f32[20,64,128]{2,1,0:T(8,128)S(1)}, f32[6,80,512]{2,1,0:T(8,128)S(1)}) custom-call(f32[5,64,512]{2,1,0:T(8,128)S(1)} %copy-done, f32[4,128]{1,0:T(4,128)S(1)} %bitcast.5, s32[6,512]{1,0:T(8,128)S(1)} %copy-done.1, f32[3,5]{1,0:T(4,128)S(1)} %copy-done.7, f32[64,128]{1,0:T(8,128)S(1)} %copy-done.2), custom_call_target="tpu_custom_call" | custom-call | tf_op jit(solution)/shard_map/local/pallas_call | solution.py:472
  19.3 0.0 copy-start.4
  19.3 0.0 collective-permute-done.r0
  19.4 1.9 %faces.1 = (f32[10,64,128]{2,1,0:T(8,128)S(1)}, f32[10,64,128]{2,1,0:T(8,128)S(1)}, f32[16,128]{1,0:T(8,128)S(1)}) custom-call(f32[20,64,128]{2,1,0:T(8,128)S(1)} %get-tuple-element.14.base_ref, f32[20,64,128]{2,1,0:T(8,128)S(1)} %get-tuple-element.15.slab_ref, f32[6,80,512]{2,1,0:T(8,128)S(1)} %get-tuple-element.16.out_ref, s32[6,512]{1,0:T(8,128)S(1)} %copy-done.1, ...), custom_call_target="tpu_custom_call" | custom-call | tf_op jit(solution)/shard_map/faces/pallas_call | solution.py:480
  21.3 1.6 %collective-permute-start.4 = (f32[10,64,128]{2,1,0:T(8,128)S(1)}, f32[10,64,128]{2,1,0:T(8,128)S(1)}, u32[]{:S(2)}, u32[]{:S(2)}) collective-permute-start(f32[10,64,128]{2,1,0:T(8,128)S(1)} %get-tuple-element.21.tail_ref), channel_id=1, source_target_pairs={{0,1},{1,2},{2,3},{3,4},{4,5},{5,6},{6,7},{7,8},{8,9},{9,10},{10,1... | collective-permute-start | bytes 983048 | tf_op jit(solution)/shard_map/ppermute | solution.py:488
  22.9 1.3 %collective-permute-start.5 = (f32[10,64,128]{2,1,0:T(8,128)S(1)}, f32[10,64,128]{2,1,0:T(8,128)S(1)}, u32[]{:S(2)}, u32[]{:S(2)}) collective-permute-start(f32[10,64,128]{2,1,0:T(8,128)S(1)} %get-tuple-element.22.head_ref), channel_id=1, source_target_pairs={{1,0},{2,1},{3,2},{4,3},{5,4},{6,5},{7,6},{8,7},{9,8},{10,9},{11,1... | collective-permute-start | bytes 983048 | tf_op jit(solution)/shard_map/ppermute | solution.py:489
  24.2 4.4 %collective-permute-start.7 = (f32[16,128]{1,0:T(8,128)S(1)}, f32[16,128]{1,0:T(8,128)S(1)}, u32[]{:S(2)}, u32[]{:S(2)}) collective-permute-start(f32[16,128]{1,0:T(8,128)S(1)} %get-tuple-element.23.refs_0_.own_ref), channel_id=1, source_target_pairs={{0,6},{1,7},{2,8},{3,9},{4,10},{5,11},{6,12},{7,13},{8,14},{9,15},... | collective-permute-start | bytes 24584 | tf_op jit(solution)/shard_map/ppermute | solution.py:499
  28.6 2.6 %collective-permute-start.6 = (f32[16,128]{1,0:T(8,128)S(1)}, f32[16,128]{1,0:T(8,128)S(1)}, u32[]{:S(2)}, u32[]{:S(2)}) collective-permute-start(f32[16,128]{1,0:T(8,128)S(1)} %get-tuple-element.23.refs_0_.own_ref), channel_id=1, source_target_pairs={{0,3},{1,4},{2,5},{3,6},{4,7},{5,8},{6,9},{7,10},{8,11},{9,12},{10... | collective-permute-start | bytes 24584 | tf_op jit(solution)/shard_map/ppermute | solution.py:499
  31.2 1.3 %collective-permute-done.6.refs_1_ = f32[16,128]{1,0:T(8,128)S(1)} collective-permute-done((f32[16,128]{1,0:T(8,128)S(1)}, f32[16,128]{1,0:T(8,128)S(1)}, u32[]{:S(2)}, u32[]{:S(2)}) %collective-permute-start.6) | collective-permute-done | bytes 8224 | tf_op jit(solution)/shard_map/ppermute | solution.py:499
  32.5 6.4 %collective-permute-start.8 = (f32[16,128]{1,0:T(8,128)S(1)}, f32[16,128]{1,0:T(8,128)S(1)}, u32[]{:S(2)}, u32[]{:S(2)}) collective-permute-start(f32[16,128]{1,0:T(8,128)S(1)} %add.2.refs_0_), channel_id=1, source_target_pairs={{0,9},{1,10},{2,11},{3,12},{4,13},{5,14},{6,15},{25,16},{26,17},{2... | collective-permute-start | bytes 24584 | tf_op jit(solution)/shard_map/ppermute | solution.py:499
  38.9 1.3 %collective-permute-done.8.refs_1_ = f32[16,128]{1,0:T(8,128)S(1)} collective-permute-done((f32[16,128]{1,0:T(8,128)S(1)}, f32[16,128]{1,0:T(8,128)S(1)}, u32[]{:S(2)}, u32[]{:S(2)}) %collective-permute-start.8) | collective-permute-done | bytes 8224 | tf_op jit(solution)/shard_map/ppermute | solution.py:499
  40.3 5.6 %refine.1 = (f32[5,64,960]{2,1,0:T(8,128)}, f32[1,960]{1,0:T(1,128)}) custom-call(f32[10,64,128]{2,1,0:T(8,128)S(1)} %collective-permute-done.4.low_ref, f32[10,64,128]{2,1,0:T(8,128)S(1)} %get-tuple-element.22.head_ref, f32[10,64,128]{2,1,0:T(8,128)S(1)} %get-tuple-element.21.tail_ref, f32[10,64,128]{2,1,0:T(8,128)S(1)} %collective-permute-done.5.up_ref, ...), custom_call_target="tpu_custom_call" | custom-call | tf_op jit(solution)/shard_map/refine/pallas_call | solution.py:503
  (18 shorter events, 0.0 us)
Async XLA Ops:
  0.6 18.7 %copy-start.6 = (s32[512]{0:T(512)S(1)}, s32[512]{0:T(512)}, u32[]{:S(2)}) copy-start(s32[512]{0:T(512)} %param.10) | copy-start | bytes 6148
  0.6 1.1 %copy-start = (f32[5,64,512]{2,1,0:T(8,128)S(1)}, f32[5,64,512]{2,1,0:T(8,128)}, u32[]{:S(2)}) copy-start(f32[5,64,512]{2,1,0:T(8,128)} %u_ref.3) | copy-start | bytes 1966084
  1.7 0.7 %copy-start.3 = (f32[512]{0:T(512)S(1)}, f32[512]{0:T(512)}, u32[]{:S(2)}) copy-start(f32[512]{0:T(512)} %param.8) | copy-start | bytes 6148
  2.4 0.7 %copy-start.5 = (s32[512]{0:T(512)S(1)}, s32[512]{0:T(512)}, u32[]{:S(2)}) copy-start(s32[512]{0:T(512)} %param.10) | copy-start | bytes 6148
  3.1 0.7 %copy-start.8 = (s32[384]{0:T(512)S(1)}, s32[384]{0:T(512)}, u32[]{:S(2)}) copy-start(s32[384]{0:T(512)} %param.11) | copy-start | bytes 4612
  4.4 14.9 %collective-permute-start = (f32[88,128]{1,0:T(8,128)S(1)}, f32[88,128]{1,0:T(8,128)S(1)}, u32[]{:S(2)}, u32[]{:S(2)}) collective-permute-start(f32[88,128]{1,0:T(8,128)S(1)} %get-tuple-element.17), channel_id=1, source_target_pairs={{0,2},{1,3},{2,4},{3,5},{4,6},{5,7},{6,8},{7,9},{8,10},{9,11},{10,... | collective-permute-start | bytes 135176 | tf_op jit(solution)/shard_map/ppermute | solution.py:470
  7.4 11.9 %collective-permute-start.1 = (f32[88,128]{1,0:T(8,128)S(1)}, f32[88,128]{1,0:T(8,128)S(1)}, u32[]{:S(2)}, u32[]{:S(2)}) collective-permute-start(f32[88,128]{1,0:T(8,128)S(1)} %get-tuple-element.18), channel_id=1, source_target_pairs={{0,1},{1,2},{2,3},{3,4},{4,5},{5,6},{6,7},{7,8},{8,9},{9,10},{10,1... | collective-permute-start | bytes 135176 | tf_op jit(solution)/shard_map/ppermute | solution.py:470
  7.4 11.9 %collective-permute-start.2 = (f32[88,128]{1,0:T(8,128)S(1)}, f32[88,128]{1,0:T(8,128)S(1)}, u32[]{:S(2)}, u32[]{:S(2)}) collective-permute-start(f32[88,128]{1,0:T(8,128)S(1)} %get-tuple-element.19), channel_id=1, source_target_pairs={{0,31},{1,0},{2,1},{3,2},{4,3},{5,4},{6,5},{7,6},{8,7},{9,8},{10,9... | collective-permute-start | bytes 135176 | tf_op jit(solution)/shard_map/ppermute | solution.py:470
  12.8 6.6 %collective-permute-start.3 = (f32[88,128]{1,0:T(8,128)S(1)}, f32[88,128]{1,0:T(8,128)S(1)}, u32[]{:S(2)}, u32[]{:S(2)}) collective-permute-start(f32[88,128]{1,0:T(8,128)S(1)} %get-tuple-element.20), channel_id=1, source_target_pairs={{0,30},{1,31},{2,0},{3,1},{4,2},{5,3},{6,4},{7,5},{8,6},{9,7},{10,... | collective-permute-start | bytes 135176 | tf_op jit(solution)/shard_map/ppermute | solution.py:470
  13.2 0.7 %copy-start.1 = (s32[6,512]{1,0:T(8,128)S(1)}, s32[6,512]{1,0:T(8,128)}, u32[]{:S(2)}) copy-start(s32[6,512]{1,0:T(8,128)} %fs_ref.3) | copy-start | bytes 36868
  13.9 0.8 %copy-start.2 = (f32[64,128]{1,0:T(8,128)S(1)}, f32[64,128]{1,0:T(8,128)}, u32[]{:S(2)}) copy-start(f32[64,128]{1,0:T(8,128)} %constant.2.clone.modes_ref) | copy-start | bytes 98308
  14.7 0.7 %copy-start.7 = (f32[3,5]{1,0:T(4,128)S(1)}, f32[3,5]{1,0:T(4,128)}, u32[]{:S(2)}) copy-start(f32[3,5]{1,0:T(4,128)} %sp_ref.3) | copy-start | bytes 184
  19.3 21.0 %copy-start.4 = (f32[512]{0:T(512)S(1)}, f32[512]{0:T(512)}, u32[]{:S(2)}) copy-start(f32[512]{0:T(512)} %param.8) | copy-start | bytes 6148
  21.3 19.0 %collective-permute-start.4 = (f32[10,64,128]{2,1,0:T(8,128)S(1)}, f32[10,64,128]{2,1,0:T(8,128)S(1)}, u32[]{:S(2)}, u32[]{:S(2)}) collective-permute-start(f32[10,64,128]{2,1,0:T(8,128)S(1)} %get-tuple-element.21.tail_ref), channel_id=1, source_target_pairs={{0,1},{1,2},{2,3},{3,4},{4,5},{5,6},{6,7},{7,8},{8,9},{9,10},{10,1... | collective-permute-start | bytes 983048 | tf_op jit(solution)/shard_map/ppermute | solution.py:488
  22.9 17.4 %collective-permute-start.5 = (f32[10,64,128]{2,1,0:T(8,128)S(1)}, f32[10,64,128]{2,1,0:T(8,128)S(1)}, u32[]{:S(2)}, u32[]{:S(2)}) collective-permute-start(f32[10,64,128]{2,1,0:T(8,128)S(1)} %get-tuple-element.22.head_ref), channel_id=1, source_target_pairs={{1,0},{2,1},{3,2},{4,3},{5,4},{6,5},{7,6},{8,7},{9,8},{10,9},{11,1... | collective-permute-start | bytes 983048 | tf_op jit(solution)/shard_map/ppermute | solution.py:489
  24.2 7.0 %collective-permute-start.7 = (f32[16,128]{1,0:T(8,128)S(1)}, f32[16,128]{1,0:T(8,128)S(1)}, u32[]{:S(2)}, u32[]{:S(2)}) collective-permute-start(f32[16,128]{1,0:T(8,128)S(1)} %get-tuple-element.23.refs_0_.own_ref), channel_id=1, source_target_pairs={{0,6},{1,7},{2,8},{3,9},{4,10},{5,11},{6,12},{7,13},{8,14},{9,15},... | collective-permute-start | bytes 24584 | tf_op jit(solution)/shard_map/ppermute | solution.py:499
  28.6 3.9 %collective-permute-start.6 = (f32[16,128]{1,0:T(8,128)S(1)}, f32[16,128]{1,0:T(8,128)S(1)}, u32[]{:S(2)}, u32[]{:S(2)}) collective-permute-start(f32[16,128]{1,0:T(8,128)S(1)} %get-tuple-element.23.refs_0_.own_ref), channel_id=1, source_target_pairs={{0,3},{1,4},{2,5},{3,6},{4,7},{5,8},{6,9},{7,10},{8,11},{9,12},{10... | collective-permute-start | bytes 24584 | tf_op jit(solution)/shard_map/ppermute | solution.py:499
  32.5 7.8 %collective-permute-start.8 = (f32[16,128]{1,0:T(8,128)S(1)}, f32[16,128]{1,0:T(8,128)S(1)}, u32[]{:S(2)}, u32[]{:S(2)}) collective-permute-start(f32[16,128]{1,0:T(8,128)S(1)} %add.2.refs_0_), channel_id=1, source_target_pairs={{0,9},{1,10},{2,11},{3,12},{4,13},{5,14},{6,15},{25,16},{26,17},{2... | collective-permute-start | bytes 24584 | tf_op jit(solution)/shard_map/ppermute | solution.py:499

commit v2 on v1

--- a/solution.py
+++ b/solution.py
@@ -108,14 +108,32 @@
     return jnp.dot(a, b, preferred_element_type=F32)
 
 
-def send_kernel(u_ref, idx_ref, jac_ref, flag_ref, *rest):
-    outs, lhs, gathered = rest[:4], rest[4], rest[5]
-    elements = u_ref.shape[2]
+def send_kernel(u_hbm, idx_hbm, jac_hbm, flag_hbm, fs_hbm, sp_hbm, modes_hbm, *rest):
+    outs = rest[:4]
+    slab_ref, jac_ref, flag_ref, fs_ref, speed_ref, modes_ref = rest[4:10]
+    lhs, gathered, idx_ref, flag_raw, sp_ref, sems = rest[10:]
+    elements = u_hbm.shape[2]
+    groups = elements // LANES
+    loads = [pltpu.make_async_copy(idx_hbm, idx_ref, sems.at[0])]
+    for g in range(groups):
+        for v in range(5):
+            loads.append(
+                pltpu.make_async_copy(
+                    u_hbm.at[v, :, pl.ds(g * LANES, LANES)], slab_ref.at[g * 5 + v], sems.at[len(loads)]
+                )
+            )
+    for src, dst in (
+        (jac_hbm, jac_ref),
+        (flag_hbm, flag_raw),
+        (fs_hbm, fs_ref),
+        (sp_hbm, sp_ref),
+        (modes_hbm, modes_ref),
+    ):
+        loads.append(pltpu.make_async_copy(src, dst, sems.at[len(loads)]))
+    for load in loads:
+        load.start()
+    loads[0].wait()
     slots = idx_ref.shape[0] * LANES // 4
-    for v in range(5):
-        high, low = split_two(u_ref[v])
-        lhs[v * 64 : (v + 1) * 64, :] = high
-        lhs[320 + v * 64 : 320 + (v + 1) * 64, :] = low
     row = jnp.concatenate([idx_ref[r : r + 1, :] for r in range(idx_ref.shape[0])], axis=1)
     row = jnp.broadcast_to(row, (8, 4 * slots))
     row = jnp.concatenate([row, jnp.zeros((8, 512 - 4 * slots), jnp.int32)], axis=1)
@@ -127,14 +145,24 @@
     for f in range(1, 6):
         face = face + (idx >= f * elements).astype(jnp.int32)
     elem = idx - face * elements
-    picked = dot32(lhs[...], one_hot(elem[0:1], elements))
+    wanted = one_hot(elem[0:1], elements)
+    for g in range(groups):
+        for v in range(5):
+            loads[1 + g * 5 + v].wait()
+            high, low = split_two(slab_ref[g * 5 + v])
+            lanes = slice(g * LANES, (g + 1) * LANES)
+            lhs[v * 64 : (v + 1) * 64, lanes] = high
+            lhs[320 + v * 64 : 320 + (v + 1) * 64, lanes] = low
+    picked = dot32(lhs[...], wanted)
     for b in range(4):
         part = picked[:320, b * LANES : (b + 1) * LANES] + picked[320:, b * LANES : (b + 1) * LANES]
         gathered[b * 5 : (b + 1) * 5] = part.reshape(5, 64, LANES)
-    flags = flag_ref[...].astype(F32)
+    for load in loads[1 + 5 * groups :]:
+        load.wait()
+    flags = flag_raw[...].astype(F32)
+    flag_ref[...] = flags
     count = elements + 7.0 * jnp.sum(flags)
     rows = lax.broadcasted_iota(jnp.int32, (8, LANES), 0)
-    groups = elements // LANES
     for b in range(4):
         fb = jnp.broadcast_to(face[0:1, b * LANES : (b + 1) * LANES], (16, LANES))
         for v in range(5):
@@ -148,6 +176,9 @@
             meta = jnp.where(rows == r, jac_ref[near + r : near + r + 1, :], meta)
             meta = jnp.where(rows == 2 + r, flags[near + r : near + r + 1, :], meta)
         outs[b][80:88, :] = meta
+    for d in range(3):
+        for v in range(5):
+            speed_ref[d * 5 + v] = jnp.broadcast_to(sp_ref[d : d + 1, v : v + 1], (16, LANES))
 
 
 def line_rates(x, speed, blend):
@@ -184,14 +215,12 @@
     return out
 
 
-def local_kernel(u_ref, jac_ref, fs_ref, sp_ref, modes_ref, base_ref, slab_ref, out_ref, lhs, rows_s):
-    elements = u_ref.shape[2]
-    groups = elements // LANES
-    for v in range(5):
-        for g in range(groups):
-            slab_ref[g * 5 + v] = u_ref[v, :, g * LANES : (g + 1) * LANES]
+def local_kernel(slab_ref, jac_ref, sp_ref, modes_ref, base_ref, first, rows_s):
+    groups = jac_ref.shape[0]
+    for g in range(groups):
+        first[:, g * LANES : (g + 1) * LANES] = slab_ref[g * 5]
     modal = jnp.dot(
-        modes_ref[:, :64], u_ref[0], precision=lax.Precision.HIGHEST, preferred_element_type=F32
+        modes_ref[:, :64], first[...], precision=lax.Precision.HIGHEST, preferred_element_type=F32
     )
     energy = modal * modal
     top = jnp.sum(energy * modes_ref[:, 64:65], axis=0, keepdims=True)
@@ -208,15 +237,16 @@
         blend = rows_s[g]
         scale = rows_s[groups + g]
         low = low_half()
+        speeds = [sp_ref[5 * d + v, 0:8, :] for d in range(3)]
         for kh in range(2):
             at = [(t, pl.ds(32 * kh + i, 8, stride=4), slice(None)) for i in range(4)]
-            rate = line_rates([slab_ref[a] for a in at], sp_ref[0, v], blend)
+            rate = line_rates([slab_ref[a] for a in at], speeds[0], blend)
             for i in range(4):
                 base_ref[at[i]] = rate[i]
         tile = [[slab_ref[t, 16 * k + 8 * h : 16 * k + 8 * h + 8, :] for h in range(2)] for k in range(4)]
         rates = [[None, None] for _ in range(4)]
         for h in range(2):
-            r = line_rates([tile[k][h] for k in range(4)], sp_ref[2, v], blend)
+            r = line_rates([tile[k][h] for k in range(4)], speeds[2], blend)
             for k in range(4):
                 rates[k][h] = r[k]
         for k in (0, 2):
@@ -224,11 +254,11 @@
             for h in range(2):
                 x.append(jnp.where(low, tile[k][h], swap_halves(tile[k + 1][h])))
                 x.append(jnp.where(low, swap_halves(tile[k][h]), tile[k + 1][h]))
-            r = line_rates(x, sp_ref[1, v], blend)
+            r = line_rates(x, speeds[1], blend)
             for h in range(2):
-                first, second = r[2 * h], r[2 * h + 1]
-                rates[k][h] = rates[k][h] + jnp.where(low, first, swap_halves(second))
-                rates[k + 1][h] = rates[k + 1][h] + jnp.where(low, swap_halves(first), second)
+                one_row, two_row = r[2 * h], r[2 * h + 1]
+                rates[k][h] = rates[k][h] + jnp.where(low, one_row, swap_halves(two_row))
+                rates[k + 1][h] = rates[k + 1][h] + jnp.where(low, swap_halves(one_row), two_row)
         for k in range(4):
             for h in range(2):
                 at = (t, slice(16 * k + 8 * h, 16 * k + 8 * h + 8), slice(None))
@@ -237,6 +267,11 @@
 
     lax.fori_loop(0, 5 * groups, one, 0)
 
+
+def outside_kernel(slab_ref, fs_ref, after_ref, out_ref, lhs):
+    del after_ref
+    elements = fs_ref.shape[1]
+    groups = elements // LANES
     for f in range(6):
         partner = f + 1 - 2 * (f % 2)
         for g in range(groups):
@@ -249,8 +284,26 @@
         out_ref[f] = jnp.where(near, picked[:80] + picked[80:], 0.0)
 
 
-def face_kernel(base_ref, slab_ref, out_ref, fs_ref, jac_ref, sp_ref, flag_ref, r0, r1, r2, r3, *rest):
-    head_ref, tail_ref, width_ref, lhs, outside = rest
+def window_kernel(flag_ref, after_ref, r0, r1, r2, r3, width_ref):
+    del after_ref
+    me = lax.axis_index("curve")
+    total = lax.axis_size("curve")
+    lower = me < total // 2
+    elements = flag_ref.shape[0] * LANES
+    count = jnp.full((8, LANES), elements + 7.0 * jnp.sum(flag_ref[...]), F32)
+    own = count
+    for o, ref in zip(OFFSETS, (r0, r1, r2, r3)):
+        there = me + o
+        wanted = jnp.logical_and(lower if o < 0 else jnp.logical_not(lower), jnp.logical_and(there >= 0, there < total))
+        value = jnp.broadcast_to(ref[87:88, :], (8, LANES))
+        count = count + value * jnp.where(wanted, 1.0, 0.0)
+    width_ref[0:8] = count
+    width_ref[8:16] = own
+
+
+def face_kernel(base_ref, slab_ref, out_ref, fs_ref, jac_ref, sp_ref, after_ref, r0, r1, r2, r3, *rest):
+    del after_ref
+    head_ref, tail_ref, lhs, outside = rest
     elements = fs_ref.shape[1]
     groups = elements // LANES
     slots = 96
@@ -275,7 +328,7 @@
         for v in range(5):
             t = g * 5 + v
             for f in range(6):
-                speed = sp_ref[f // 2, v]
+                speed = sp_ref[5 * (f // 2) + v]
                 inner = trace_of(slab_ref, t, f)
                 outer = outside[f, v * 16 : (v + 1) * 16, g * LANES : (g + 1) * LANES]
                 central = inner * inner + inner * outer + outer * outer
@@ -283,39 +336,63 @@
                 sign = 1.0 if f % 2 == 0 else -1.0
                 value = (sign * speed) * central - reach * (inner - outer)
                 add_to_face(ref, (g - first) * 5 + v, f, scale * value)
-    me = lax.axis_index("curve")
-    total = lax.axis_size("curve")
-    lower = me < total // 2
-    count = jnp.full((8, LANES), elements + 7.0 * jnp.sum(flag_ref[...].astype(F32)), F32)
-    own = count
-    for o, ref in zip(OFFSETS, (r0, r1, r2, r3)):
-        there = me + o
-        wanted = jnp.logical_and(lower if o < 0 else jnp.logical_not(lower), jnp.logical_and(there >= 0, there < total))
-        value = jnp.broadcast_to(ref[87:88, :], (8, LANES))
-        count = count + value * jnp.where(wanted, 1.0, 0.0)
-    width_ref[0:8] = count
-    width_ref[8:16] = own
-
-
-def refine_kernel(low_ref, head_ref, tail_ref, up_ref, w_ref, own_ref, r1, r2, jac_ref, flag_ref, *rest):
-    out_ref, jout_ref, lhs, res, coef, cols = rest
-    halves = (low_ref, head_ref, tail_ref, up_ref)
+
+
+EDGE_GROUPS = (0, 1, 5, 6, 7)
+SPANS = ((0, 768), (256, 768), (256, 1024), (256, 1024))
+
+
+def interpolate(res, v, coef, first, store):
+    def apply(d, x):
+        out = []
+        for i in range(4):
+            acc = coef[first + 16 * d + 4 * i] * x[0]
+            for m in range(1, 4):
+                acc = acc + coef[first + 16 * d + 4 * i + m] * x[m]
+            out.append(acc)
+        return out
+
+    low = low_half()
+    for kh in range(2):
+        at = [(v, pl.ds(32 * kh + i, 8, stride=4), slice(None)) for i in range(4)]
+        y = apply(0, [res[a] for a in at])
+        for i in range(4):
+            res[at[i]] = y[i]
+    tile = [[res[v, 16 * k + 8 * q : 16 * k + 8 * q + 8, :] for q in range(2)] for k in range(4)]
+    for q in range(2):
+        y = apply(2, [tile[k][q] for k in range(4)])
+        for k in range(4):
+            tile[k][q] = y[k]
+    for k in (0, 2):
+        x = []
+        for q in range(2):
+            x.append(jnp.where(low, tile[k][q], swap_halves(tile[k + 1][q])))
+            x.append(jnp.where(low, swap_halves(tile[k][q]), tile[k + 1][q]))
+        y = apply(1, x)
+        for q in range(2):
+            one_row, two_row = y[2 * q], y[2 * q + 1]
+            store(16 * k + 8 * q, jnp.where(low, one_row, swap_halves(two_row)))
+            store(16 * (k + 1) + 8 * q, jnp.where(low, swap_halves(one_row), two_row))
+
+
+def own_kernel(head_ref, tail_ref, w_ref, own_ref, r1, r2, jac_ref, flag_ref, *rest):
+    mid_ref, part_ref, low_hot, up_hot, coef_out, jout_ref = rest[:6]
+    lhs, meta, res, coef_mid, cols = rest[6:]
     total = lax.axis_size("curve")
     me = lax.axis_index("curve")
-    for b, ref in enumerate(halves):
+    for b, ref in enumerate((head_ref, tail_ref)):
         for g in range(2):
             high, low = split_two(ref[5 * g : 5 * g + 5].reshape(320, LANES))
             at = slice((2 * b + g) * LANES, (2 * b + g + 1) * LANES)
             lhs[0:320, at] = high
             lhs[320:640, at] = low
     jac = jnp.concatenate([r1[80:82, :], jac_ref[...], r2[80:82, :]], axis=0)
-    flag = jnp.concatenate([r1[82:84, :], flag_ref[...].astype(F32), r2[82:84, :]], axis=0)
+    flag = jnp.concatenate([r1[82:84, :], flag_ref[...], r2[82:84, :]], axis=0)
     sizes = 1.0 + 7.0 * flag
     lane0 = lax.broadcasted_iota(jnp.int32, (LANES, LANES), 0)
     lane1 = lax.broadcasted_iota(jnp.int32, (LANES, LANES), 1)
     upper = jnp.where(lane0 < lane1, 1.0, 0.0).astype(BF)
-    sizes_b = sizes.astype(BF)
-    within = dot32(sizes_b, upper)
+    before = dot32(sizes.astype(BF), upper)
     row_total = jnp.sum(sizes, axis=1, keepdims=True)
     running = jnp.zeros((1, 1), F32)
     starts = []
@@ -323,12 +400,9 @@
         starts.append(running)
         running = running + row_total[r : r + 1]
     row0 = lax.broadcasted_iota(jnp.int32, (8, LANES), 0)
-    before = within
     for r in range(8):
         before = before + jnp.where(row0 == r, starts[r], 0.0)
     width = w_ref[0:8]
-    if own_ref is not None:
-        width = width
     mine = own_ref[8:16]
     lower = jnp.where(me < total // 2, 1.0, 0.0)
     begin = lower * (width - mine) + (1.0 - lower) * (float(total * E_NEW) - width)
@@ -346,25 +420,32 @@
         block = jnp.zeros((16, LANES), F32)
         for q, item in enumerate(extras):
             block = jnp.where(rows16 == q, jnp.broadcast_to(item[r : r + 1, :], (16, LANES)), block)
-        lhs[640:656, r * LANES : (r + 1) * LANES] = block.astype(BF)
-        cols[0, r * LANES : (r + 1) * LANES, :] = jnp.transpose(jnp.broadcast_to(place[r : r + 1, :], (LANES, LANES)))
-        cols[1, r * LANES : (r + 1) * LANES, :] = jnp.transpose(jnp.broadcast_to(ends[r : r + 1, :], (LANES, LANES)))
-
-    spans = ((0, 768), (256, 768), (256, 1024), (256, 1024))
-    for pair, (k0, k1) in enumerate(spans):
+        at = slice(r * LANES, (r + 1) * LANES)
+        meta[:, at] = block.astype(BF)
+        cols[0, at, :] = jnp.transpose(jnp.broadcast_to(place[r : r + 1, :], (LANES, LANES)))
+        cols[1, at, :] = jnp.transpose(jnp.broadcast_to(ends[r : r + 1, :], (LANES, LANES)))
+
+    for pair, (k0, k1) in enumerate(SPANS):
         pieces = []
         for h in range(2):
             slot = (lax.broadcasted_iota(jnp.int32, (8, LANES), 1) + (2 * pair + h) * LANES).astype(F32)
             slot_b = jnp.broadcast_to(slot[0:1], (k1 - k0, LANES))
             hit = jnp.logical_and(slot_b >= cols[0, k0:k1, :], slot_b < cols[1, k0:k1, :])
             pieces.append(jnp.where(hit, 1.0, 0.0).astype(BF))
-        picked = dot32(lhs[:, k0:k1], jnp.concatenate(pieces, axis=1))
+        hot = jnp.concatenate(pieces, axis=1)
+        if pair == 0:
+            low_hot[...] = hot[0:256]
+        elif pair == 2:
+            up_hot[:, 0:LANES] = hot[512:768, LANES : 2 * LANES]
+        elif pair == 3:
+            up_hot[:, LANES : 3 * LANES] = hot[512:768]
+        picked = dot32(lhs[...], hot[256 - k0 : 768 - k0])
+        known = dot32(meta[:, k0:k1], hot)
         for h in range(2):
             g = 2 * pair + h
             lanes = slice(h * LANES, (h + 1) * LANES)
             width_at = min(LANES, E_NEW - g * LANES)
-            res[...] = (picked[0:320, lanes] + picked[320:640, lanes]).reshape(5, 64, LANES)
-            extra = picked[640:656, lanes]
+            extra = known[:, lanes]
             jac_new = (extra[0:1] + extra[1:2] + extra[2:3]) * (1.0 + extra[3:4])
             jout_ref[0:1, g * LANES : g * LANES + width_at] = jac_new[:, :width_at]
             fl = jnp.broadcast_to(extra[3:4], (8, LANES))
@@ -374,51 +455,58 @@
             child = child - 4.0 * bit2
             bit1 = jnp.where(child >= 2.0, 1.0, 0.0)
             bit0 = child - 2.0 * bit1
+            edge = g in EDGE_GROUPS
+            coef, first = (coef_out, 48 * EDGE_GROUPS.index(g)) if edge else (coef_mid, 48 * (g - 2))
             for d, bit in enumerate((bit0, bit1, bit2)):
                 both = fl * bit
                 for i in range(4):
                     for m in range(4):
                         eye = 1.0 if i == m else 0.0
                         c = fl * float(SIDES[0][i, m] - eye) + both * float(SIDES[1][i, m] - SIDES[0][i, m]) + eye
-                        coef[16 * d + 4 * i + m] = c
-
-            def apply(d, x):
-                out = []
-                for i in range(4):
-                    acc = coef[16 * d + 4 * i] * x[0]
-                    for m in range(1, 4):
-                        acc = acc + coef[16 * d + 4 * i + m] * x[m]
-                    out.append(acc)
-                return out
-
-            def one(v, carry):
-                low = low_half()
-                for kh in range(2):
-                    at = [(v, pl.ds(32 * kh + i, 8, stride=4), slice(None)) for i in range(4)]
-                    y = apply(0, [res[a] for a in at])
-                    for i in range(4):
-                        res[at[i]] = y[i]
-                tile = [[res[v, 16 * k + 8 * q : 16 * k + 8 * q + 8, :] for q in range(2)] for k in range(4)]
-                for q in range(2):
-                    y = apply(2, [tile[k][q] for k in range(4)])
-                    for k in range(4):
-                        tile[k][q] = y[k]
-                for k in (0, 2):
-                    x = []
-                    for q in range(2):
-                        x.append(jnp.where(low, tile[k][q], swap_halves(tile[k + 1][q])))
-                        x.append(jnp.where(low, swap_halves(tile[k][q]), tile[k + 1][q]))
-                    y = apply(1, x)
-                    for q in range(2):
-                        first, second = y[2 * q], y[2 * q + 1]
-                        a = jnp.where(low, first, swap_halves(second))
-                        b = jnp.where(low, swap_halves(first), second)
-                        lanes_out = slice(g * LANES, g * LANES + width_at)
-                        out_ref[v, 16 * k + 8 * q : 16 * k + 8 * q + 8, lanes_out] = a[:, :width_at]
-                        out_ref[v, 16 * (k + 1) + 8 * q : 16 * (k + 1) + 8 * q + 8, lanes_out] = b[:, :width_at]
-                return carry
-
-            lax.fori_loop(0, 5, one, 0)
+                        coef[first + 16 * d + 4 * i + m] = c
+            value = (picked[0:320, lanes] + picked[320:640, lanes]).reshape(5, 64, LANES)
+            if edge:
+                q = EDGE_GROUPS.index(g)
+                part_ref[5 * q : 5 * q + 5] = value
+            else:
+                res[...] = value
+
+                def one(v, carry, g=g, first=first):
+                    def store(row, x):
+                        mid_ref[5 * (g - 2) + v, row : row + 8, :] = x
+
+                    interpolate(res, v, coef_mid, first, store)
+                    return carry
+
+                lax.fori_loop(0, 5, one, 0)
+
+
+def edge_kernel(low_ref, up_ref, mid_ref, part_ref, low_hot, up_hot, coef_ref, out_hbm, lhs, res, out, sems):
+    for b, ref in enumerate((low_ref, up_ref)):
+        for g in range(2):
+            high, low = split_two(ref[5 * g : 5 * g + 5].reshape(320, LANES))
+            at = slice((2 * b + g) * LANES, (2 * b + g + 1) * LANES)
+            lhs[0:320, at] = high
+            lhs[320:640, at] = low
+    picked = (dot32(lhs[:, 0:256], low_hot[...]), dot32(lhs[:, 256:512], up_hot[...]))
+    for q, g in enumerate(EDGE_GROUPS):
+        from_up = int(g >= 5)
+        at = (g - 5 * from_up) * LANES
+        value = picked[from_up][0:320, at : at + LANES] + picked[from_up][320:640, at : at + LANES]
+        res[5 * q : 5 * q + 5] = part_ref[5 * q : 5 * q + 5] + value.reshape(5, 64, LANES)
+    for v in range(5):
+        for g in (2, 3, 4):
+            out[v, :, g * LANES : (g + 1) * LANES] = mid_ref[5 * (g - 2) + v]
+        for q, g in enumerate(EDGE_GROUPS):
+            width_at = min(LANES, E_NEW - g * LANES)
+
+            def store(row, x, v=v, g=g, width_at=width_at):
+                out[v, row : row + 8, g * LANES : g * LANES + width_at] = x[:, :width_at]
+
+            interpolate(res, 5 * q + v, coef_ref, 48 * q, store)
+        pltpu.make_async_copy(out.at[v], out_hbm.at[v], sems.at[v]).start()
+    for v in range(5):
+        pltpu.make_async_copy(out.at[v], out_hbm.at[v], sems.at[v]).wait()
 
 
 def add_kernel(*refs):
@@ -429,15 +517,23 @@
 
 
 VMEM = pl.BlockSpec(memory_space=pltpu.MemorySpace.VMEM)
-SMEM = pl.BlockSpec(memory_space=pltpu.MemorySpace.SMEM)
-
-
-def call(body, outs, specs, scratch, name):
+HBM = pl.BlockSpec(memory_space=pltpu.MemorySpace.HBM)
+
+
+def in_hbm(x):
+    return pltpu.with_memory_space_constraint(x, pltpu.MemorySpace.HBM)
+
+
+def call(body, outs, specs, scratch, name, out_spec=VMEM, flops=100_000_000):
+    shapes = []
+    for item in outs:
+        shape, dtype = item if isinstance(item[0], tuple) else (item, F32)
+        shapes.append(jax.ShapeDtypeStruct(shape, dtype))
     return pl.pallas_call(
         body,
-        out_shape=tuple(jax.ShapeDtypeStruct(s, F32) for s in outs),
+        out_shape=tuple(shapes),
         in_specs=specs,
-        out_specs=tuple(VMEM for _ in outs),
+        out_specs=tuple(out_spec for _ in outs),
         scratch_shapes=scratch,
         name=name,
         compiler_params=pltpu.CompilerParams(vmem_limit_bytes=16 << 20),
@@ -456,62 +552,108 @@
     top = (np.maximum(np.maximum(degrees[:, None, None], degrees[None, :, None]), degrees) == 3).reshape(64, 1)
     kron = np.kron(MODES, np.kron(MODES, MODES))
     modes = jnp.asarray(np.concatenate([kron, np.repeat(top, 64, axis=1)], axis=1), F32)
-
-    sends = call(
+    slabs = 5 * groups
+
+    outs = call(
         send_kernel,
-        [(88, LANES)] * 4,
-        [VMEM] * 4,
-        [pltpu.VMEM((640, elements), BF), pltpu.VMEM((20, 64, LANES), F32)],
+        [(88, LANES)] * 4
+        + [
+            (slabs, 64, LANES),
+            (groups, LANES),
+            (groups, LANES),
+            ((6, elements), jnp.int32),
+            (15, 16, LANES),
+            (64, LANES),
+        ],
+        [HBM] * 7,
+        [
+            pltpu.VMEM((640, elements), BF),
+            pltpu.VMEM((20, 64, LANES), F32),
+            pltpu.VMEM(idx.shape, jnp.int32),
+            pltpu.VMEM((groups, LANES), jnp.int32),
+            pltpu.VMEM(speeds.shape, F32),
+            pltpu.SemaphoreType.DMA((slabs + 6,)),
+        ],
         "send",
-    )(nodal_state, idx, jac, flags)
+    )(*(in_hbm(x) for x in (nodal_state, idx, jac, flags, face_source, speeds, modes)))
+    sends = outs[:4]
+    slab, jac, flags, face_source, speeds, modes = outs[4:]
     received = [None] * 4
     for b, o in enumerate(OFFSETS):
         pairs = [(i, (i + o) % total) for i in range(total)]
         received[3 - b] = lax.ppermute(sends[b], "curve", pairs)
 
-    base, slab, outside = call(
+    (base,) = call(
         local_kernel,
-        [(5 * groups, 64, LANES), (5 * groups, 64, LANES), (6, 80, elements)],
-        [VMEM, VMEM, VMEM, SMEM, VMEM],
-        [pltpu.VMEM((160, elements), BF), pltpu.VMEM((2 * groups, 8, LANES), F32)],
+        [(slabs, 64, LANES)],
+        [VMEM] * 4,
+        [pltpu.VMEM((64, elements), F32), pltpu.VMEM((2 * groups, 8, LANES), F32)],
         "local",
-    )(nodal_state, jac, face_source, speeds, modes)
-
-    head, tail, width = call(
-        face_kernel,
-        [(5 * groups // 2, 64, LANES), (5 * groups // 2, 64, LANES), (16, LANES)],
-        [VMEM] * 5 + [SMEM] + [VMEM] * 5,
-        [pltpu.VMEM((160, 4 * LANES), BF), pltpu.VMEM((6, 80, elements), F32)],
-        "faces",
-    )(base, slab, outside, face_source, jac, speeds, flags, *received)
-
-    from_lower = lax.ppermute(tail, "curve", [(i, i + 1) for i in range(total - 1)])
-    from_upper = lax.ppermute(head, "curve", [(i + 1, i) for i in range(total - 1)])
-
+    )(slab, jac, speeds, modes)
+
+    (width,) = call(window_kernel, [(16, LANES)], [VMEM] * 6, [], "window")(flags, base, *received)
     own = width
+    (outside,) = call(
+        outside_kernel, [(6, 80, elements)], [VMEM] * 3, [pltpu.VMEM((160, elements), BF)], "outside"
+    )(slab, face_source, width)
+    after = width
     reach = 3
     while reach < half:
+        after = width
         shifts = (reach,) if 2 * reach >= half else (reach, 2 * reach)
         parts = [width]
         for s in shifts:
             pairs = [(i, i + s) for i in range(half - s)]
             pairs += [(i, i - s) for i in range(half + s, total)]
             parts.append(lax.ppermute(width, "curve", pairs))
-        width = call(add_kernel, [(16, LANES)], [VMEM] * len(parts), [], "add")(*parts)[0]
+        (width,) = call(add_kernel, [(16, LANES)], [VMEM] * len(parts), [], "add")(*parts)
         reach *= len(shifts) + 1
 
-    state, new_jac = call(
-        refine_kernel,
-        [(5, 64, E_NEW), (1, E_NEW)],
-        [VMEM] * 10,
+    half_slabs = (slabs // 2, 64, LANES)
+    head, tail = call(
+        face_kernel,
+        [half_slabs, half_slabs],
+        [VMEM] * 11,
+        [pltpu.VMEM((160, 4 * LANES), BF), pltpu.VMEM((6, 80, elements), F32)],
+        "faces",
+    )(base, slab, outside, face_source, jac, speeds, after, *received)
+
+    from_lower = lax.ppermute(tail, "curve", [(i, i + 1) for i in range(total - 1)])
+    from_upper = lax.ppermute(head, "curve", [(i + 1, i) for i in range(total - 1)])
+
+    *kept, new_jac = call(
+        own_kernel,
         [
-            pltpu.VMEM((656, 8 * LANES), BF),
+            (15, 64, LANES),
+            (25, 64, LANES),
+            ((256, 256), BF),
+            ((256, 384), BF),
+            (5 * 48, 8, LANES),
+            (1, E_NEW),
+        ],
+        [VMEM] * 8,
+        [
+            pltpu.VMEM((640, elements), BF),
+            pltpu.VMEM((16, 8 * LANES), BF),
             pltpu.VMEM((5, 64, LANES), F32),
-            pltpu.VMEM((48, 8, LANES), F32),
+            pltpu.VMEM((3 * 48, 8, LANES), F32),
             pltpu.VMEM((2, 8 * LANES, LANES), F32),
         ],
-        "refine",
-    )(from_lower, head, tail, from_upper, width, own, received[1], received[2], jac, flags)
+        "own",
+    )(head, tail, width, own, received[1], received[2], jac, flags)
+    (state,) = call(
+        edge_kernel,
+        [(5, 64, E_NEW)],
+        [VMEM] * 7,
+        [
+            pltpu.VMEM((640, 4 * LANES), BF),
+            pltpu.VMEM((25, 64, LANES), F32),
+            pltpu.VMEM((5, 64, E_NEW), F32),
+            pltpu.SemaphoreType.DMA((5,)),
+        ],
+        "edge",
+        HBM,
+    )(from_lower, from_upper, *kept)
     return state, new_jac.reshape(E_NEW)
 
 

time: 46.4 us -> 39.6 us (0.85)
  the two profiles are of different devices: /device:TPU:0 before, /device:TPU:7 now
where the time goes in v2:
time: 39.6 us; the launch traced here: 39.3 us
  starting transfers between devices  16.9 us (43%)
  Pallas kernels  11.8 us (30%)
  waiting for transfers between devices  9.86 us (25%)
  between operations  0.75 us (2%)
    ppermute x1, starting transfers between devices, shards(): lax.ppermute(tail, 'curve', [(i, i + 1) for i in range(total - 1)])  6.11 us
    ppermute x3, starting transfers between devices, shards(): parts.append(lax.ppermute(width, 'curve', pairs))  5.31 us
    ppermute x1, waiting for transfers between devices, shards(): lax.ppermute(head, 'curve', [(i + 1, i) for i in range(total - 1)])  4.54 us
    ppermute x4, starting transfers between devices, shards(): received[3 - b] = lax.ppermute(sends[b], 'curve', pairs)  3.57 us
    pallas_call x1, Pallas kernels, shards(): call(own_kernel, [(15, 64, LANES), (25, 64, LANES), ((256, 256), BF), ((2...  3.02 us
    ppermute x4, waiting for transfers between devices, shards(): received[3 - b] = lax.ppermute(sends[b], 'curve', pairs)  2.87 us
    ppermute x3, waiting for transfers between devices, shards(): parts.append(lax.ppermute(width, 'curve', pairs))  2.45 us
    pallas_call x1, Pallas kernels, shards(): call(local_kernel, [(slabs, 64, LANES)], [VMEM] * 4, [pltpu.VMEM((64, ele...  2.12 us
  transfers between devices with their start and end apart: 9, of which 3 were waited for; matrix products, arithmetic and copies ran while one was open for 0% of the time, Pallas kernels for 16%

profile of v2, /device:TPU:7, one launch (start us, length us, event | category | flops | bytes accessed | tf_op | source)
XLA Modules:
  0.0 39.3 jit_solution(6961500699508878577)
XLA Ops:
  0.6 2.0 %send.1 = (f32[88,128]{1,0:T(8,128)S(1)}, f32[88,128]{1,0:T(8,128)S(1)}, f32[88,128]{1,0:T(8,128)S(1)}, f32[88,128]{1,0:T(8,128)S(1)}, f32[20,64,128]{2,1,0:T(8,...) custom-call(f32[5,64,512]{2,1,0:T(8,128)} %u_hbm.1, ...), custom_call_target="tpu_custom_call" | custom-call | tf_op jit(solution)/shard_map/send/pallas_call | solution.py:557
  2.6 1.3 %collective-permute-start = (f32[88,128]{1,0:T(8,128)S(1)}, f32[88,128]{1,0:T(8,128)S(1)}, u32[]{:S(2)}, u32[]{:S(2)}) collective-permute-start(f32[88,128]{1,0:T(8,128)S(1)} %get-tuple-element.26), channel_id=1, source_target_pairs={{0,2},{1,3},{2,4},{3,5},{4,6},{5,7},{6,8},{7,9},{8,10},{9,11},{10,... | collective-permute-start | bytes 135176 | tf_op jit(solution)/shard_map/ppermute | solution.py:584
  3.9 2.1 %collective-permute-start.1 = (f32[88,128]{1,0:T(8,128)S(1)}, f32[88,128]{1,0:T(8,128)S(1)}, u32[]{:S(2)}, u32[]{:S(2)}) collective-permute-start(f32[88,128]{1,0:T(8,128)S(1)} %get-tuple-element.27), channel_id=1, source_target_pairs={{0,1},{1,2},{2,3},{3,4},{4,5},{5,6},{6,7},{7,8},{8,9},{9,10},{10,1... | collective-permute-start | bytes 135176 | tf_op jit(solution)/shard_map/ppermute | solution.py:584
  5.9 0.0 collective-permute-start.2
  5.9 0.3 collective-permute-start.3
  6.2 2.1 %local.1.after_ref.base_ref = f32[20,64,128]{2,1,0:T(8,128)S(1)} custom-call(f32[20,64,128]{2,1,0:T(8,128)S(1)} %get-tuple-element.20.slab_ref, f32[4,128]{1,0:T(4,128)S(1)} %get-tuple-element.21.jac_ref, f32[15,16,128]{2,1,0:T(8,128)S(1)} %get-tuple-element.22.sp_ref, f32[64,128]{1,0:T(8,128)S(1)} %get-tuple-element.23.modes_ref), custom_call_target="tpu_custom_call" | custom-call | tf_op jit(solution)/shard_map/local/pallas_call | solution.py:586
  8.3 0.0 collective-permute-done.r0
  8.3 0.0 collective-permute-done.1.r1
  8.4 2.9 %collective-permute-done.2.r2 = f32[88,128]{1,0:T(8,128)S(1)} collective-permute-done((f32[88,128]{1,0:T(8,128)S(1)}, f32[88,128]{1,0:T(8,128)S(1)}, u32[]{:S(2)}, u32[]{:S(2)}) %collective-permute-start.2) | collective-permute-done | bytes 45088 | tf_op jit(solution)/shard_map/ppermute | solution.py:584
  11.2 0.0 collective-permute-done.3.r3
  11.2 0.1 window.1.after_ref.refs_0_.own_ref
  11.3 1.9 %collective-permute-start.5 = (f32[16,128]{1,0:T(8,128)S(1)}, f32[16,128]{1,0:T(8,128)S(1)}, u32[]{:S(2)}, u32[]{:S(2)}) collective-permute-start(f32[16,128]{1,0:T(8,128)S(1)} %window.1.after_ref.refs_0_.own_ref), channel_id=1, source_target_pairs={{0,6},{1,7},{2,8},{3,9},{4,10},{5,11},{6,12},{7,13},{8,14},{9,15},... | collective-permute-start | bytes 24584 | tf_op jit(solution)/shard_map/ppermute | solution.py:608
  13.3 2.7 %collective-permute-start.4 = (f32[16,128]{1,0:T(8,128)S(1)}, f32[16,128]{1,0:T(8,128)S(1)}, u32[]{:S(2)}, u32[]{:S(2)}) collective-permute-start(f32[16,128]{1,0:T(8,128)S(1)} %window.1.after_ref.refs_0_.own_ref), channel_id=1, source_target_pairs={{0,3},{1,4},{2,5},{3,6},{4,7},{5,8},{6,9},{7,10},{8,11},{9,12},{10... | collective-permute-start | bytes 24584 | tf_op jit(solution)/shard_map/ppermute | solution.py:608
  16.0 1.2 %outside.1.out_ref = f32[6,80,512]{2,1,0:T(8,128)S(1)} custom-call(f32[20,64,128]{2,1,0:T(8,128)S(1)} %get-tuple-element.20.slab_ref, s32[6,512]{1,0:T(8,128)S(1)} %get-tuple-element.24.fs_ref, f32[16,128]{1,0:T(8,128)S(1)} %window.1.after_ref.refs_0_.own_ref), custom_call_target="tpu_custom_call" | custom-call | tf_op jit(solution)/shard_map/outside/pallas_call | solution.py:596
  17.2 0.0 collective-permute-done.5.refs_2_
  17.3 2.4 %collective-permute-done.4.refs_1_ = f32[16,128]{1,0:T(8,128)S(1)} collective-permute-done((f32[16,128]{1,0:T(8,128)S(1)}, f32[16,128]{1,0:T(8,128)S(1)}, u32[]{:S(2)}, u32[]{:S(2)}) %collective-permute-start.4) | collective-permute-done | bytes 8224 | tf_op jit(solution)/shard_map/ppermute | solution.py:608
  19.7 1.4 %faces.1 = (f32[10,64,128]{2,1,0:T(8,128)S(1)}, f32[10,64,128]{2,1,0:T(8,128)S(1)}) custom-call(f32[20,64,128]{2,1,0:T(8,128)S(1)} %local.1.after_ref.base_ref, f32[20,64,128]{2,1,0:T(8,128)S(1)} %get-tuple-element.20.slab_ref, f32[6,80,512]{2,1,0:T(8,128)S(1)} %outside.1.out_ref, s32[6,512]{1,0:T(8,128)S(1)} %get-tuple-element.24.fs_ref, ...), custom_call_target="tpu_custom_call" | custom-call | tf_op jit(solution)/shard_map/faces/pallas_call | solution.py:613
  21.1 6.1 %collective-permute-start.6 = (f32[10,64,128]{2,1,0:T(8,128)S(1)}, f32[10,64,128]{2,1,0:T(8,128)S(1)}, u32[]{:S(2)}, u32[]{:S(2)}) collective-permute-start(f32[10,64,128]{2,1,0:T(8,128)S(1)} %get-tuple-element.30.tail_ref), channel_id=1, source_target_pairs={{0,1},{1,2},{2,3},{3,4},{4,5},{5,6},{6,7},{7,8},{8,9},{9,10},{10,1... | collective-permute-start | bytes 983048 | tf_op jit(solution)/shard_map/ppermute | solution.py:621
  27.2 1.9 %collective-permute-start.7 = (f32[10,64,128]{2,1,0:T(8,128)S(1)}, f32[10,64,128]{2,1,0:T(8,128)S(1)}, u32[]{:S(2)}, u32[]{:S(2)}) collective-permute-start(f32[10,64,128]{2,1,0:T(8,128)S(1)} %get-tuple-element.31.head_ref), channel_id=1, source_target_pairs={{1,0},{2,1},{3,2},{4,3},{5,4},{6,5},{7,6},{8,7},{9,8},{10,9},{11,1... | collective-permute-start | bytes 983048 | tf_op jit(solution)/shard_map/ppermute | solution.py:622
  29.1 0.7 %collective-permute-start.8 = (f32[16,128]{1,0:T(8,128)S(1)}, f32[16,128]{1,0:T(8,128)S(1)}, u32[]{:S(2)}, u32[]{:S(2)}) collective-permute-start(f32[16,128]{1,0:T(8,128)S(1)} %add.2.after_ref.refs_0_), channel_id=1, source_target_pairs={{0,9},{1,10},{2,11},{3,12},{4,13},{5,14},{6,15},{25,16},{26,17},{2... | collective-permute-start | bytes 24584 | tf_op jit(solution)/shard_map/ppermute | solution.py:608
  29.8 0.0 collective-permute-done.8.refs_1_
  29.8 3.0 %own.1 = (f32[15,64,128]{2,1,0:T(8,128)S(1)}, f32[25,64,128]{2,1,0:T(8,128)S(1)}, bf16[256,256]{1,0:T(8,128)(2,1)S(1)}, bf16[256,384]{1,0:T(8,128)(2,1)S(1)}, f3...) custom-call(f32[10,64,128]{2,1,0:T(8,128)S(1)} %get-tuple-element.31.head_ref, f32[10,64,128]{2,1,0:T(8,128)S(1)} %get-tuple-element.30.tail_ref, ...), custom_call_target="tpu_custom_call" | custom-call | tf_op jit(solution)/shard_map/own/pallas_call | solution.py:624
  32.9 4.5 %collective-permute-done.7.up_ref = f32[10,64,128]{2,1,0:T(8,128)S(1)} collective-permute-done((f32[10,64,128]{2,1,0:T(8,128)S(1)}, f32[10,64,128]{2,1,0:T(8,128)S(1)}, u32[]{:S(2)}, u32[]{:S(2)}) %collective-permute-start.7) | collective-permute-done | bytes 327712 | tf_op jit(solution)/shard_map/ppermute | solution.py:622
  37.4 1.9 %edge.1 = f32[5,64,960]{2,1,0:T(8,128)} custom-call(f32[10,64,128]{2,1,0:T(8,128)S(1)} %collective-permute-done.6.low_ref, f32[10,64,128]{2,1,0:T(8,128)S(1)} %collective-permute-done.7.up_ref, f32[15,64,128]{2,1,0:T(8,128)S(1)} %get-tuple-element.32.mid_ref, f32[25,64,128]{2,1,0:T(8,128)S(1)} %get-tuple-element.33.part_ref, ...), custom_call_target="tpu_custom_call" | custom-call | tf_op jit(solution)/shard_map/edge/pallas_call | solution.py:644
  (3 shorter events, 0.0 us)
Async XLA Ops:
  2.6 5.7 %collective-permute-start = (f32[88,128]{1,0:T(8,128)S(1)}, f32[88,128]{1,0:T(8,128)S(1)}, u32[]{:S(2)}, u32[]{:S(2)}) collective-permute-start(f32[88,128]{1,0:T(8,128)S(1)} %get-tuple-element.26), channel_id=1, source_target_pairs={{0,2},{1,3},{2,4},{3,5},{4,6},{5,7},{6,8},{7,9},{8,10},{9,11},{10,... | collective-permute-start | bytes 135176 | tf_op jit(solution)/shard_map/ppermute | solution.py:584
  3.9 4.5 %collective-permute-start.1 = (f32[88,128]{1,0:T(8,128)S(1)}, f32[88,128]{1,0:T(8,128)S(1)}, u32[]{:S(2)}, u32[]{:S(2)}) collective-permute-start(f32[88,128]{1,0:T(8,128)S(1)} %get-tuple-element.27), channel_id=1, source_target_pairs={{0,1},{1,2},{2,3},{3,4},{4,5},{5,6},{6,7},{7,8},{8,9},{9,10},{10,1... | collective-permute-start | bytes 135176 | tf_op jit(solution)/shard_map/ppermute | solution.py:584
  5.9 5.3 %collective-permute-start.2 = (f32[88,128]{1,0:T(8,128)S(1)}, f32[88,128]{1,0:T(8,128)S(1)}, u32[]{:S(2)}, u32[]{:S(2)}) collective-permute-start(f32[88,128]{1,0:T(8,128)S(1)} %get-tuple-element.28), channel_id=1, source_target_pairs={{0,31},{1,0},{2,1},{3,2},{4,3},{5,4},{6,5},{7,6},{8,7},{9,8},{10,9... | collective-permute-start | bytes 135176 | tf_op jit(solution)/shard_map/ppermute | solution.py:584
  5.9 5.3 %collective-permute-start.3 = (f32[88,128]{1,0:T(8,128)S(1)}, f32[88,128]{1,0:T(8,128)S(1)}, u32[]{:S(2)}, u32[]{:S(2)}) collective-permute-start(f32[88,128]{1,0:T(8,128)S(1)} %get-tuple-element.29), channel_id=1, source_target_pairs={{0,30},{1,31},{2,0},{3,1},{4,2},{5,3},{6,4},{7,5},{8,6},{9,7},{10,... | collective-permute-start | bytes 135176 | tf_op jit(solution)/shard_map/ppermute | solution.py:584
  11.3 5.9 %collective-permute-start.5 = (f32[16,128]{1,0:T(8,128)S(1)}, f32[16,128]{1,0:T(8,128)S(1)}, u32[]{:S(2)}, u32[]{:S(2)}) collective-permute-start(f32[16,128]{1,0:T(8,128)S(1)} %window.1.after_ref.refs_0_.own_ref), channel_id=1, source_target_pairs={{0,6},{1,7},{2,8},{3,9},{4,10},{5,11},{6,12},{7,13},{8,14},{9,15},... | collective-permute-start | bytes 24584 | tf_op jit(solution)/shard_map/ppermute | solution.py:608
  13.3 6.4 %collective-permute-start.4 = (f32[16,128]{1,0:T(8,128)S(1)}, f32[16,128]{1,0:T(8,128)S(1)}, u32[]{:S(2)}, u32[]{:S(2)}) collective-permute-start(f32[16,128]{1,0:T(8,128)S(1)} %window.1.after_ref.refs_0_.own_ref), channel_id=1, source_target_pairs={{0,3},{1,4},{2,5},{3,6},{4,7},{5,8},{6,9},{7,10},{8,11},{9,12},{10... | collective-permute-start | bytes 24584 | tf_op jit(solution)/shard_map/ppermute | solution.py:608
  21.1 11.8 %collective-permute-start.6 = (f32[10,64,128]{2,1,0:T(8,128)S(1)}, f32[10,64,128]{2,1,0:T(8,128)S(1)}, u32[]{:S(2)}, u32[]{:S(2)}) collective-permute-start(f32[10,64,128]{2,1,0:T(8,128)S(1)} %get-tuple-element.30.tail_ref), channel_id=1, source_target_pairs={{0,1},{1,2},{2,3},{3,4},{4,5},{5,6},{6,7},{7,8},{8,9},{9,10},{10,1... | collective-permute-start | bytes 983048 | tf_op jit(solution)/shard_map/ppermute | solution.py:621
  27.2 10.2 %collective-permute-start.7 = (f32[10,64,128]{2,1,0:T(8,128)S(1)}, f32[10,64,128]{2,1,0:T(8,128)S(1)}, u32[]{:S(2)}, u32[]{:S(2)}) collective-permute-start(f32[10,64,128]{2,1,0:T(8,128)S(1)} %get-tuple-element.31.head_ref), channel_id=1, source_target_pairs={{1,0},{2,1},{3,2},{4,3},{5,4},{6,5},{7,6},{8,7},{9,8},{10,9},{11,1... | collective-permute-start | bytes 983048 | tf_op jit(solution)/shard_map/ppermute | solution.py:622
  29.1 0.7 %collective-permute-start.8 = (f32[16,128]{1,0:T(8,128)S(1)}, f32[16,128]{1,0:T(8,128)S(1)}, u32[]{:S(2)}, u32[]{:S(2)}) collective-permute-start(f32[16,128]{1,0:T(8,128)S(1)} %add.2.after_ref.refs_0_), channel_id=1, source_target_pairs={{0,9},{1,10},{2,11},{3,12},{4,13},{5,14},{6,15},{25,16},{26,17},{2... | collective-permute-start | bytes 24584 | tf_op jit(solution)/shard_map/ppermute | solution.py:608

commit v3 on v2

--- a/solution.py
+++ b/solution.py
@@ -56,6 +56,15 @@
 
 def swap_halves(x):
     return pltpu.roll(x, 4, axis=0)
+
+
+def position():
+    me = lax.axis_index("curve")
+    return me, me % 2 == 0, (me // 2) % 2 == 0
+
+
+def pick(flag, yes, no):
+    return jnp.where(flag, yes, no)
 
 
 def trace_of(ref, t, face):
@@ -75,13 +84,13 @@
     return jnp.concatenate(halves, axis=0)
 
 
-def add_to_face(ref, t, face, value):
+def add_to_face(ref, first, face, value):
     dim, side = face // 2, face % 2
     if dim == 0:
-        where_at = (t, pl.ds(3 * side, 16, stride=4), slice(None))
+        where_at = (pl.ds(first + 3 * side, 16, stride=4), slice(None))
         ref[where_at] = ref[where_at] + value
     elif dim == 2:
-        where_at = (t, slice(48 * side, 48 * side + 16), slice(None))
+        where_at = (slice(first + 48 * side, first + 48 * side + 16), slice(None))
         ref[where_at] = ref[where_at] + value
     else:
         low = low_half()
@@ -90,7 +99,7 @@
             half = value[8 * (k // 2) : 8 * (k // 2) + 8, :]
             if (k % 2) != side:
                 half = swap_halves(half)
-            where_at = (t, slice(16 * k + 8 * side, 16 * k + 8 * side + 8), slice(None))
+            where_at = (slice(first + 16 * k + 8 * side, first + 16 * k + 8 * side + 8), slice(None))
             ref[where_at] = ref[where_at] + jnp.where(keep, half, 0.0)
 
 
@@ -111,7 +120,7 @@
 def send_kernel(u_hbm, idx_hbm, jac_hbm, flag_hbm, fs_hbm, sp_hbm, modes_hbm, *rest):
     outs = rest[:4]
     slab_ref, jac_ref, flag_ref, fs_ref, speed_ref, modes_ref = rest[4:10]
-    lhs, gathered, idx_ref, flag_raw, sp_ref, sems = rest[10:]
+    lhs, gathered, faces, idx_ref, flag_raw, sp_ref, sems = rest[10:]
     elements = u_hbm.shape[2]
     groups = elements // LANES
     loads = [pltpu.make_async_copy(idx_hbm, idx_ref, sems.at[0])]
@@ -164,18 +173,23 @@
     count = elements + 7.0 * jnp.sum(flags)
     rows = lax.broadcasted_iota(jnp.int32, (8, LANES), 0)
     for b in range(4):
-        fb = jnp.broadcast_to(face[0:1, b * LANES : (b + 1) * LANES], (16, LANES))
+        faces[b] = jnp.broadcast_to(face[0:1, b * LANES : (b + 1) * LANES], (16, LANES))
+    me, even, even_chip = position()
+    sent = (pick(even, 2, 1), pick(even, 1, 2), pick(even_chip, 3, 0), pick(even_chip, 0, 3))
+    for q, b in enumerate(sent):
+        fb = faces[b]
         for v in range(5):
             value = trace_of(gathered, b * 5 + v, 0)
             for f in range(1, 6):
                 value = jnp.where(fb == f, trace_of(gathered, b * 5 + v, f), value)
-            outs[b][v * 16 : (v + 1) * 16, :] = value
-        near = 0 if OFFSETS[b] < 0 else groups - 2
+            outs[q][v * 16 : (v + 1) * 16, :] = value
+        last = b >= 2
         meta = jnp.full((8, LANES), count, F32)
         for r in range(2):
-            meta = jnp.where(rows == r, jac_ref[near + r : near + r + 1, :], meta)
-            meta = jnp.where(rows == 2 + r, flags[near + r : near + r + 1, :], meta)
-        outs[b][80:88, :] = meta
+            far = groups - 2 + r
+            meta = jnp.where(rows == r, pick(last, jac_ref[far : far + 1, :], jac_ref[r : r + 1, :]), meta)
+            meta = jnp.where(rows == 2 + r, pick(last, flags[far : far + 1, :], flags[r : r + 1, :]), meta)
+        outs[q][80:88, :] = meta
     for d in range(3):
         for v in range(5):
             speed_ref[d * 5 + v] = jnp.broadcast_to(sp_ref[d : d + 1, v : v + 1], (16, LANES))
@@ -268,8 +282,7 @@
     lax.fori_loop(0, 5 * groups, one, 0)
 
 
-def outside_kernel(slab_ref, fs_ref, after_ref, out_ref, lhs):
-    del after_ref
+def outside_kernel(slab_ref, fs_ref, out_ref, lhs):
     elements = fs_ref.shape[1]
     groups = elements // LANES
     for f in range(6):
@@ -281,39 +294,23 @@
                 lhs[80 + v * 16 : 80 + (v + 1) * 16, g * LANES : (g + 1) * LANES] = low
         picked = dot32(lhs[...], one_hot(fs_ref[f : f + 1, :] - partner * elements, elements))
         near = fs_ref[f : f + 1, :] < 6 * elements
-        out_ref[f] = jnp.where(near, picked[:80] + picked[80:], 0.0)
-
-
-def window_kernel(flag_ref, after_ref, r0, r1, r2, r3, width_ref):
+        value = jnp.where(near, picked[:80] + picked[80:], 0.0)
+        for g in range(groups):
+            out_ref[f * groups + g] = value[:, g * LANES : (g + 1) * LANES]
+
+
+def ghost_kernel(out_ref, fs_ref, after_ref, rd, rb, rc, ra, full_ref, lhs):
     del after_ref
-    me = lax.axis_index("curve")
-    total = lax.axis_size("curve")
-    lower = me < total // 2
-    elements = flag_ref.shape[0] * LANES
-    count = jnp.full((8, LANES), elements + 7.0 * jnp.sum(flag_ref[...]), F32)
-    own = count
-    for o, ref in zip(OFFSETS, (r0, r1, r2, r3)):
-        there = me + o
-        wanted = jnp.logical_and(lower if o < 0 else jnp.logical_not(lower), jnp.logical_and(there >= 0, there < total))
-        value = jnp.broadcast_to(ref[87:88, :], (8, LANES))
-        count = count + value * jnp.where(wanted, 1.0, 0.0)
-    width_ref[0:8] = count
-    width_ref[8:16] = own
-
-
-def face_kernel(base_ref, slab_ref, out_ref, fs_ref, jac_ref, sp_ref, after_ref, r0, r1, r2, r3, *rest):
-    del after_ref
-    head_ref, tail_ref, lhs, outside = rest
     elements = fs_ref.shape[1]
     groups = elements // LANES
     slots = 96
-    for b, ref in enumerate((r0, r1, r2, r3)):
+    me, even, even_chip = position()
+    spots = (pick(even, 2, 1), pick(even, 1, 2), pick(even_chip, 3, 0), pick(even_chip, 0, 3))
+    for spot, ref in zip(spots, (ra, rb, rc, rd)):
         high, low = split_two(ref[0:80, :])
-        lhs[0:80, b * LANES : (b + 1) * LANES] = high
-        lhs[80:160, b * LANES : (b + 1) * LANES] = low
-    half = 5 * (groups // 2)
-    head_ref[...] = base_ref[0:half]
-    tail_ref[...] = base_ref[half : 2 * half]
+        lanes = pl.ds(pl.multiple_of(spot * LANES, LANES), LANES)
+        lhs[0:80, lanes] = high
+        lhs[80:160, lanes] = low
     for f in range(6):
         ghost = fs_ref[f : f + 1, :] - 6 * elements
         place = jnp.zeros_like(ghost)
@@ -321,21 +318,35 @@
             place = place + (ghost >= b * slots).astype(jnp.int32)
         column = ghost + place * (LANES - slots)
         picked = dot32(lhs[...], one_hot(column, 4 * LANES))
-        outside[f] = out_ref[f] + (picked[:80] + picked[80:])
+        picked = picked[:80] + picked[80:]
+        for g in range(groups):
+            full_ref[f * groups + g] = out_ref[f * groups + g] + picked[:, g * LANES : (g + 1) * LANES]
+
+
+def face_kernel(base_ref, slab_ref, full_ref, jac_ref, sp_ref, flag_ref, first_ref, second_ref, counts_ref, scales):
+    groups = jac_ref.shape[0]
+    half = groups // 2
+    me, even, _ = position()
     for g in range(groups):
-        ref, first = (head_ref, 0) if g < groups // 2 else (tail_ref, groups // 2)
-        scale = jnp.broadcast_to(jac_ref[g : g + 1, :] * TIME_STEP, (16, LANES))
-        for v in range(5):
-            t = g * 5 + v
-            for f in range(6):
-                speed = sp_ref[5 * (f // 2) + v]
-                inner = trace_of(slab_ref, t, f)
-                outer = outside[f, v * 16 : (v + 1) * 16, g * LANES : (g + 1) * LANES]
-                central = inner * inner + inner * outer + outer * outer
-                reach = (3.0 * jnp.abs(speed)) * jnp.maximum(jnp.abs(inner), jnp.abs(outer))
-                sign = 1.0 if f % 2 == 0 else -1.0
-                value = (sign * speed) * central - reach * (inner - outer)
-                add_to_face(ref, (g - first) * 5 + v, f, scale * value)
+        scales[g] = jnp.broadcast_to(jac_ref[g : g + 1, :] * TIME_STEP, (16, LANES))
+    for ref, start in ((first_ref, pick(even, half, 0)), (second_ref, pick(even, 0, half))):
+        for i in range(half):
+            g = start + i
+            scale = scales[g]
+            for v in range(5):
+                t = g * 5 + v
+                row = (i * 5 + v) * 64
+                ref[row : row + 64, :] = base_ref[t]
+                for f in range(6):
+                    speed = sp_ref[5 * (f // 2) + v]
+                    inner = trace_of(slab_ref, t, f)
+                    outer = full_ref[f * groups + g, v * 16 : (v + 1) * 16, :]
+                    central = inner * inner + inner * outer + outer * outer
+                    reach = (3.0 * jnp.abs(speed)) * jnp.maximum(jnp.abs(inner), jnp.abs(outer))
+                    sign = 1.0 if f % 2 == 0 else -1.0
+                    value = (sign * speed) * central - reach * (inner - outer)
+                    add_to_face(ref, row, f, scale * value)
+    counts_ref[...] = jnp.full(counts_ref.shape, groups * LANES + 7.0 * jnp.sum(flag_ref[...]), F32)
 
 
 EDGE_GROUPS = (0, 1, 5, 6, 7)
@@ -375,19 +386,20 @@
             store(16 * (k + 1) + 8 * q, jnp.where(low, swap_halves(one_row), two_row))
 
 
-def own_kernel(head_ref, tail_ref, w_ref, own_ref, r1, r2, jac_ref, flag_ref, *rest):
+def own_kernel(first_ref, second_ref, counts_ref, ra, rb, jac_ref, flag_ref, *rest):
     mid_ref, part_ref, low_hot, up_hot, coef_out, jout_ref = rest[:6]
     lhs, meta, res, coef_mid, cols = rest[6:]
-    total = lax.axis_size("curve")
-    me = lax.axis_index("curve")
-    for b, ref in enumerate((head_ref, tail_ref)):
+    me, even, _ = position()
+    for ref, start in ((first_ref, pick(even, 2, 0)), (second_ref, pick(even, 0, 2))):
         for g in range(2):
-            high, low = split_two(ref[5 * g : 5 * g + 5].reshape(320, LANES))
-            at = slice((2 * b + g) * LANES, (2 * b + g + 1) * LANES)
+            high, low = split_two(ref[320 * g : 320 * g + 320, :])
+            at = pl.ds(pl.multiple_of((start + g) * LANES, LANES), LANES)
             lhs[0:320, at] = high
             lhs[320:640, at] = low
-    jac = jnp.concatenate([r1[80:82, :], jac_ref[...], r2[80:82, :]], axis=0)
-    flag = jnp.concatenate([r1[82:84, :], flag_ref[...], r2[82:84, :]], axis=0)
+    near_a, near_b = ra[80:88, :], rb[80:88, :]
+    below, above = pick(even, near_b, near_a), pick(even, near_a, near_b)
+    jac = jnp.concatenate([below[0:2], jac_ref[...], above[0:2]], axis=0)
+    flag = jnp.concatenate([below[2:4], flag_ref[...], above[2:4]], axis=0)
     sizes = 1.0 + 7.0 * flag
     lane0 = lax.broadcasted_iota(jnp.int32, (LANES, LANES), 0)
     lane1 = lax.broadcasted_iota(jnp.int32, (LANES, LANES), 1)
@@ -402,10 +414,13 @@
     row0 = lax.broadcasted_iota(jnp.int32, (8, LANES), 0)
     for r in range(8):
         before = before + jnp.where(row0 == r, starts[r], 0.0)
-    width = w_ref[0:8]
-    mine = own_ref[8:16]
-    lower = jnp.where(me < total // 2, 1.0, 0.0)
-    begin = lower * (width - mine) + (1.0 - lower) * (float(total * E_NEW) - width)
+    counts = counts_ref[...]
+    half = counts.shape[0]
+    upper = me >= half
+    earlier = lax.broadcasted_iota(jnp.int32, counts.shape, 0) < me % half
+    begin = jnp.sum(jnp.where(earlier, counts, 0.0), axis=0, keepdims=True)
+    rest = float(2 * half * E_NEW) - jnp.sum(counts, axis=0, keepdims=True)
+    begin = begin + pick(upper, rest, jnp.zeros_like(rest))
     begin = begin - (me * E_NEW).astype(F32)
     place = before + (begin - starts[2])
     ends = place + sizes
@@ -481,11 +496,12 @@
                 lax.fori_loop(0, 5, one, 0)
 
 
-def edge_kernel(low_ref, up_ref, mid_ref, part_ref, low_hot, up_hot, coef_ref, out_hbm, lhs, res, out, sems):
-    for b, ref in enumerate((low_ref, up_ref)):
+def edge_kernel(b_ref, a_ref, mid_ref, part_ref, low_hot, up_hot, coef_ref, out_hbm, lhs, res, out, sems):
+    _, even, _ = position()
+    for ref, start in ((a_ref, pick(even, 2, 0)), (b_ref, pick(even, 0, 2))):
         for g in range(2):
-            high, low = split_two(ref[5 * g : 5 * g + 5].reshape(320, LANES))
-            at = slice((2 * b + g) * LANES, (2 * b + g + 1) * LANES)
+            high, low = split_two(ref[320 * g : 320 * g + 320, :])
+            at = pl.ds(pl.multiple_of((start + g) * LANES, LANES), LANES)
             lhs[0:320, at] = high
             lhs[320:640, at] = low
     picked = (dot32(lhs[:, 0:256], low_hot[...]), dot32(lhs[:, 256:512], up_hot[...]))
@@ -509,15 +525,12 @@
         pltpu.make_async_copy(out.at[v], out_hbm.at[v], sems.at[v]).wait()
 
 
-def add_kernel(*refs):
-    total = refs[0][...]
-    for ref in refs[1:-1]:
-        total = total + ref[...]
-    refs[-1][...] = total
-
-
 VMEM = pl.BlockSpec(memory_space=pltpu.MemorySpace.VMEM)
 HBM = pl.BlockSpec(memory_space=pltpu.MemorySpace.HBM)
+
+
+def swap(x, pairs):
+    return lax.ppermute(x, "curve", list(pairs) + [(b, a) for a, b in pairs])
 
 
 def in_hbm(x):
@@ -569,6 +582,7 @@
         [
             pltpu.VMEM((640, elements), BF),
             pltpu.VMEM((20, 64, LANES), F32),
+            pltpu.VMEM((4, 16, LANES), jnp.int32),
             pltpu.VMEM(idx.shape, jnp.int32),
             pltpu.VMEM((groups, LANES), jnp.int32),
             pltpu.VMEM(speeds.shape, F32),
@@ -578,10 +592,11 @@
     )(*(in_hbm(x) for x in (nodal_state, idx, jac, flags, face_source, speeds, modes)))
     sends = outs[:4]
     slab, jac, flags, face_source, speeds, modes = outs[4:]
-    received = [None] * 4
-    for b, o in enumerate(OFFSETS):
-        pairs = [(i, (i + o) % total) for i in range(total)]
-        received[3 - b] = lax.ppermute(sends[b], "curve", pairs)
+    pair_a = [(i, i + 1) for i in range(0, total, 2)]
+    pair_b = [(i, (i + 1) % total) for i in range(1, total, 2)]
+    pair_c = [(i, i + 2) for i in range(total) if (i // 2) % 2 == 0]
+    pair_d = [(i, (i + 2) % total) for i in range(total) if (i // 2) % 2 == 1]
+    received = [swap(x, pairs) for x, pairs in zip(sends, (pair_a, pair_b, pair_c, pair_d))]
 
     (base,) = call(
         local_kernel,
@@ -591,35 +606,26 @@
         "local",
     )(slab, jac, speeds, modes)
 
-    (width,) = call(window_kernel, [(16, LANES)], [VMEM] * 6, [], "window")(flags, base, *received)
-    own = width
     (outside,) = call(
-        outside_kernel, [(6, 80, elements)], [VMEM] * 3, [pltpu.VMEM((160, elements), BF)], "outside"
-    )(slab, face_source, width)
-    after = width
-    reach = 3
-    while reach < half:
-        after = width
-        shifts = (reach,) if 2 * reach >= half else (reach, 2 * reach)
-        parts = [width]
-        for s in shifts:
-            pairs = [(i, i + s) for i in range(half - s)]
-            pairs += [(i, i - s) for i in range(half + s, total)]
-            parts.append(lax.ppermute(width, "curve", pairs))
-        (width,) = call(add_kernel, [(16, LANES)], [VMEM] * len(parts), [], "add")(*parts)
-        reach *= len(shifts) + 1
-
-    half_slabs = (slabs // 2, 64, LANES)
-    head, tail = call(
+        outside_kernel, [(6 * groups, 80, LANES)], [VMEM] * 2, [pltpu.VMEM((160, elements), BF)], "outside"
+    )(slab, face_source)
+    (full,) = call(
+        ghost_kernel, [(6 * groups, 80, LANES)], [VMEM] * 7, [pltpu.VMEM((160, 4 * LANES), BF)], "ghost"
+    )(outside, face_source, base, *(received[q] for q in (3, 1, 2, 0)))
+    rows = slabs // 2 * 64
+    first, second, counts = call(
         face_kernel,
-        [half_slabs, half_slabs],
-        [VMEM] * 11,
-        [pltpu.VMEM((160, 4 * LANES), BF), pltpu.VMEM((6, 80, elements), F32)],
+        [(rows, LANES), (rows, LANES), (half, LANES)],
+        [VMEM] * 6,
+        [pltpu.VMEM((groups, 16, LANES), F32)],
         "faces",
-    )(base, slab, outside, face_source, jac, speeds, after, *received)
-
-    from_lower = lax.ppermute(tail, "curve", [(i, i + 1) for i in range(total - 1)])
-    from_upper = lax.ppermute(head, "curve", [(i + 1, i) for i in range(total - 1)])
+    )(base, slab, full, jac, speeds, flags)
+
+    from_a = swap(first, pair_a)
+    from_b = swap(second, pair_b[:-1])
+
+    halves = [list(range(half)), list(range(half, total))]
+    counts = lax.all_to_all(counts, "curve", 0, 0, axis_index_groups=halves, tiled=True)
 
     *kept, new_jac = call(
         own_kernel,
@@ -631,7 +637,7 @@
             (5 * 48, 8, LANES),
             (1, E_NEW),
         ],
-        [VMEM] * 8,
+        [VMEM] * 7,
         [
             pltpu.VMEM((640, elements), BF),
             pltpu.VMEM((16, 8 * LANES), BF),
@@ -640,7 +646,7 @@
             pltpu.VMEM((2, 8 * LANES, LANES), F32),
         ],
         "own",
-    )(head, tail, width, own, received[1], received[2], jac, flags)
+    )(first, second, counts, received[0], received[1], jac, flags)
     (state,) = call(
         edge_kernel,
         [(5, 64, E_NEW)],
@@ -653,7 +659,7 @@
         ],
         "edge",
         HBM,
-    )(from_lower, from_upper, *kept)
+    )(from_b, from_a, *kept)
     return state, new_jac.reshape(E_NEW)
 
 

time: 39.6 us -> 32.5 us (0.82)
  the two profiles are of different devices: /device:TPU:7 before, /device:TPU:0 now
where the time goes in v3:
time: 32.5 us; the launch traced here: 32.1 us
  Pallas kernels  11.8 us (36%)
  starting transfers between devices  8.97 us (28%)
  blocking collectives  8.18 us (25%)
  waiting for transfers between devices  2.51 us (8%)
  between operations  0.69 us (2%)
    ppermute x6, starting transfers between devices, swap(): return lax.ppermute(x, 'curve', list(pairs) + [(b, a) for a, b in pairs])  8.97 us
    all_to_all x1, blocking collectives, shards(): lax.all_to_all(counts, 'curve', 0, 0, axis_index_groups=halves, tiled=True)  8.18 us
    pallas_call x1, Pallas kernels, shards(): call(own_kernel, [(15, 64, LANES), (25, 64, LANES), ((256, 256), BF), ((2...  3.15 us
    ppermute x6, waiting for transfers between devices, swap(): return lax.ppermute(x, 'curve', list(pairs) + [(b, a) for a, b in pairs])  2.51 us
    pallas_call x1, Pallas kernels, shards(): call(local_kernel, [(slabs, 64, LANES)], [VMEM] * 4, [pltpu.VMEM((64, ele...  2.12 us
    pallas_call x1, Pallas kernels, shards(): call(edge_kernel, [(5, 64, E_NEW)], [VMEM] * 7, [pltpu.VMEM((640, 4 * LAN...  1.94 us
    pallas_call x1, Pallas kernels, shards(): call(send_kernel, [(88, LANES)] * 4 + [(slabs, 64, LANES), (groups, LANES...  1.94 us
    pallas_call x1, Pallas kernels, shards(): call(outside_kernel, [(6 * groups, 80, LANES)], [VMEM] * 2, [pltpu.VMEM((...  1.23 us
  transfers between devices with their start and end apart: 6, of which 1 were waited for; matrix products, arithmetic and copies ran while one was open for 0% of the time, Pallas kernels for 20%

profile of v3, /device:TPU:0, one launch (start us, length us, event | category | flops | bytes accessed | tf_op | source)
XLA Modules:
  0.0 32.1 jit_solution(11450125785906004557)
XLA Ops:
  0.6 1.9 %send.1 = (f32[88,128]{1,0:T(8,128)S(1)}, f32[88,128]{1,0:T(8,128)S(1)}, f32[88,128]{1,0:T(8,128)S(1)}, f32[88,128]{1,0:T(8,128)S(1)}, f32[20,64,128]{2,1,0:T(8,...) custom-call(f32[5,64,512]{2,1,0:T(8,128)} %u_hbm.1, ...), custom_call_target="tpu_custom_call" | custom-call | tf_op jit(solution)/shard_map/send/pallas_call | solution.py:570
  2.6 7.0 %collective-permute-start = (f32[88,128]{1,0:T(8,128)S(1)}, f32[88,128]{1,0:T(8,128)S(1)}, u32[]{:S(2)}, u32[]{:S(2)}) collective-permute-start(f32[88,128]{1,0:T(8,128)S(1)} %get-tuple-element.26), channel_id=1, source_target_pairs={{2,4},{3,5},{6,8},{7,9},{10,12},{11,13},{14,16},{15,17},{18,20},{1... | collective-permute-start | bytes 135176 | tf_op jit(solution)/shard_map/ppermute | solution.py:533
  9.6 0.0 collective-permute-start.1
  9.6 1.2 %collective-permute-start.2 = (f32[88,128]{1,0:T(8,128)S(1)}, f32[88,128]{1,0:T(8,128)S(1)}, u32[]{:S(2)}, u32[]{:S(2)}) collective-permute-start(f32[88,128]{1,0:T(8,128)S(1)} %get-tuple-element.28), channel_id=1, source_target_pairs={{0,2},{1,3},{4,6},{5,7},{8,10},{9,11},{12,14},{13,15},{16,18},{17,... | collective-permute-start | bytes 135176 | tf_op jit(solution)/shard_map/ppermute | solution.py:533
  10.8 0.0 collective-permute-start.3
  10.8 1.2 %outside.1.out_ref = f32[24,80,128]{2,1,0:T(8,128)S(1)} custom-call(f32[20,64,128]{2,1,0:T(8,128)S(1)} %get-tuple-element.21.slab_ref, s32[6,512]{1,0:T(8,128)S(1)} %get-tuple-element.25.fs_ref), custom_call_target="tpu_custom_call" | custom-call | tf_op jit(solution)/shard_map/outside/pallas_call | solution.py:609
  12.0 2.1 %local.1.after_ref.base_ref = f32[20,64,128]{2,1,0:T(8,128)S(1)} custom-call(f32[20,64,128]{2,1,0:T(8,128)S(1)} %get-tuple-element.21.slab_ref, f32[4,128]{1,0:T(4,128)S(1)} %get-tuple-element.22.jac_ref, f32[15,16,128]{2,1,0:T(8,128)S(1)} %get-tuple-element.23.sp_ref, f32[64,128]{1,0:T(8,128)S(1)} %get-tuple-element.24.modes_ref), custom_call_target="tpu_custom_call" | custom-call | tf_op jit(solution)/shard_map/local/pallas_call | solution.py:601
  14.2 0.0 collective-permute-done.rd
  14.2 2.5 %collective-permute-done.1.rb = f32[88,128]{1,0:T(8,128)S(1)} collective-permute-done((f32[88,128]{1,0:T(8,128)S(1)}, f32[88,128]{1,0:T(8,128)S(1)}, u32[]{:S(2)}, u32[]{:S(2)}) %collective-permute-start.1) | collective-permute-done | bytes 45088 | tf_op jit(solution)/shard_map/ppermute | solution.py:533
  16.7 0.0 collective-permute-done.2.rc
  16.7 0.0 collective-permute-done.3.ra
  16.7 0.8 %ghost.1.full_ref = f32[24,80,128]{2,1,0:T(8,128)S(1)} custom-call(f32[24,80,128]{2,1,0:T(8,128)S(1)} %outside.1.out_ref, s32[6,512]{1,0:T(8,128)S(1)} %get-tuple-element.25.fs_ref, f32[20,64,128]{2,1,0:T(8,128)S(1)} %local.1.after_ref.base_ref, f32[88,128]{1,0:T(8,128)S(1)} %collective-permute-done.rd, f32[88,128]{1,0:T(8,128)S(1)} %collective-permute-done.1.rb, ...), custom_call_target="tpu_custom_call" | custom-call | tf_op jit(solution)/shard_map/ghost/pallas_call | solution.py:612
  17.5 0.6 %faces.1 = (f32[640,128]{1,0:T(8,128)S(1)}, f32[640,128]{1,0:T(8,128)S(1)}, f32[16,128]{1,0:T(8,128)S(1)}) custom-call(f32[20,64,128]{2,1,0:T(8,128)S(1)} %local.1.after_ref.base_ref, f32[20,64,128]{2,1,0:T(8,128)S(1)} %get-tuple-element.21.slab_ref, f32[24,80,128]{2,1,0:T(8,128)S(1)} %ghost.1.full_ref, f32[4,128]{1,0:T(4,128)S(1)} %get-tuple-element.22.jac_ref, ...), custom_call_target="tpu_custom_call" | custom-call | tf_op jit(solution)/shard_map/faces/pallas_call | solution.py:616
  18.1 0.7 %collective-permute-start.4 = (f32[640,128]{1,0:T(8,128)S(1)}, f32[640,128]{1,0:T(8,128)S(1)}, u32[]{:S(2)}, u32[]{:S(2)}) collective-permute-start(f32[640,128]{1,0:T(8,128)S(1)} %get-tuple-element.31.second_ref), channel_id=1, source_target_pairs={{1,2},{3,4},{5,6},{7,8},{9,10},{11,12},{13,14},{15,16},{17,18},{19... | collective-permute-start | bytes 983048 | tf_op jit(solution)/shard_map/ppermute | solution.py:533
  18.8 0.1 collective-permute-start.5
  18.8 8.2 %all_to_all.11 = f32[16,1,128]{2,1,0:T(1,128)S(1)} all-to-all(f32[16,1,128]{2,1,0:T(1,128)S(1)} %bitcast.9), channel_id=1, replica_groups={{0,1,2,3,4,5,6,7,8,9,10,11,12,13,14,15},{16,17,18,19,20,21,22,23,24,25,..., dimensions={0} | all-to-all | bytes 16384 | tf_op jit(solution)/shard_map/all_to_all | solution.py:628
  27.0 3.2 %own.1 = (f32[15,64,128]{2,1,0:T(8,128)S(1)}, f32[25,64,128]{2,1,0:T(8,128)S(1)}, bf16[256,256]{1,0:T(8,128)(2,1)S(1)}, bf16[256,384]{1,0:T(8,128)(2,1)S(1)}, f3...) custom-call(f32[640,128]{1,0:T(8,128)S(1)} %get-tuple-element.32.first_ref, f32[640,128]{1,0:T(8,128)S(1)} %get-tuple-element.31.second_ref, ...), custom_call_target="tpu_custom_call" | custom-call | tf_op jit(solution)/shard_map/own/pallas_call | solution.py:630
  30.2 0.0 collective-permute-done.4.b_ref
  30.2 0.0 collective-permute-done.5.a_ref
  30.2 1.9 %edge.1 = f32[5,64,960]{2,1,0:T(8,128)} custom-call(f32[640,128]{1,0:T(8,128)S(1)} %collective-permute-done.4.b_ref, f32[640,128]{1,0:T(8,128)S(1)} %collective-permute-done.5.a_ref, f32[15,64,128]{2,1,0:T(8,128)S(1)} %get-tuple-element.34.mid_ref, f32[25,64,128]{2,1,0:T(8,128)S(1)} %get-tuple-element.35.part_ref, ...), custom_call_target="tpu_custom_call" | custom-call | tf_op jit(solution)/shard_map/edge/pallas_call | solution.py:650
Async XLA Ops:
  2.6 11.6 %collective-permute-start = (f32[88,128]{1,0:T(8,128)S(1)}, f32[88,128]{1,0:T(8,128)S(1)}, u32[]{:S(2)}, u32[]{:S(2)}) collective-permute-start(f32[88,128]{1,0:T(8,128)S(1)} %get-tuple-element.26), channel_id=1, source_target_pairs={{2,4},{3,5},{6,8},{7,9},{10,12},{11,13},{14,16},{15,17},{18,20},{1... | collective-permute-start | bytes 135176 | tf_op jit(solution)/shard_map/ppermute | solution.py:533
  9.6 7.1 %collective-permute-start.1 = (f32[88,128]{1,0:T(8,128)S(1)}, f32[88,128]{1,0:T(8,128)S(1)}, u32[]{:S(2)}, u32[]{:S(2)}) collective-permute-start(f32[88,128]{1,0:T(8,128)S(1)} %get-tuple-element.27), channel_id=1, source_target_pairs={{1,2},{3,4},{5,6},{7,8},{9,10},{11,12},{13,14},{15,16},{17,18},{19... | collective-permute-start | bytes 135176 | tf_op jit(solution)/shard_map/ppermute | solution.py:533
  9.6 7.1 %collective-permute-start.2 = (f32[88,128]{1,0:T(8,128)S(1)}, f32[88,128]{1,0:T(8,128)S(1)}, u32[]{:S(2)}, u32[]{:S(2)}) collective-permute-start(f32[88,128]{1,0:T(8,128)S(1)} %get-tuple-element.28), channel_id=1, source_target_pairs={{0,2},{1,3},{4,6},{5,7},{8,10},{9,11},{12,14},{13,15},{16,18},{17,... | collective-permute-start | bytes 135176 | tf_op jit(solution)/shard_map/ppermute | solution.py:533
  10.8 5.9 %collective-permute-start.3 = (f32[88,128]{1,0:T(8,128)S(1)}, f32[88,128]{1,0:T(8,128)S(1)}, u32[]{:S(2)}, u32[]{:S(2)}) collective-permute-start(f32[88,128]{1,0:T(8,128)S(1)} %get-tuple-element.29), channel_id=1, source_target_pairs={{0,1},{2,3},{4,5},{6,7},{8,9},{10,11},{12,13},{14,15},{16,17},{18,... | collective-permute-start | bytes 135176 | tf_op jit(solution)/shard_map/ppermute | solution.py:533
  18.1 12.1 %collective-permute-start.4 = (f32[640,128]{1,0:T(8,128)S(1)}, f32[640,128]{1,0:T(8,128)S(1)}, u32[]{:S(2)}, u32[]{:S(2)}) collective-permute-start(f32[640,128]{1,0:T(8,128)S(1)} %get-tuple-element.31.second_ref), channel_id=1, source_target_pairs={{1,2},{3,4},{5,6},{7,8},{9,10},{11,12},{13,14},{15,16},{17,18},{19... | collective-permute-start | bytes 983048 | tf_op jit(solution)/shard_map/ppermute | solution.py:533
  18.8 11.4 %collective-permute-start.5 = (f32[640,128]{1,0:T(8,128)S(1)}, f32[640,128]{1,0:T(8,128)S(1)}, u32[]{:S(2)}, u32[]{:S(2)}) collective-permute-start(f32[640,128]{1,0:T(8,128)S(1)} %get-tuple-element.32.first_ref), channel_id=1, source_target_pairs={{0,1},{2,3},{4,5},{6,7},{8,9},{10,11},{12,13},{14,15},{16,17},{18,... | collective-permute-start | bytes 983048 | tf_op jit(solution)/shard_map/ppermute | solution.py:533

commit v4 on v3

--- a/solution.py
+++ b/solution.py
@@ -108,9 +108,18 @@
     return high, (x - high.astype(F32)).astype(BF)
 
 
-def one_hot(row, count):
-    ids = lax.broadcasted_iota(jnp.int32, (count, row.shape[1]), 0)
-    return jnp.where(ids == row, 1.0, 0.0).astype(BF)
+def one_hot(row, count, used=None, block=1):
+    lanes = row.shape[1]
+    packed = jnp.broadcast_to(row, (16, lanes)).astype(jnp.int16)
+    ids = lax.broadcasted_iota(jnp.int32, (16, lanes), 0).astype(jnp.int16)
+    one, zero = jnp.ones((16, lanes), BF), jnp.zeros((16, lanes), BF)
+    pieces = []
+    for first in range(0, count, 16):
+        if used is not None and first % block >= used:
+            pieces.append(zero)
+        else:
+            pieces.append(jnp.where(packed == ids + jnp.int16(first), one, zero))
+    return jnp.concatenate(pieces, axis=0)
 
 
 def dot32(a, b):
@@ -229,8 +238,9 @@
     return out
 
 
-def local_kernel(slab_ref, jac_ref, sp_ref, modes_ref, base_ref, first, rows_s):
+def local_kernel(slab_ref, jac_ref, sp_ref, modes_ref, fs_ref, base_ref, out_ref, first, rows_s, lhs):
     groups = jac_ref.shape[0]
+    outside_traces(slab_ref, fs_ref, out_ref, lhs)
     for g in range(groups):
         first[:, g * LANES : (g + 1) * LANES] = slab_ref[g * 5]
     modal = jnp.dot(
@@ -282,7 +292,7 @@
     lax.fori_loop(0, 5 * groups, one, 0)
 
 
-def outside_kernel(slab_ref, fs_ref, out_ref, lhs):
+def outside_traces(slab_ref, fs_ref, out_ref, lhs):
     elements = fs_ref.shape[1]
     groups = elements // LANES
     for f in range(6):
@@ -299,8 +309,7 @@
             out_ref[f * groups + g] = value[:, g * LANES : (g + 1) * LANES]
 
 
-def ghost_kernel(out_ref, fs_ref, after_ref, rd, rb, rc, ra, full_ref, lhs):
-    del after_ref
+def add_ghosts(out_ref, fs_ref, rd, rb, rc, ra, full_ref, lhs):
     elements = fs_ref.shape[1]
     groups = elements // LANES
     slots = 96
@@ -317,13 +326,56 @@
         for b in range(1, 4):
             place = place + (ghost >= b * slots).astype(jnp.int32)
         column = ghost + place * (LANES - slots)
-        picked = dot32(lhs[...], one_hot(column, 4 * LANES))
+        picked = dot32(lhs[...], one_hot(column, 4 * LANES, slots, LANES))
         picked = picked[:80] + picked[80:]
         for g in range(groups):
             full_ref[f * groups + g] = out_ref[f * groups + g] + picked[:, g * LANES : (g + 1) * LANES]
 
 
-def face_kernel(base_ref, slab_ref, full_ref, jac_ref, sp_ref, flag_ref, first_ref, second_ref, counts_ref, scales):
+def refine_tables(ra, rb, jac_ref, flag_ref, meta_ref, cols_ref):
+    _, even, _ = position()
+    near_a, near_b = ra[80:88, :], rb[80:88, :]
+    below, above = pick(even, near_b, near_a), pick(even, near_a, near_b)
+    jac = jnp.concatenate([below[0:2], jac_ref[...], above[0:2]], axis=0)
+    flag = jnp.concatenate([below[2:4], flag_ref[...], above[2:4]], axis=0)
+    sizes = 1.0 + 7.0 * flag
+    lane0 = lax.broadcasted_iota(jnp.int32, (LANES, LANES), 0)
+    lane1 = lax.broadcasted_iota(jnp.int32, (LANES, LANES), 1)
+    upper = jnp.where(lane0 < lane1, 1.0, 0.0).astype(BF)
+    before = dot32(sizes.astype(BF), upper)
+    row_total = jnp.sum(sizes, axis=1, keepdims=True)
+    running = jnp.zeros((1, 1), F32)
+    starts = []
+    for r in range(8):
+        starts.append(running)
+        running = running + row_total[r : r + 1]
+    row0 = lax.broadcasted_iota(jnp.int32, (8, LANES), 0)
+    for r in range(8):
+        before = before + jnp.where(row0 == r, starts[r], 0.0)
+    place = before - starts[2]
+    ends = place + sizes
+    place_hi = jnp.floor(place * (1.0 / 256.0))
+    place_lo = place - 256.0 * place_hi
+    jac_a = jac.astype(BF)
+    jac_b = (jac - jac_a.astype(F32)).astype(BF)
+    jac_c = (jac - jac_a.astype(F32) - jac_b.astype(F32)).astype(BF)
+    rows16 = lax.broadcasted_iota(jnp.int32, (16, LANES), 0)
+    extras = [jac_a.astype(F32), jac_b.astype(F32), jac_c.astype(F32), flag, place_hi, place_lo]
+    for r in range(8):
+        block = jnp.zeros((16, LANES), F32)
+        for q, item in enumerate(extras):
+            block = jnp.where(rows16 == q, jnp.broadcast_to(item[r : r + 1, :], (16, LANES)), block)
+        at = slice(r * LANES, (r + 1) * LANES)
+        meta_ref[:, at] = block.astype(BF)
+        for q, item in enumerate((place, ends)):
+            column = jnp.transpose(jnp.broadcast_to(item[r : r + 1, :], (LANES, LANES)))
+            cols_ref[q, at, :] = column.astype(jnp.int32).astype(jnp.int16)
+
+
+def face_kernel(base_ref, slab_ref, out_ref, fs_ref, jac_ref, sp_ref, flag_ref, rd, rb, rc, ra, *rest):
+    first_ref, second_ref, counts_ref, meta_ref, cols_ref, scales, full_ref, lhs = rest
+    refine_tables(ra, rb, jac_ref, flag_ref, meta_ref, cols_ref)
+    add_ghosts(out_ref, fs_ref, rd, rb, rc, ra, full_ref, lhs)
     groups = jac_ref.shape[0]
     half = groups // 2
     me, even, _ = position()
@@ -386,9 +438,9 @@
             store(16 * (k + 1) + 8 * q, jnp.where(low, swap_halves(one_row), two_row))
 
 
-def own_kernel(first_ref, second_ref, counts_ref, ra, rb, jac_ref, flag_ref, *rest):
+def own_kernel(first_ref, second_ref, counts_ref, meta, cols, *rest):
     mid_ref, part_ref, low_hot, up_hot, coef_out, jout_ref = rest[:6]
-    lhs, meta, res, coef_mid, cols = rest[6:]
+    lhs, res, coef_mid = rest[6:]
     me, even, _ = position()
     for ref, start in ((first_ref, pick(even, 2, 0)), (second_ref, pick(even, 0, 2))):
         for g in range(2):
@@ -396,24 +448,6 @@
             at = pl.ds(pl.multiple_of((start + g) * LANES, LANES), LANES)
             lhs[0:320, at] = high
             lhs[320:640, at] = low
-    near_a, near_b = ra[80:88, :], rb[80:88, :]
-    below, above = pick(even, near_b, near_a), pick(even, near_a, near_b)
-    jac = jnp.concatenate([below[0:2], jac_ref[...], above[0:2]], axis=0)
-    flag = jnp.concatenate([below[2:4], flag_ref[...], above[2:4]], axis=0)
-    sizes = 1.0 + 7.0 * flag
-    lane0 = lax.broadcasted_iota(jnp.int32, (LANES, LANES), 0)
-    lane1 = lax.broadcasted_iota(jnp.int32, (LANES, LANES), 1)
-    upper = jnp.where(lane0 < lane1, 1.0, 0.0).astype(BF)
-    before = dot32(sizes.astype(BF), upper)
-    row_total = jnp.sum(sizes, axis=1, keepdims=True)
-    running = jnp.zeros((1, 1), F32)
-    starts = []
-    for r in range(8):
-        starts.append(running)
-        running = running + row_total[r : r + 1]
-    row0 = lax.broadcasted_iota(jnp.int32, (8, LANES), 0)
-    for r in range(8):
-        before = before + jnp.where(row0 == r, starts[r], 0.0)
     counts = counts_ref[...]
     half = counts.shape[0]
     upper = me >= half
@@ -422,31 +456,20 @@
     rest = float(2 * half * E_NEW) - jnp.sum(counts, axis=0, keepdims=True)
     begin = begin + pick(upper, rest, jnp.zeros_like(rest))
     begin = begin - (me * E_NEW).astype(F32)
-    place = before + (begin - starts[2])
-    ends = place + sizes
-    place_hi = jnp.floor(place * (1.0 / 256.0))
-    place_lo = place - 256.0 * place_hi
-    jac_a = jac.astype(BF)
-    jac_b = (jac - jac_a.astype(F32)).astype(BF)
-    jac_c = (jac - jac_a.astype(F32) - jac_b.astype(F32)).astype(BF)
-    rows16 = lax.broadcasted_iota(jnp.int32, (16, LANES), 0)
-    extras = [jac_a.astype(F32), jac_b.astype(F32), jac_c.astype(F32), flag, place_hi, place_lo]
-    for r in range(8):
-        block = jnp.zeros((16, LANES), F32)
-        for q, item in enumerate(extras):
-            block = jnp.where(rows16 == q, jnp.broadcast_to(item[r : r + 1, :], (16, LANES)), block)
-        at = slice(r * LANES, (r + 1) * LANES)
-        meta[:, at] = block.astype(BF)
-        cols[0, at, :] = jnp.transpose(jnp.broadcast_to(place[r : r + 1, :], (LANES, LANES)))
-        cols[1, at, :] = jnp.transpose(jnp.broadcast_to(ends[r : r + 1, :], (LANES, LANES)))
+    slots = [
+        (lax.broadcasted_iota(jnp.int32, (16, LANES), 1) + g * LANES).astype(F32) - begin for g in range(8)
+    ]
 
     for pair, (k0, k1) in enumerate(SPANS):
         pieces = []
+        one, zero = jnp.ones((16, LANES), BF), jnp.zeros((16, LANES), BF)
         for h in range(2):
-            slot = (lax.broadcasted_iota(jnp.int32, (8, LANES), 1) + (2 * pair + h) * LANES).astype(F32)
-            slot_b = jnp.broadcast_to(slot[0:1], (k1 - k0, LANES))
-            hit = jnp.logical_and(slot_b >= cols[0, k0:k1, :], slot_b < cols[1, k0:k1, :])
-            pieces.append(jnp.where(hit, 1.0, 0.0).astype(BF))
+            slot = slots[2 * pair + h].astype(jnp.int32).astype(jnp.int16)
+            column = []
+            for k in range(k0, k1, 16):
+                hit = jnp.logical_and(slot >= cols[0, k : k + 16, :], slot < cols[1, k : k + 16, :])
+                column.append(jnp.where(hit, one, zero))
+            pieces.append(jnp.concatenate(column, axis=0))
         hot = jnp.concatenate(pieces, axis=1)
         if pair == 0:
             low_hot[...] = hot[0:256]
@@ -464,8 +487,7 @@
             jac_new = (extra[0:1] + extra[1:2] + extra[2:3]) * (1.0 + extra[3:4])
             jout_ref[0:1, g * LANES : g * LANES + width_at] = jac_new[:, :width_at]
             fl = jnp.broadcast_to(extra[3:4], (8, LANES))
-            slot = (lax.broadcasted_iota(jnp.int32, (8, LANES), 1) + g * LANES).astype(F32)
-            child = slot - (256.0 * extra[4:5] + extra[5:6])
+            child = slots[g][0:8] - (256.0 * extra[4:5] + extra[5:6])
             bit2 = jnp.where(child >= 4.0, 1.0, 0.0)
             child = child - 4.0 * bit2
             bit1 = jnp.where(child >= 2.0, 1.0, 0.0)
@@ -496,7 +518,10 @@
                 lax.fori_loop(0, 5, one, 0)
 
 
-def edge_kernel(b_ref, a_ref, mid_ref, part_ref, low_hot, up_hot, coef_ref, out_hbm, lhs, res, out, sems):
+def edge_kernel(b_ref, a_ref, mid_ref, part_ref, low_hot, up_hot, coef_ref, jac_ref, out_hbm, jac_hbm, *rest):
+    lhs, res, out, sems = rest
+    jac_out = pltpu.make_async_copy(jac_ref, jac_hbm, sems.at[5])
+    jac_out.start()
     _, even, _ = position()
     for ref, start in ((a_ref, pick(even, 2, 0)), (b_ref, pick(even, 0, 2))):
         for g in range(2):
@@ -523,6 +548,7 @@
         pltpu.make_async_copy(out.at[v], out_hbm.at[v], sems.at[v]).start()
     for v in range(5):
         pltpu.make_async_copy(out.at[v], out_hbm.at[v], sems.at[v]).wait()
+    jac_out.wait()
 
 
 VMEM = pl.BlockSpec(memory_space=pltpu.MemorySpace.VMEM)
@@ -598,28 +624,35 @@
     pair_d = [(i, (i + 2) % total) for i in range(total) if (i // 2) % 2 == 1]
     received = [swap(x, pairs) for x, pairs in zip(sends, (pair_a, pair_b, pair_c, pair_d))]
 
-    (base,) = call(
+    base, outside = call(
         local_kernel,
-        [(slabs, 64, LANES)],
-        [VMEM] * 4,
-        [pltpu.VMEM((64, elements), F32), pltpu.VMEM((2 * groups, 8, LANES), F32)],
+        [(slabs, 64, LANES), (6 * groups, 80, LANES)],
+        [VMEM] * 5,
+        [
+            pltpu.VMEM((64, elements), F32),
+            pltpu.VMEM((2 * groups, 8, LANES), F32),
+            pltpu.VMEM((160, elements), BF),
+        ],
         "local",
-    )(slab, jac, speeds, modes)
-
-    (outside,) = call(
-        outside_kernel, [(6 * groups, 80, LANES)], [VMEM] * 2, [pltpu.VMEM((160, elements), BF)], "outside"
-    )(slab, face_source)
-    (full,) = call(
-        ghost_kernel, [(6 * groups, 80, LANES)], [VMEM] * 7, [pltpu.VMEM((160, 4 * LANES), BF)], "ghost"
-    )(outside, face_source, base, *(received[q] for q in (3, 1, 2, 0)))
+    )(slab, jac, speeds, modes, face_source)
     rows = slabs // 2 * 64
-    first, second, counts = call(
+    first, second, counts, meta, cols = call(
         face_kernel,
-        [(rows, LANES), (rows, LANES), (half, LANES)],
-        [VMEM] * 6,
-        [pltpu.VMEM((groups, 16, LANES), F32)],
+        [
+            (rows, LANES),
+            (rows, LANES),
+            (half, LANES),
+            ((16, 8 * LANES), BF),
+            ((2, 8 * LANES, LANES), jnp.int16),
+        ],
+        [VMEM] * 11,
+        [
+            pltpu.VMEM((groups, 16, LANES), F32),
+            pltpu.VMEM((6 * groups, 80, LANES), F32),
+            pltpu.VMEM((160, 4 * LANES), BF),
+        ],
         "faces",
-    )(base, slab, full, jac, speeds, flags)
+    )(base, slab, outside, face_source, jac, speeds, flags, *(received[q] for q in (3, 1, 2, 0)))
 
     from_a = swap(first, pair_a)
     from_b = swap(second, pair_b[:-1])
@@ -627,7 +660,7 @@
     halves = [list(range(half)), list(range(half, total))]
     counts = lax.all_to_all(counts, "curve", 0, 0, axis_index_groups=halves, tiled=True)
 
-    *kept, new_jac = call(
+    kept = call(
         own_kernel,
         [
             (15, 64, LANES),
@@ -637,25 +670,23 @@
             (5 * 48, 8, LANES),
             (1, E_NEW),
         ],
-        [VMEM] * 7,
+        [VMEM] * 5,
         [
             pltpu.VMEM((640, elements), BF),
-            pltpu.VMEM((16, 8 * LANES), BF),
             pltpu.VMEM((5, 64, LANES), F32),
             pltpu.VMEM((3 * 48, 8, LANES), F32),
-            pltpu.VMEM((2, 8 * LANES, LANES), F32),
         ],
         "own",
-    )(first, second, counts, received[0], received[1], jac, flags)
-    (state,) = call(
+    )(first, second, counts, meta, cols)
+    state, new_jac = call(
         edge_kernel,
-        [(5, 64, E_NEW)],
-        [VMEM] * 7,
+        [(5, 64, E_NEW), (1, E_NEW)],
+        [VMEM] * 8,
         [
             pltpu.VMEM((640, 4 * LANES), BF),
             pltpu.VMEM((25, 64, LANES), F32),
             pltpu.VMEM((5, 64, E_NEW), F32),
-            pltpu.SemaphoreType.DMA((5,)),
+            pltpu.SemaphoreType.DMA((6,)),
         ],
         "edge",
         HBM,

time: 32.5 us -> 31.5 us (0.969)
  Pallas kernels: 11.8 us -> 10.3 us
  waiting for transfers between devices: 2.51 us -> 3.17 us
    pallas_call x1, Pallas kernels: 3.15 us -> 2.32 us  [shards(): call(own_kernel, [(15, 64, LANES), (25, 64, LANES), ((256, 256), BF), ((2...]
    ppermute x6, waiting for transfers between devices: 2.51 us -> 3.17 us  [swap(): return lax.ppermute(x, 'curve', list(pairs) + [(b, a) for a, b in pairs])]
    pallas_call x5 -> x3, Pallas kernels: 6.68 us -> 6.07 us  [the longest x1 2.7 us: shards(): call(local_kernel, [(slabs, 64, LANES), (6 * groups, 80, LANES)], [VMEM]...]
  transfers between devices with their start and end apart: 6 -> 6, of which waited for: 1 -> 1; matrix products, arithmetic and copies ran while one was open for 0% -> 0% of each run, Pallas kernels for 20% -> 16%
where the time goes in v4:
time: 31.5 us; the launch traced here: 31.3 us
  Pallas kernels  10.3 us (33%)
  starting transfers between devices  8.96 us (28%)
  blocking collectives  8.09 us (26%)
  waiting for transfers between devices  3.17 us (10%)
  between operations  0.71 us (2%)
    ppermute x6, starting transfers between devices, swap(): return lax.ppermute(x, 'curve', list(pairs) + [(b, a) for a, b in pairs])  8.96 us
    all_to_all x1, blocking collectives, shards(): lax.all_to_all(counts, 'curve', 0, 0, axis_index_groups=halves, tiled=True)  8.09 us
    ppermute x6, waiting for transfers between devices, swap(): return lax.ppermute(x, 'curve', list(pairs) + [(b, a) for a, b in pairs])  3.17 us
    pallas_call x1, Pallas kernels, shards(): call(local_kernel, [(slabs, 64, LANES), (6 * groups, 80, LANES)], [VMEM]...  2.7 us
    pallas_call x1, Pallas kernels, shards(): call(own_kernel, [(15, 64, LANES), (25, 64, LANES), ((256, 256), BF), ((2...  2.32 us
    pallas_call x1, Pallas kernels, shards(): call(edge_kernel, [(5, 64, E_NEW), (1, E_NEW)], [VMEM] * 8, [pltpu.VMEM((...  2.03 us
    pallas_call x1, Pallas kernels, shards(): call(send_kernel, [(88, LANES)] * 4 + [(slabs, 64, LANES), (groups, LANES...  1.94 us
    pallas_call x1, Pallas kernels, shards(): call(face_kernel, [(rows, LANES), (rows, LANES), (half, LANES), ((16, 8 *...  1.34 us
  transfers between devices with their start and end apart: 6, of which 1 were waited for; matrix products, arithmetic and copies ran while one was open for 0% of the time, Pallas kernels for 16%

profile of v4, /device:TPU:0, one launch (start us, length us, event | category | flops | bytes accessed | tf_op | source)
XLA Modules:
  0.0 31.3 jit_solution(3449797036042214828)
XLA Ops:
  0.6 1.9 %send.1 = (f32[88,128]{1,0:T(8,128)S(1)}, f32[88,128]{1,0:T(8,128)S(1)}, f32[88,128]{1,0:T(8,128)S(1)}, f32[88,128]{1,0:T(8,128)S(1)}, f32[20,64,128]{2,1,0:T(8,...) custom-call(f32[5,64,512]{2,1,0:T(8,128)} %u_hbm.1, ...), custom_call_target="tpu_custom_call" | custom-call | tf_op jit(solution)/shard_map/send/pallas_call | solution.py:596
  2.6 7.0 %collective-permute-start = (f32[88,128]{1,0:T(8,128)S(1)}, f32[88,128]{1,0:T(8,128)S(1)}, u32[]{:S(2)}, u32[]{:S(2)}) collective-permute-start(f32[88,128]{1,0:T(8,128)S(1)} %get-tuple-element.35), channel_id=1, source_target_pairs={{2,4},{3,5},{6,8},{7,9},{10,12},{11,13},{14,16},{15,17},{18,20},{1... | collective-permute-start | bytes 135176 | tf_op jit(solution)/shard_map/ppermute | solution.py:559
  9.6 0.0 collective-permute-start.1
  9.6 1.2 %collective-permute-start.2 = (f32[88,128]{1,0:T(8,128)S(1)}, f32[88,128]{1,0:T(8,128)S(1)}, u32[]{:S(2)}, u32[]{:S(2)}) collective-permute-start(f32[88,128]{1,0:T(8,128)S(1)} %get-tuple-element.37), channel_id=1, source_target_pairs={{0,2},{1,3},{4,6},{5,7},{8,10},{9,11},{12,14},{13,15},{16,18},{17,... | collective-permute-start | bytes 135176 | tf_op jit(solution)/shard_map/ppermute | solution.py:559
  10.8 0.0 collective-permute-start.3
  10.8 2.7 %local.1 = (f32[20,64,128]{2,1,0:T(8,128)S(1)}, f32[24,80,128]{2,1,0:T(8,128)S(1)}) custom-call(f32[20,64,128]{2,1,0:T(8,128)S(1)} %get-tuple-element.27.slab_ref, f32[4,128]{1,0:T(4,128)S(1)} %get-tuple-element.28.jac_ref, f32[15,16,128]{2,1,0:T(8,128)S(1)} %get-tuple-element.29.sp_ref, f32[64,128]{1,0:T(8,128)S(1)} %get-tuple-element.30.modes_ref, ...), custom_call_target="tpu_custom_call" | custom-call | tf_op jit(solution)/shard_map/local/pallas_call | solution.py:627
  13.5 0.0 collective-permute-done.rd
  13.5 3.2 %collective-permute-done.1.rb = f32[88,128]{1,0:T(8,128)S(1)} collective-permute-done((f32[88,128]{1,0:T(8,128)S(1)}, f32[88,128]{1,0:T(8,128)S(1)}, u32[]{:S(2)}, u32[]{:S(2)}) %collective-permute-start.1) | collective-permute-done | bytes 45088 | tf_op jit(solution)/shard_map/ppermute | solution.py:559
  16.7 0.0 collective-permute-done.2.rc
  16.7 0.0 collective-permute-done.3.ra
  16.7 1.3 %faces.1 = (f32[640,128]{1,0:T(8,128)S(1)}, f32[640,128]{1,0:T(8,128)S(1)}, f32[16,128]{1,0:T(8,128)S(1)}, bf16[16,1024]{1,0:T(8,128)(2,1)S(1)}, s16[2,1024,128]{2,1,0:T(8,128)(2,1)S(1)}) custom-call(f32[20,64,128]{2,1,0:T(8,128)S(1)} %get-tuple-element.32.base_ref, f32[20,64,128]{2,1,0:T(8,128)S(1)} %get-tuple-element.27.slab_ref, ...), custom_call_target="tpu_custom_call" | custom-call | tf_op jit(solution)/shard_map/faces/pallas_call | solution.py:639
  18.0 0.7 %collective-permute-start.4 = (f32[640,128]{1,0:T(8,128)S(1)}, f32[640,128]{1,0:T(8,128)S(1)}, u32[]{:S(2)}, u32[]{:S(2)}) collective-permute-start(f32[640,128]{1,0:T(8,128)S(1)} %get-tuple-element.39.second_ref), channel_id=1, source_target_pairs={{1,2},{3,4},{5,6},{7,8},{9,10},{11,12},{13,14},{15,16},{17,18},{19... | collective-permute-start | bytes 983048 | tf_op jit(solution)/shard_map/ppermute | solution.py:559
  18.7 0.1 collective-permute-start.5
  18.8 8.1 %all_to_all.11 = f32[16,1,128]{2,1,0:T(1,128)S(1)} all-to-all(f32[16,1,128]{2,1,0:T(1,128)S(1)} %bitcast.9), channel_id=1, replica_groups={{0,1,2,3,4,5,6,7,8,9,10,11,12,13,14,15},{16,17,18,19,20,21,22,23,24,25,..., dimensions={0} | all-to-all | bytes 16384 | tf_op jit(solution)/shard_map/all_to_all | solution.py:661
  26.9 2.3 %own.1 = (f32[15,64,128]{2,1,0:T(8,128)S(1)}, f32[25,64,128]{2,1,0:T(8,128)S(1)}, bf16[256,256]{1,0:T(8,128)(2,1)S(1)}, bf16[256,384]{1,0:T(8,128)(2,1)S(1)}, f3...) custom-call(f32[640,128]{1,0:T(8,128)S(1)} %get-tuple-element.40.first_ref, f32[640,128]{1,0:T(8,128)S(1)} %get-tuple-element.39.second_ref, ...), custom_call_target="tpu_custom_call" | custom-call | tf_op jit(solution)/shard_map/own/pallas_call | solution.py:663
  29.2 0.0 collective-permute-done.4.b_ref
  29.2 0.0 collective-permute-done.5.a_ref
  29.2 2.0 %edge.1 = (f32[5,64,960]{2,1,0:T(8,128)}, f32[1,960]{1,0:T(1,128)}) custom-call(f32[640,128]{1,0:T(8,128)S(1)} %collective-permute-done.4.b_ref, f32[640,128]{1,0:T(8,128)S(1)} %collective-permute-done.5.a_ref, f32[15,64,128]{2,1,0:T(8,128)S(1)} %get-tuple-element.44.mid_ref, f32[25,64,128]{2,1,0:T(8,128)S(1)} %get-tuple-element.45.part_ref, ...), custom_call_target="tpu_custom_call" | custom-call | tf_op jit(solution)/shard_map/edge/pallas_call | solution.py:681
Async XLA Ops:
  2.6 10.9 %collective-permute-start = (f32[88,128]{1,0:T(8,128)S(1)}, f32[88,128]{1,0:T(8,128)S(1)}, u32[]{:S(2)}, u32[]{:S(2)}) collective-permute-start(f32[88,128]{1,0:T(8,128)S(1)} %get-tuple-element.35), channel_id=1, source_target_pairs={{2,4},{3,5},{6,8},{7,9},{10,12},{11,13},{14,16},{15,17},{18,20},{1... | collective-permute-start | bytes 135176 | tf_op jit(solution)/shard_map/ppermute | solution.py:559
  9.6 7.1 %collective-permute-start.1 = (f32[88,128]{1,0:T(8,128)S(1)}, f32[88,128]{1,0:T(8,128)S(1)}, u32[]{:S(2)}, u32[]{:S(2)}) collective-permute-start(f32[88,128]{1,0:T(8,128)S(1)} %get-tuple-element.36), channel_id=1, source_target_pairs={{1,2},{3,4},{5,6},{7,8},{9,10},{11,12},{13,14},{15,16},{17,18},{19... | collective-permute-start | bytes 135176 | tf_op jit(solution)/shard_map/ppermute | solution.py:559
  9.6 7.1 %collective-permute-start.2 = (f32[88,128]{1,0:T(8,128)S(1)}, f32[88,128]{1,0:T(8,128)S(1)}, u32[]{:S(2)}, u32[]{:S(2)}) collective-permute-start(f32[88,128]{1,0:T(8,128)S(1)} %get-tuple-element.37), channel_id=1, source_target_pairs={{0,2},{1,3},{4,6},{5,7},{8,10},{9,11},{12,14},{13,15},{16,18},{17,... | collective-permute-start | bytes 135176 | tf_op jit(solution)/shard_map/ppermute | solution.py:559
  10.8 5.9 %collective-permute-start.3 = (f32[88,128]{1,0:T(8,128)S(1)}, f32[88,128]{1,0:T(8,128)S(1)}, u32[]{:S(2)}, u32[]{:S(2)}) collective-permute-start(f32[88,128]{1,0:T(8,128)S(1)} %get-tuple-element.38), channel_id=1, source_target_pairs={{0,1},{2,3},{4,5},{6,7},{8,9},{10,11},{12,13},{14,15},{16,17},{18,... | collective-permute-start | bytes 135176 | tf_op jit(solution)/shard_map/ppermute | solution.py:559
  18.0 11.2 %collective-permute-start.4 = (f32[640,128]{1,0:T(8,128)S(1)}, f32[640,128]{1,0:T(8,128)S(1)}, u32[]{:S(2)}, u32[]{:S(2)}) collective-permute-start(f32[640,128]{1,0:T(8,128)S(1)} %get-tuple-element.39.second_ref), channel_id=1, source_target_pairs={{1,2},{3,4},{5,6},{7,8},{9,10},{11,12},{13,14},{15,16},{17,18},{19... | collective-permute-start | bytes 983048 | tf_op jit(solution)/shard_map/ppermute | solution.py:559
  18.7 10.5 %collective-permute-start.5 = (f32[640,128]{1,0:T(8,128)S(1)}, f32[640,128]{1,0:T(8,128)S(1)}, u32[]{:S(2)}, u32[]{:S(2)}) collective-permute-start(f32[640,128]{1,0:T(8,128)S(1)} %get-tuple-element.40.first_ref), channel_id=1, source_target_pairs={{0,1},{2,3},{4,5},{6,7},{8,9},{10,11},{12,13},{14,15},{16,17},{18,... | collective-permute-start | bytes 983048 | tf_op jit(solution)/shard_map/ppermute | solution.py:559

commit v5 on v4

--- a/solution.py
+++ b/solution.py
@@ -204,37 +204,40 @@
             speed_ref[d * 5 + v] = jnp.broadcast_to(sp_ref[d : d + 1, v : v + 1], (16, LANES))
 
 
-def line_rates(x, speed, blend):
+def line_weights(speed, blend):
+    return speed * (1.0 - blend), blend * speed * (1.0 / 6.0), blend * (0.5 * jnp.abs(speed))
+
+
+def line_rates(x, weights):
+    high_weight, central_weight, jump_weight = weights
     square = [x[m] * x[m] for m in range(4)]
+    size = [jnp.abs(x[m]) for m in range(4)]
     prod = {}
     for m in range(4):
         for n in range(m + 1, 4):
             prod[m, n] = x[m] * x[n]
-    half_speed = 0.5 * jnp.abs(speed)
+    pair = {(n, m): prod[min(m, n), max(m, n)] + square[m] for n in range(4) for m in range(4) if m != n}
     flux = []
     for m in range(3):
-        central = square[m] + prod[m, m + 1] + square[m + 1]
-        reach = jnp.maximum(jnp.abs(x[m]), jnp.abs(x[m + 1]))
-        flux.append((speed / 6.0) * central - half_speed * reach * (x[m + 1] - x[m]))
+        central = pair[m, m + 1] + square[m]
+        jump = jnp.maximum(size[m], size[m + 1]) * (x[m + 1] - x[m])
+        flux.append(central_weight * central - jump_weight * jump)
+    low = (
+        -INV_W[0] * flux[0],
+        INV_W[1] * (flux[0] - flux[1]),
+        INV_W[2] * (flux[1] - flux[2]),
+        INV_W[3] * flux[2],
+    )
     out = []
     for n in range(4):
         high = None
-        diag = -2.0 * DERIV[n, n] / 3.0 + SELF_SURFACE[n]
         for m in range(4):
             if m != n:
-                pair = prod[min(m, n), max(m, n)] + square[m]
-                term = float(-DERIV[n, m] / 3.0) * pair
+                term = float(-DERIV[n, m] / 3.0) * pair[n, m]
                 high = term if high is None else high + term
         if n in (0, 3):
-            high = high + float(diag) * square[n]
-        high = speed * high
-        if n == 0:
-            low = -INV_W[0] * flux[0]
-        elif n == 3:
-            low = INV_W[3] * flux[2]
-        else:
-            low = INV_W[n] * (flux[n - 1] - flux[n])
-        out.append(high + blend * (low - high))
+            high = high + float(-2.0 * DERIV[n, n] / 3.0 + SELF_SURFACE[n]) * square[n]
+        out.append(high_weight * high + low[n])
     return out
 
 
@@ -261,16 +264,16 @@
         blend = rows_s[g]
         scale = rows_s[groups + g]
         low = low_half()
-        speeds = [sp_ref[5 * d + v, 0:8, :] for d in range(3)]
+        weights = [line_weights(sp_ref[5 * d + v, 0:8, :], blend) for d in range(3)]
         for kh in range(2):
             at = [(t, pl.ds(32 * kh + i, 8, stride=4), slice(None)) for i in range(4)]
-            rate = line_rates([slab_ref[a] for a in at], speeds[0], blend)
+            rate = line_rates([slab_ref[a] for a in at], weights[0])
             for i in range(4):
                 base_ref[at[i]] = rate[i]
         tile = [[slab_ref[t, 16 * k + 8 * h : 16 * k + 8 * h + 8, :] for h in range(2)] for k in range(4)]
         rates = [[None, None] for _ in range(4)]
         for h in range(2):
-            r = line_rates([tile[k][h] for k in range(4)], speeds[2], blend)
+            r = line_rates([tile[k][h] for k in range(4)], weights[2])
             for k in range(4):
                 rates[k][h] = r[k]
         for k in (0, 2):
@@ -278,7 +281,7 @@
             for h in range(2):
                 x.append(jnp.where(low, tile[k][h], swap_halves(tile[k + 1][h])))
                 x.append(jnp.where(low, swap_halves(tile[k][h]), tile[k + 1][h]))
-            r = line_rates(x, speeds[1], blend)
+            r = line_rates(x, weights[1])
             for h in range(2):
                 one_row, two_row = r[2 * h], r[2 * h + 1]
                 rates[k][h] = rates[k][h] + jnp.where(low, one_row, swap_halves(two_row))
@@ -401,7 +404,6 @@
     counts_ref[...] = jnp.full(counts_ref.shape, groups * LANES + 7.0 * jnp.sum(flag_ref[...]), F32)
 
 
-EDGE_GROUPS = (0, 1, 5, 6, 7)
 SPANS = ((0, 768), (256, 768), (256, 1024), (256, 1024))
 
 
@@ -438,11 +440,16 @@
             store(16 * (k + 1) + 8 * q, jnp.where(low, swap_halves(one_row), two_row))
 
 
-def own_kernel(first_ref, second_ref, counts_ref, meta, cols, *rest):
-    mid_ref, part_ref, low_hot, up_hot, coef_out, jout_ref = rest[:6]
-    lhs, res, coef_mid = rest[6:]
+def refine_kernel(b_ref, a_ref, first_ref, second_ref, counts_ref, meta, cols, out_hbm, jac_hbm, *rest):
+    lhs, res, coef, out, jout_ref, sems = rest
     me, even, _ = position()
-    for ref, start in ((first_ref, pick(even, 2, 0)), (second_ref, pick(even, 0, 2))):
+    parts = (
+        (first_ref, pick(even, 4, 2)),
+        (second_ref, pick(even, 2, 4)),
+        (b_ref, pick(even, 0, 6)),
+        (a_ref, pick(even, 6, 0)),
+    )
+    for ref, start in parts:
         for g in range(2):
             high, low = split_two(ref[320 * g : 320 * g + 320, :])
             at = pl.ds(pl.multiple_of((start + g) * LANES, LANES), LANES)
@@ -471,13 +478,7 @@
                 column.append(jnp.where(hit, one, zero))
             pieces.append(jnp.concatenate(column, axis=0))
         hot = jnp.concatenate(pieces, axis=1)
-        if pair == 0:
-            low_hot[...] = hot[0:256]
-        elif pair == 2:
-            up_hot[:, 0:LANES] = hot[512:768, LANES : 2 * LANES]
-        elif pair == 3:
-            up_hot[:, LANES : 3 * LANES] = hot[512:768]
-        picked = dot32(lhs[...], hot[256 - k0 : 768 - k0])
+        picked = dot32(lhs[:, k0:k1], hot)
         known = dot32(meta[:, k0:k1], hot)
         for h in range(2):
             g = 2 * pair + h
@@ -492,63 +493,28 @@
             child = child - 4.0 * bit2
             bit1 = jnp.where(child >= 2.0, 1.0, 0.0)
             bit0 = child - 2.0 * bit1
-            edge = g in EDGE_GROUPS
-            coef, first = (coef_out, 48 * EDGE_GROUPS.index(g)) if edge else (coef_mid, 48 * (g - 2))
             for d, bit in enumerate((bit0, bit1, bit2)):
                 both = fl * bit
                 for i in range(4):
                     for m in range(4):
                         eye = 1.0 if i == m else 0.0
                         c = fl * float(SIDES[0][i, m] - eye) + both * float(SIDES[1][i, m] - SIDES[0][i, m]) + eye
-                        coef[first + 16 * d + 4 * i + m] = c
-            value = (picked[0:320, lanes] + picked[320:640, lanes]).reshape(5, 64, LANES)
-            if edge:
-                q = EDGE_GROUPS.index(g)
-                part_ref[5 * q : 5 * q + 5] = value
-            else:
-                res[...] = value
-
-                def one(v, carry, g=g, first=first):
-                    def store(row, x):
-                        mid_ref[5 * (g - 2) + v, row : row + 8, :] = x
-
-                    interpolate(res, v, coef_mid, first, store)
-                    return carry
-
-                lax.fori_loop(0, 5, one, 0)
-
-
-def edge_kernel(b_ref, a_ref, mid_ref, part_ref, low_hot, up_hot, coef_ref, jac_ref, out_hbm, jac_hbm, *rest):
-    lhs, res, out, sems = rest
-    jac_out = pltpu.make_async_copy(jac_ref, jac_hbm, sems.at[5])
-    jac_out.start()
-    _, even, _ = position()
-    for ref, start in ((a_ref, pick(even, 2, 0)), (b_ref, pick(even, 0, 2))):
-        for g in range(2):
-            high, low = split_two(ref[320 * g : 320 * g + 320, :])
-            at = pl.ds(pl.multiple_of((start + g) * LANES, LANES), LANES)
-            lhs[0:320, at] = high
-            lhs[320:640, at] = low
-    picked = (dot32(lhs[:, 0:256], low_hot[...]), dot32(lhs[:, 256:512], up_hot[...]))
-    for q, g in enumerate(EDGE_GROUPS):
-        from_up = int(g >= 5)
-        at = (g - 5 * from_up) * LANES
-        value = picked[from_up][0:320, at : at + LANES] + picked[from_up][320:640, at : at + LANES]
-        res[5 * q : 5 * q + 5] = part_ref[5 * q : 5 * q + 5] + value.reshape(5, 64, LANES)
+                        coef[48 * g + 16 * d + 4 * i + m] = c
+            res[5 * g : 5 * g + 5] = (picked[0:320, lanes] + picked[320:640, lanes]).reshape(5, 64, LANES)
+    copies = [pltpu.make_async_copy(jout_ref, jac_hbm, sems.at[5])]
+    copies[0].start()
     for v in range(5):
-        for g in (2, 3, 4):
-            out[v, :, g * LANES : (g + 1) * LANES] = mid_ref[5 * (g - 2) + v]
-        for q, g in enumerate(EDGE_GROUPS):
+        for g in range(8):
             width_at = min(LANES, E_NEW - g * LANES)
 
             def store(row, x, v=v, g=g, width_at=width_at):
                 out[v, row : row + 8, g * LANES : g * LANES + width_at] = x[:, :width_at]
 
-            interpolate(res, 5 * q + v, coef_ref, 48 * q, store)
-        pltpu.make_async_copy(out.at[v], out_hbm.at[v], sems.at[v]).start()
-    for v in range(5):
-        pltpu.make_async_copy(out.at[v], out_hbm.at[v], sems.at[v]).wait()
-    jac_out.wait()
+            interpolate(res, 5 * g + v, coef, 48 * g, store)
+        copies.append(pltpu.make_async_copy(out.at[v], out_hbm.at[v], sems.at[v]))
+        copies[-1].start()
+    for copy in copies:
+        copy.wait()
 
 
 VMEM = pl.BlockSpec(memory_space=pltpu.MemorySpace.VMEM)
@@ -660,37 +626,21 @@
     halves = [list(range(half)), list(range(half, total))]
     counts = lax.all_to_all(counts, "curve", 0, 0, axis_index_groups=halves, tiled=True)
 
-    kept = call(
-        own_kernel,
+    state, new_jac = call(
+        refine_kernel,
+        [(5, 64, E_NEW), (1, E_NEW)],
+        [VMEM] * 7,
         [
-            (15, 64, LANES),
-            (25, 64, LANES),
-            ((256, 256), BF),
-            ((256, 384), BF),
-            (5 * 48, 8, LANES),
-            (1, E_NEW),
-        ],
-        [VMEM] * 5,
-        [
-            pltpu.VMEM((640, elements), BF),
-            pltpu.VMEM((5, 64, LANES), F32),
-            pltpu.VMEM((3 * 48, 8, LANES), F32),
-        ],
-        "own",
-    )(first, second, counts, meta, cols)
-    state, new_jac = call(
-        edge_kernel,
-        [(5, 64, E_NEW), (1, E_NEW)],
-        [VMEM] * 8,
-        [
-            pltpu.VMEM((640, 4 * LANES), BF),
-            pltpu.VMEM((25, 64, LANES), F32),
+            pltpu.VMEM((640, 8 * LANES), BF),
+            pltpu.VMEM((40, 64, LANES), F32),
+            pltpu.VMEM((8 * 48, 8, LANES), F32),
             pltpu.VMEM((5, 64, E_NEW), F32),
+            pltpu.VMEM((1, E_NEW), F32),
             pltpu.SemaphoreType.DMA((6,)),
         ],
-        "edge",
+        "refine",
         HBM,
-    )(from_b, from_a, *kept)
+    )(from_b, from_a, first, second, counts, meta, cols)
     return state, new_jac.reshape(E_NEW)
 
 

time: 31.5 us -> 30.6 us (0.971)
  Pallas kernels: 10.3 us -> 9.26 us
    pallas_call x2 -> x1, Pallas kernels: 4.35 us -> 3.41 us  [shards(): call(refine_kernel, [(5, 64, E_NEW), (1, E_NEW)], [VMEM] * 7, [pltpu.VMEM...]
  transfers between devices with their start and end apart: 6 -> 6, of which waited for: 1 -> 1; matrix products, arithmetic and copies ran while one was open for 0% -> 0% of each run, Pallas kernels for 16% -> 8%
where the time goes in v5:
time: 30.6 us; the launch traced here: 30.3 us
  Pallas kernels  9.26 us (30%)
  starting transfers between devices  8.96 us (29%)
  blocking collectives  8.09 us (26%)
  waiting for transfers between devices  3.3 us (11%)
  between operations  0.68 us (2%)
    ppermute x6, starting transfers between devices, swap(): return lax.ppermute(x, 'curve', list(pairs) + [(b, a) for a, b in pairs])  8.96 us
    all_to_all x1, blocking collectives, shards(): lax.all_to_all(counts, 'curve', 0, 0, axis_index_groups=halves, tiled=True)  8.09 us
    pallas_call x1, Pallas kernels, shards(): call(refine_kernel, [(5, 64, E_NEW), (1, E_NEW)], [VMEM] * 7, [pltpu.VMEM...  3.41 us
    ppermute x6, waiting for transfers between devices, swap(): return lax.ppermute(x, 'curve', list(pairs) + [(b, a) for a, b in pairs])  3.3 us
    pallas_call x1, Pallas kernels, shards(): call(local_kernel, [(slabs, 64, LANES), (6 * groups, 80, LANES)], [VMEM]...  2.57 us
    pallas_call x1, Pallas kernels, shards(): call(send_kernel, [(88, LANES)] * 4 + [(slabs, 64, LANES), (groups, LANES...  1.94 us
    pallas_call x1, Pallas kernels, shards(): call(face_kernel, [(rows, LANES), (rows, LANES), (half, LANES), ((16, 8 *...  1.33 us
  transfers between devices with their start and end apart: 6, of which 1 were waited for; matrix products, arithmetic and copies ran while one was open for 0% of the time, Pallas kernels for 8%

profile of v5, /device:TPU:0, one launch (start us, length us, event | category | flops | bytes accessed | tf_op | source)
XLA Modules:
  0.0 30.3 jit_solution(11989488621763259017)
XLA Ops:
  0.6 1.9 %send.1 = (f32[88,128]{1,0:T(8,128)S(1)}, f32[88,128]{1,0:T(8,128)S(1)}, f32[88,128]{1,0:T(8,128)S(1)}, f32[88,128]{1,0:T(8,128)S(1)}, f32[20,64,128]{2,1,0:T(8,...) custom-call(f32[5,64,512]{2,1,0:T(8,128)} %u_hbm.1, ...), custom_call_target="tpu_custom_call" | custom-call | tf_op jit(solution)/shard_map/send/pallas_call | solution.py:562
  2.6 7.0 %collective-permute-start = (f32[88,128]{1,0:T(8,128)S(1)}, f32[88,128]{1,0:T(8,128)S(1)}, u32[]{:S(2)}, u32[]{:S(2)}) collective-permute-start(f32[88,128]{1,0:T(8,128)S(1)} %get-tuple-element.29), channel_id=1, source_target_pairs={{2,4},{3,5},{6,8},{7,9},{10,12},{11,13},{14,16},{15,17},{18,20},{1... | collective-permute-start | bytes 135176 | tf_op jit(solution)/shard_map/ppermute | solution.py:525
  9.6 0.0 collective-permute-start.1
  9.6 1.2 %collective-permute-start.2 = (f32[88,128]{1,0:T(8,128)S(1)}, f32[88,128]{1,0:T(8,128)S(1)}, u32[]{:S(2)}, u32[]{:S(2)}) collective-permute-start(f32[88,128]{1,0:T(8,128)S(1)} %get-tuple-element.31), channel_id=1, source_target_pairs={{0,2},{1,3},{4,6},{5,7},{8,10},{9,11},{12,14},{13,15},{16,18},{17,... | collective-permute-start | bytes 135176 | tf_op jit(solution)/shard_map/ppermute | solution.py:525
  10.8 0.0 collective-permute-start.3
  10.8 2.6 %local.1 = (f32[20,64,128]{2,1,0:T(8,128)S(1)}, f32[24,80,128]{2,1,0:T(8,128)S(1)}) custom-call(f32[20,64,128]{2,1,0:T(8,128)S(1)} %get-tuple-element.21.slab_ref, f32[4,128]{1,0:T(4,128)S(1)} %get-tuple-element.22.jac_ref, f32[15,16,128]{2,1,0:T(8,128)S(1)} %get-tuple-element.23.sp_ref, f32[64,128]{1,0:T(8,128)S(1)} %get-tuple-element.24.modes_ref, ...), custom_call_target="tpu_custom_call" | custom-call | tf_op jit(solution)/shard_map/local/pallas_call | solution.py:593
  13.4 0.0 collective-permute-done.rd
  13.4 3.3 %collective-permute-done.1.rb = f32[88,128]{1,0:T(8,128)S(1)} collective-permute-done((f32[88,128]{1,0:T(8,128)S(1)}, f32[88,128]{1,0:T(8,128)S(1)}, u32[]{:S(2)}, u32[]{:S(2)}) %collective-permute-start.1) | collective-permute-done | bytes 45088 | tf_op jit(solution)/shard_map/ppermute | solution.py:525
  16.7 0.0 collective-permute-done.2.rc
  16.7 0.0 collective-permute-done.3.ra
  16.7 1.3 %faces.1 = (f32[640,128]{1,0:T(8,128)S(1)}, f32[640,128]{1,0:T(8,128)S(1)}, f32[16,128]{1,0:T(8,128)S(1)}, bf16[16,1024]{1,0:T(8,128)(2,1)S(1)}, s16[2,1024,128]{2,1,0:T(8,128)(2,1)S(1)}) custom-call(f32[20,64,128]{2,1,0:T(8,128)S(1)} %get-tuple-element.26.base_ref, f32[20,64,128]{2,1,0:T(8,128)S(1)} %get-tuple-element.21.slab_ref, ...), custom_call_target="tpu_custom_call" | custom-call | tf_op jit(solution)/shard_map/faces/pallas_call | solution.py:605
  18.0 0.7 %collective-permute-start.4 = (f32[640,128]{1,0:T(8,128)S(1)}, f32[640,128]{1,0:T(8,128)S(1)}, u32[]{:S(2)}, u32[]{:S(2)}) collective-permute-start(f32[640,128]{1,0:T(8,128)S(1)} %get-tuple-element.33.second_ref), channel_id=1, source_target_pairs={{1,2},{3,4},{5,6},{7,8},{9,10},{11,12},{13,14},{15,16},{17,18},{19... | collective-permute-start | bytes 983048 | tf_op jit(solution)/shard_map/ppermute | solution.py:525
  18.7 0.1 collective-permute-start.5
  18.8 8.1 %all_to_all.11 = f32[16,1,128]{2,1,0:T(1,128)S(1)} all-to-all(f32[16,1,128]{2,1,0:T(1,128)S(1)} %bitcast.9), channel_id=1, replica_groups={{0,1,2,3,4,5,6,7,8,9,10,11,12,13,14,15},{16,17,18,19,20,21,22,23,24,25,..., dimensions={0} | all-to-all | bytes 16384 | tf_op jit(solution)/shard_map/all_to_all | solution.py:627
  26.9 0.0 collective-permute-done.4.b_ref
  26.9 0.0 collective-permute-done.5.a_ref
  26.9 3.4 %refine.1 = (f32[5,64,960]{2,1,0:T(8,128)}, f32[1,960]{1,0:T(1,128)}) custom-call(f32[640,128]{1,0:T(8,128)S(1)} %collective-permute-done.4.b_ref, f32[640,128]{1,0:T(8,128)S(1)} %collective-permute-done.5.a_ref, f32[640,128]{1,0:T(8,128)S(1)} %get-tuple-element.34.first_ref, f32[640,128]{1,0:T(8,128)S(1)} %get-tuple-element.33.second_ref, ...), custom_call_target="tpu_custom_call" | custom-call | tf_op jit(solution)/shard_map/refine/pallas_call | solution.py:629
Async XLA Ops:
  2.6 10.8 %collective-permute-start = (f32[88,128]{1,0:T(8,128)S(1)}, f32[88,128]{1,0:T(8,128)S(1)}, u32[]{:S(2)}, u32[]{:S(2)}) collective-permute-start(f32[88,128]{1,0:T(8,128)S(1)} %get-tuple-element.29), channel_id=1, source_target_pairs={{2,4},{3,5},{6,8},{7,9},{10,12},{11,13},{14,16},{15,17},{18,20},{1... | collective-permute-start | bytes 135176 | tf_op jit(solution)/shard_map/ppermute | solution.py:525
  9.6 7.1 %collective-permute-start.1 = (f32[88,128]{1,0:T(8,128)S(1)}, f32[88,128]{1,0:T(8,128)S(1)}, u32[]{:S(2)}, u32[]{:S(2)}) collective-permute-start(f32[88,128]{1,0:T(8,128)S(1)} %get-tuple-element.30), channel_id=1, source_target_pairs={{1,2},{3,4},{5,6},{7,8},{9,10},{11,12},{13,14},{15,16},{17,18},{19... | collective-permute-start | bytes 135176 | tf_op jit(solution)/shard_map/ppermute | solution.py:525
  9.6 7.1 %collective-permute-start.2 = (f32[88,128]{1,0:T(8,128)S(1)}, f32[88,128]{1,0:T(8,128)S(1)}, u32[]{:S(2)}, u32[]{:S(2)}) collective-permute-start(f32[88,128]{1,0:T(8,128)S(1)} %get-tuple-element.31), channel_id=1, source_target_pairs={{0,2},{1,3},{4,6},{5,7},{8,10},{9,11},{12,14},{13,15},{16,18},{17,... | collective-permute-start | bytes 135176 | tf_op jit(solution)/shard_map/ppermute | solution.py:525
  10.8 5.9 %collective-permute-start.3 = (f32[88,128]{1,0:T(8,128)S(1)}, f32[88,128]{1,0:T(8,128)S(1)}, u32[]{:S(2)}, u32[]{:S(2)}) collective-permute-start(f32[88,128]{1,0:T(8,128)S(1)} %get-tuple-element.32), channel_id=1, source_target_pairs={{0,1},{2,3},{4,5},{6,7},{8,9},{10,11},{12,13},{14,15},{16,17},{18,... | collective-permute-start | bytes 135176 | tf_op jit(solution)/shard_map/ppermute | solution.py:525
  18.0 8.9 %collective-permute-start.4 = (f32[640,128]{1,0:T(8,128)S(1)}, f32[640,128]{1,0:T(8,128)S(1)}, u32[]{:S(2)}, u32[]{:S(2)}) collective-permute-start(f32[640,128]{1,0:T(8,128)S(1)} %get-tuple-element.33.second_ref), channel_id=1, source_target_pairs={{1,2},{3,4},{5,6},{7,8},{9,10},{11,12},{13,14},{15,16},{17,18},{19... | collective-permute-start | bytes 983048 | tf_op jit(solution)/shard_map/ppermute | solution.py:525
  18.7 8.2 %collective-permute-start.5 = (f32[640,128]{1,0:T(8,128)S(1)}, f32[640,128]{1,0:T(8,128)S(1)}, u32[]{:S(2)}, u32[]{:S(2)}) collective-permute-start(f32[640,128]{1,0:T(8,128)S(1)} %get-tuple-element.34.first_ref), channel_id=1, source_target_pairs={{0,1},{2,3},{4,5},{6,7},{8,9},{10,11},{12,13},{14,15},{16,17},{18,... | collective-permute-start | bytes 983048 | tf_op jit(solution)/shard_map/ppermute | solution.py:525
